TPU v7x, 128 devices: a whole 4x4x4 slice. The times are simulated.
128 devices in a mesh: row: 8 (over x, y_hi), col: 16 (over y_lo, z, core).
Axes of the slice: x: 4, y: 4 (y_hi: 2, y_lo: 2; y = y_hi * 2 + y_lo), z: 4, core: 2. Of those that a mesh axis runs over, the one named last changes fastest.
Arguments:
- tokens: bfloat16 [256, 1024, 192], P('row', 'col'), may hold values from -6 to 6
- norm_gain: float32 [2, 3, 192], replicated, may hold values from 0.1 to 1.9
- qkv_weight: bfloat16 [2, 192, 576], replicated, may hold values from -0.4375 to 0.4375
- proj_weight: bfloat16 [2, 192, 192], replicated, may hold values from -0.4375 to 0.4375
- bias_table: float32 [2, 6, 225], replicated, may hold values from -4 to 4
- conv_weight: float32 [2, 49, 192], replicated, may hold values from -0.875 to 0.875
- up_weight: bfloat16 [2, 192, 768], replicated, may hold values from -0.4375 to 0.4375
- down_weight: bfloat16 [2, 768, 192], replicated, may hold values from -0.21875 to 0.21875
Outputs:
- mixed: bfloat16 [256, 1024, 192], P('row', 'col')
All inputs are finite; a program needn't handle non-finite values.
Results may differ from a plain program's by a relative error of at most 0.013.
Values may be sent and summed in bfloat16 or wider, within the bound.
No kernel may reach another device: no remote copies, remote signals or barrier semaphores. Data moves between devices by JAX's collectives and lax.ppermute only.
A program may use at most 64 MiB of HBM per device.

v0:
```python
import functools
import jax
import jax.numpy as jnp
from jax import lax
from jax.experimental import pallas as pl
from jax.experimental.pallas import tpu as pltpu
from jax.sharding import Mesh, PartitionSpec as P

D = 192
HEADS = 6
HID = 768
WS = 8
KS = 7
HEAD = 32
AREA = WS * WS
PAD = 256
LANES = 128
HALO = KS // 2
STRIDE = 40
EPSILON = 1e-05

f32 = jnp.float32
bf16 = jnp.bfloat16


def layer_norm(values, gain):
    centre = jnp.mean(values, axis=-1, keepdims=True)
    centred = values - centre
    spread = jnp.mean(centred * centred, axis=-1, keepdims=True)
    return centred * lax.rsqrt(spread + EPSILON) * gain


def mxu(a, b):
    return jnp.dot(a, b, preferred_element_type=f32)


def prepare_attention(table_ref, qkv_ref, bias_s, rows_s, qkv_s):
    table = table_ref[0]
    high = table.astype(bf16)
    rest = table - high.astype(f32)
    middle = rest.astype(bf16)
    low = (rest - middle.astype(f32)).astype(bf16)
    entries = (2 * WS - 1) ** 2
    lane = lax.broadcasted_iota(jnp.int32, (entries, WS * LANES), 1)
    entry = lax.broadcasted_iota(jnp.int32, (entries, WS * LANES), 0)
    target = (
        (2 * WS - 2 - ((lane & (LANES - 1)) >> 3)) * (2 * WS - 1)
        + (lane >> 7)
        - (lane & 7)
        + WS
        - 1
    )
    chosen = jnp.where(entry == target, 1.0, 0.0).astype(bf16)
    spread = mxu(high, chosen) + mxu(middle, chosen) + mxu(low, chosen)
    for place in range(WS):
        rows_s[place, 0:HEADS, :] = spread[:, place * LANES : (place + 1) * LANES]
    first = lax.broadcasted_iota(jnp.int32, (WS, LANES), 1) < AREA
    for group in range(HEADS // 2):
        left = rows_s[:, 2 * group, :]
        right = rows_s[:, 2 * group + 1, :]
        for row in range(WS):
            shift = LANES - (WS - 1 - row) * WS
            piece = jnp.where(
                first,
                pltpu.roll(left, shift % LANES, 1),
                pltpu.roll(right, (shift + AREA) % LANES, 1),
            )
            bias_s[group * AREA + row * WS : group * AREA + (row + 1) * WS, :] = piece
    weights = qkv_ref[0].astype(f32)
    gap = jnp.zeros((D, PAD - D), f32)
    qkv_s[...] = jnp.concatenate(
        [
            weights[:, 0:D],
            gap,
            weights[:, D : 2 * D],
            gap,
            weights[:, 2 * D : 3 * D],
            gap,
        ],
        axis=1,
    ).astype(bf16)


def attention_masks():
    lane = lax.broadcasted_iota(jnp.int32, (1, PAD), 1)
    groups = [
        jnp.where((lane >> 6) == g, 1.0, 0.0).astype(bf16) for g in range(HEADS // 2)
    ]
    parities = [
        jnp.where(((lane >> 5) & 1) == h, 1.0, 0.0).astype(bf16) for h in range(2)
    ]
    rows = lax.broadcasted_iota(jnp.int32, (LANES, LANES), 0) >> 6
    cols = lax.broadcasted_iota(jnp.int32, (LANES, LANES), 1) >> 6
    summing = jnp.where(rows == cols, 1.0, 0.0).astype(bf16)
    return groups, parities, summing


def attend(q, k, v, bias, masks):
    groups, parities, summing = masks
    queries = jnp.concatenate([q * m for m in groups], axis=0)
    keys = jnp.concatenate([k * m for m in parities], axis=0)
    values = jnp.concatenate([v * m for m in parities], axis=0)
    scores = lax.dot_general(
        queries, keys, (((1,), (1,)), ((), ())), preferred_element_type=f32
    )
    weights = jnp.exp(scores * HEAD ** (-0.5) + bias)
    total = mxu(weights.astype(bf16), summing)
    attention_weights = (weights / total).astype(bf16)
    mixed = mxu(attention_weights, values)
    lane = lax.broadcasted_iota(jnp.int32, (AREA, PAD), 1) >> 6
    return jnp.where(
        lane == 0,
        mixed[0:AREA],
        jnp.where(lane == 1, mixed[AREA : 2 * AREA], mixed[2 * AREA : 3 * AREA]),
    )


def plain_kernel(
    x_ref, gain_ref, qkv_ref, proj_ref, table_ref, sum_ref, normed_ref, bias_s, rows_s, qkv_s
):
    @pl.when(pl.program_id(0) == 0)
    def _():
        prepare_attention(table_ref, qkv_ref, bias_s, rows_s, qkv_s)

    cols = x_ref.shape[1]
    count = cols // WS
    grid = x_ref[...].astype(f32)
    current = jnp.concatenate(
        [grid[:, j * WS : (j + 1) * WS, :].reshape(AREA, D) for j in range(count)], axis=0
    )
    normed = layer_norm(current, gain_ref[0, 0:1, :]).astype(bf16)
    projected = mxu(normed, qkv_s[...]).astype(bf16)
    masks = attention_masks()
    bias = bias_s[...]
    outs = []
    for j in range(count):
        rows = projected[j * AREA : (j + 1) * AREA]
        outs.append(
            attend(
                rows[:, 0:PAD], rows[:, PAD : 2 * PAD], rows[:, 2 * PAD : 3 * PAD], bias, masks
            )[:, 0:D].astype(bf16)
        )
    branch = mxu(jnp.concatenate(outs, axis=0), proj_ref[0]).astype(bf16)
    after = current + branch.astype(f32)
    normed_two = layer_norm(after, gain_ref[0, 1:2, :])

    def spatial(value):
        return jnp.concatenate(
            [value[j * AREA : (j + 1) * AREA].reshape(WS, WS, D) for j in range(count)], axis=1
        )

    sum_ref[...] = spatial(after)
    normed_ref[...] = spatial(normed_two).astype(bf16)


def attention_scratch():
    return [
        pltpu.VMEM((HEADS // 2 * AREA, LANES), f32),
        pltpu.VMEM((WS, WS, LANES), f32),
        pltpu.VMEM((D, 3 * PAD), bf16),
    ]


def plain_attention(tokens, norm_gain, qkv_weight, proj_weight, bias_table, layer):
    height, width = tokens.shape[:2]
    whole = lambda *shape: pl.BlockSpec(
        (1, *shape), lambda i: (layer,) + (0,) * len(shape)
    )
    block = pl.BlockSpec((WS, width, D), lambda i: (i, 0, 0))
    return pl.pallas_call(
        plain_kernel,
        grid=(height // WS,),
        in_specs=[
            block,
            whole(3, D),
            whole(D, 3 * D),
            whole(D, D),
            whole(HEADS, (2 * WS - 1) ** 2),
        ],
        out_specs=[block, block],
        out_shape=[
            jax.ShapeDtypeStruct(tokens.shape, f32),
            jax.ShapeDtypeStruct(tokens.shape, bf16),
        ],
        scratch_shapes=attention_scratch(),
        name="plain_attention",
    )(tokens, norm_gain, qkv_weight, proj_weight, bias_table)


def pack(value):
    half = value.shape[1] // 2
    upper = jnp.concatenate(
        [value[:, :half, LANES:D], value[:, half:, LANES:D]], axis=-1
    )
    return jnp.concatenate([value[:, :, :LANES], upper], axis=1)


def unpack(value):
    count = value.shape[1] * LANES // D
    upper = value[:, count:, :]
    upper = jnp.concatenate(
        [upper[:, :, : D - LANES], upper[:, :, D - LANES :]], axis=1
    )
    return jnp.concatenate([value[:, :count, :], upper], axis=-1)


def shuffled_kernel(
    got_ref, qkv_ref, proj_ref, table_ref, out_ref, bias_s, rows_s, qkv_s, projected_s, attended_s
):
    prepare_attention(table_ref, qkv_ref, bias_s, rows_s, qkv_s)
    count = got_ref.shape[1] * LANES // D
    step = 8

    def project(c, carry):
        rows = unpack(got_ref[pl.ds(c * step, step)].astype(f32)).reshape(step * count, D)
        projected = mxu(rows.astype(bf16), qkv_s[...])
        for p in range(step):
            for t in range(6):
                projected_s[t, pl.ds((c * step + p) * STRIDE, count), :] = projected[
                    p * count : (p + 1) * count, t * LANES : (t + 1) * LANES
                ]
        return carry

    lax.fori_loop(0, AREA // step, project, 0)
    masks = attention_masks()
    unroll = 4

    def windows(c, carry):
        for n in range(unroll):
            w = c * unroll + n
            parts = [
                jnp.concatenate(
                    [
                        projected_s[2 * t, pl.ds(w, AREA, stride=STRIDE), :],
                        projected_s[2 * t + 1, pl.ds(w, AREA, stride=STRIDE), :],
                    ],
                    axis=1,
                ).astype(bf16)
                for t in range(3)
            ]
            result = attend(*parts, bias_s[...], masks)
            for t in range(2):
                attended_s[t, pl.ds(w, AREA, stride=STRIDE), :] = result[
                    :, t * LANES : (t + 1) * LANES
                ]
        return carry

    lax.fori_loop(0, count // unroll, windows, 0)

    def finish(c, carry):
        rows = jnp.concatenate(
            [
                jnp.concatenate(
                    [
                        attended_s[t, pl.ds((c * step + p) * STRIDE, count), :]
                        for p in range(step)
                    ],
                    axis=0,
                )
                for t in range(2)
            ],
            axis=1,
        )[:, 0:D]
        branch = mxu(rows.astype(bf16), proj_ref[0])
        out_ref[pl.ds(c * step, step)] = pack(branch.reshape(step, count, D)).astype(bf16)
        return carry

    lax.fori_loop(0, AREA // step, finish, 0)


def shuffled_attention(got, qkv_weight, proj_weight, bias_table, layer):
    whole = lambda *shape: pl.BlockSpec(
        (1, *shape), lambda i: (layer,) + (0,) * len(shape)
    )
    block = pl.BlockSpec(got.shape, lambda i: (0, 0, 0))
    return pl.pallas_call(
        shuffled_kernel,
        grid=(1,),
        in_specs=[block, whole(D, 3 * D), whole(D, D), whole(HEADS, (2 * WS - 1) ** 2)],
        out_specs=block,
        out_shape=jax.ShapeDtypeStruct(got.shape, bf16),
        scratch_shapes=attention_scratch()
        + [
            pltpu.VMEM((6, AREA * STRIDE, LANES), f32),
            pltpu.VMEM((2, AREA * STRIDE, LANES), f32),
        ],
        name="shuffled_attention",
    )(got, qkv_weight, proj_weight, bias_table)


def residual_kernel(back_ref, current_ref, gain_ref, sum_ref, normed_ref):
    rows, cols, _ = current_ref.shape
    count = back_ref.shape[1] * LANES // D
    high = count // WS
    branch = unpack(back_ref[...].astype(f32)).reshape(rows // high, cols // WS, high, WS, D)
    branch = branch.transpose(0, 2, 1, 3, 4).reshape(rows, cols, D)
    after = current_ref[...].astype(f32) + branch
    sum_ref[...] = after
    normed_ref[...] = layer_norm(after, gain_ref[0, 1:2, :]).astype(bf16)


def residual(back, current, norm_gain, layer):
    height, width = current.shape[:2]
    steps = height // WS
    block = pl.BlockSpec((WS, width, D), lambda i: (i, 0, 0))
    return pl.pallas_call(
        residual_kernel,
        grid=(steps,),
        in_specs=[
            pl.BlockSpec((back.shape[0] // steps, *back.shape[1:]), lambda i: (i, 0, 0)),
            block,
            pl.BlockSpec((1, 3, D), lambda i: (layer, 0, 0)),
        ],
        out_specs=[block, block],
        out_shape=[
            jax.ShapeDtypeStruct(current.shape, f32),
            jax.ShapeDtypeStruct(current.shape, bf16),
        ],
        name="residual",
    )(back, current, norm_gain)


def finish_kernel(send, *refs):
    (
        sum_ref,
        normed_ref,
        top_ref,
        bottom_ref,
        left_ref,
        right_ref,
        gain_ref,
        next_ref,
        taps_ref,
        up_ref,
        down_ref,
        out_ref,
        *refs,
    ) = refs
    if send:
        send_ref, *refs = refs
    padded_s, after_s, taps_s = refs
    step = pl.program_id(0)
    height, width, _ = normed_ref.shape
    rows = sum_ref.shape[0]

    @pl.when(step == 0)
    def _():
        def place(r, middle):
            padded_s[r] = jnp.concatenate(
                [left_ref[r].astype(f32), middle.astype(f32), right_ref[r].astype(f32)], axis=0
            ).astype(bf16)

        for r in range(HALO):
            place(r, top_ref[r])
            place(height + HALO + r, bottom_ref[r])

        def body(r, carry):
            place(r + HALO, normed_ref[r])
            return carry

        lax.fori_loop(0, height, body, 0)
        for t in range(KS * KS):
            taps_s[t] = jnp.broadcast_to(taps_ref[0, t : t + 1, :], (16, D)).astype(bf16)

    def row(r, carry):
        total = sum_ref[r]
        for v in range(KS):
            part = None
            for u in range(KS):
                x = padded_s[step * rows + r + u].reshape(-1, 16, D)
                term = x * taps_s[u * KS + v][None]
                part = term if part is None else part + term
            part = part.reshape(-1, D).astype(f32)
            start = WS - HALO + v
            total = total + part[start : start + width]
        after_s[pl.ds(pl.multiple_of(r * width, width), width), :] = total
        return carry

    lax.fori_loop(0, rows, row, 0)
    after = after_s[...]
    normed = layer_norm(after, gain_ref[0, 2:3, :]).astype(bf16)
    raised = mxu(normed, up_ref[0])
    hidden = (0.5 * raised * (1.0 + lax.erf(raised * 0.5**0.5))).astype(bf16)
    outcome = (after + mxu(hidden, down_ref[0])).astype(bf16)
    out_ref[...] = outcome.reshape(rows, width, D)
    if send:
        normed = layer_norm(outcome.astype(f32), next_ref[0, 0:1, :])
        high = send_ref.shape[1] * LANES // D // WS
        pieces = normed.reshape(rows // high, high, width // WS, WS, D)
        pieces = pieces.transpose(0, 2, 1, 3, 4).reshape(-1, high * WS, D)
        send_ref[...] = pack(pieces).astype(bf16)


def finish_layer(
    after, normed, halo, norm_gain, conv_weight, up_weight, down_weight, layer, send, group
):
    height, width = normed.shape[:2]
    steps = height // WS
    whole = lambda *shape: pl.BlockSpec(
        (1, *shape), lambda i: (layer,) + (0,) * len(shape)
    )
    full = lambda a: pl.BlockSpec(a.shape, lambda i: (0,) * a.ndim)
    block = pl.BlockSpec((WS, width, D), lambda i: (i, 0, 0))
    out_specs = [block]
    out_shape = [jax.ShapeDtypeStruct(normed.shape, bf16)]
    if send:
        rows = height * width // group * D // LANES
        out_specs.append(pl.BlockSpec((group // steps, rows, LANES), lambda i: (i, 0, 0)))
        out_shape.append(jax.ShapeDtypeStruct((group, rows, LANES), bf16))
    following = min(layer + 1, norm_gain.shape[0] - 1)
    return pl.pallas_call(
        functools.partial(finish_kernel, send),
        grid=(steps,),
        in_specs=[
            block,
            full(normed),
            *[full(h) for h in halo],
            whole(3, D),
            pl.BlockSpec((1, 3, D), lambda i: (following, 0, 0)),
            whole(KS * KS, D),
            whole(D, HID),
            whole(HID, D),
        ],
        out_specs=out_specs,
        out_shape=out_shape,
        scratch_shapes=[
            pltpu.VMEM((height + 2 * HALO, width + 2 * WS, D), bf16),
            pltpu.VMEM((WS * width, D), f32),
            pltpu.VMEM((KS * KS, 16, D), bf16),
        ],
        name="finish_layer",
    )(after, normed, *halo, norm_gain, norm_gain, conv_weight, up_weight, down_weight)


def halo_of(normed):
    height, width = normed.shape[:2]

    def shift(value, axes, forward):
        count = lax.axis_size(axes)
        pairs = [(i, i + 1) if forward else (i + 1, i) for i in range(count - 1)]
        return lax.ppermute(value, axes, pairs)

    top = shift(normed[height - HALO :], "row", True)
    bottom = shift(normed[:HALO], "row", False)
    columns = lambda part: jnp.concatenate([part(top), part(normed), part(bottom)], axis=0)
    left = shift(columns(lambda a: a[:, width - WS :]), ("block", "core"), True)
    right = shift(columns(lambda a: a[:, :WS]), ("block", "core"), False)
    return top, bottom, left, right


def on_device(
    tokens, norm_gain, qkv_weight, proj_weight, bias_table, conv_weight, up_weight, down_weight
):
    members = ("row", "block")
    group = lax.axis_size(members)
    after, normed = plain_attention(tokens, norm_gain, qkv_weight, proj_weight, bias_table, 0)
    current, outgoing = finish_layer(
        after, normed, halo_of(normed), norm_gain, conv_weight, up_weight, down_weight, 0, True, group
    )
    got = lax.all_to_all(outgoing, members, 0, 0, tiled=True)
    branch = shuffled_attention(got, qkv_weight, proj_weight, bias_table, 1)
    back = lax.all_to_all(branch, members, 0, 0, tiled=True)
    after, normed = residual(back, current, norm_gain, 1)
    (outcome,) = finish_layer(
        after, normed, halo_of(normed), norm_gain, conv_weight, up_weight, down_weight, 1, False, group
    )
    return outcome


def solution(mesh):
    split = Mesh(
        mesh.devices.reshape(mesh.shape["row"], mesh.shape["col"] // 2, 2), ("row", "block", "core")
    )
    spec = P("row", ("block", "core"), None)
    return jax.shard_map(
        on_device, mesh=split, in_specs=(spec,) + (P(),) * 7, out_specs=spec, check_vma=False
    )
```

profile of v0, /device:TPU:1, one launch (start us, length us, event | category | flops | bytes accessed | tf_op | source)
XLA Modules:
  0.0 154.8 jit_solution(11148695858635125456)
XLA Ops:
  0.0 1.4 copy.9.gain_ref.refs_6_.refs_7_
  1.4 1.3 copy.10.table_ref
  2.7 13.2 %plain_attention.1 = (f32[32,64,192]{2,1,0:T(8,128)}, bf16[32,64,192]{2,1,0:T(8,128)(2,1)}) custom-call(bf16[32,64,192]{2,1,0:T(8,128)(2,1)} %x_ref.1, f32[2,3,192]{2,1,0:T(4,128)} %copy.9.gain_ref.refs_6_.refs_7_, bf16[2,192,576]{2,1,0:T(8,128)(2,1)} %qkv_ref.3, bf16[2,192,192]{2,1,0:T(8,128)(2,1)} %proj_ref.3, f32[2,6,225]{2,1,0:T(8,128)} %copy.10.table_ref), custom_call_target="tpu_custom_call" | custom-call | tf_op jit(solution)/shard_map/plain_attention/pallas_call | solution.py:170
  15.9 1.0 fusion.3
  16.8 1.3 collective-permute-start.1
  18.1 6.3 %collective-permute-start = (bf16[3,64,192]{2,1,0:T(8,128)(2,1)S(1)}, bf16[3,64,192]{2,1,0:T(8,128)(2,1)S(1)}, u32[]{:S(2)}, u32[]{:S(2)}) collective-permute-start(bf16[3,64,192]{2,1,0:T(8,128)(2,1)S(1)} %get-tuple-element.24), channel_id=1, source_target_pairs={{0,16},{16,32},{32,48},{48,64},{64,80},{80,96},{96,112},{1,17},{17... | collective-permute-start | bytes 221192 | tf_op jit(solution)/shard_map/ppermute | solution.py:441
  24.4 1.0 fusion.2
  25.4 0.0 collective-permute-done.1.refs_3_
  25.4 2.4 %collective-permute-done.refs_2_ = bf16[3,64,192]{2,1,0:T(8,128)(2,1)S(1)} collective-permute-done((bf16[3,64,192]{2,1,0:T(8,128)(2,1)S(1)}, bf16[3,64,192]{2,1,0:T(8,128)(2,1)S(1)}, u32[]{:S(2)}, u32[]{:S(2)}) %collective-permute-start) | collective-permute-done | bytes 73760 | tf_op jit(solution)/shard_map/ppermute | solution.py:441
  27.9 4.1 %collective-permute-start.2 = (bf16[38,8,192]{2,1,0:T(8,128)(2,1)S(1)}, bf16[38,8,192]{2,1,0:T(8,128)(2,1)S(1)}, u32[]{:S(2)}, u32[]{:S(2)}) collective-permute-start(bf16[38,8,192]{2,1,0:T(8,128)(2,1)S(1)} %pad_maximum_fusion), channel_id=1, source_target_pairs={{0,1},{1,2},{2,3},{3,4},{4,5},{5,6},{6,7},{7,8},{8,9},{9,10},{10,1... | collective-permute-start | bytes 350216 | tf_op jit(solution)/shard_map/ppermute | solution.py:441
  32.0 1.9 %collective-permute-start.3 = (bf16[38,8,192]{2,1,0:T(8,128)(2,1)S(1)}, bf16[38,8,192]{2,1,0:T(8,128)(2,1)S(1)}, u32[]{:S(2)}, u32[]{:S(2)}) collective-permute-start(bf16[38,8,192]{2,1,0:T(8,128)(2,1)S(1)} %pad_maximum_fusion.1), channel_id=1, source_target_pairs={{1,0},{2,1},{3,2},{4,3},{5,4},{6,5},{7,6},{8,7},{9,8},{10,9},{11,1... | collective-permute-start | bytes 350216 | tf_op jit(solution)/shard_map/ppermute | solution.py:441
  34.0 0.7 copy.13.refs_8_
  34.6 1.2 copy.14.refs_10_
  35.8 2.8 %collective-permute-done.3.refs_5_ = bf16[38,8,192]{2,1,0:T(8,128)(2,1)S(1)} collective-permute-done((bf16[38,8,192]{2,1,0:T(8,128)(2,1)S(1)}, bf16[38,8,192]{2,1,0:T(8,128)(2,1)S(1)}, u32[]{:S(2)}, u32[]{:S(2)}) %collective-permute-start.3) | collective-permute-done | bytes 116768 | tf_op jit(solution)/shard_map/ppermute | solution.py:441
  38.6 0.7 copy-done.3
  39.3 12.9 %finish_layer.2 = (bf16[32,64,192]{2,1,0:T(8,128)(2,1)}, bf16[64,48,128]{2,1,0:T(8,128)(2,1)}) custom-call(f32[32,64,192]{2,1,0:T(8,128)} %get-tuple-element.11.refs_0_, bf16[32,64,192]{2,1,0:T(8,128)(2,1)} %get-tuple-element.12.refs_1_, bf16[3,64,192]{2,1,0:T(8,128)(2,1)} %copy-done.7, bf16[3,64,192]{2,1,0:T(8,128)(2,1)} %copy-done.5, ...), custom_call_target="tpu_custom_call" | custom-call | tf_op jit(solution)/shard_map/finish_layer/pallas_call | solution.py:411
  52.2 27.8 %all_to_all.10.got_ref = bf16[64,48,128]{2,1,0:T(8,128)(2,1)} all-to-all(bf16[64,48,128]{2,1,0:T(8,128)(2,1)} %get-tuple-element.13), channel_id=1, replica_groups=mesh['row'=8,'block'=8,'core'=2] {'row','block'}, dimensions={0} | all-to-all | bytes 1572864 | tf_op jit(solution)/shard_map/all_to_all | solution.py:460
  79.9 16.4 %shuffled_attention.1 = bf16[64,48,128]{2,1,0:T(8,128)(2,1)} custom-call(bf16[64,48,128]{2,1,0:T(8,128)(2,1)} %all_to_all.10.got_ref, bf16[2,192,576]{2,1,0:T(8,128)(2,1)} %qkv_ref.3, bf16[2,192,192]{2,1,0:T(8,128)(2,1)} %proj_ref.3, f32[2,6,225]{2,1,0:T(8,128)} %copy.10.table_ref), custom_call_target="tpu_custom_call" | custom-call | tf_op jit(solution)/shard_map/shuffled_attention/pallas_call | solution.py:276
  96.3 21.3 %all_to_all.11.back_ref = bf16[64,48,128]{2,1,0:T(8,128)(2,1)} all-to-all(bf16[64,48,128]{2,1,0:T(8,128)(2,1)} %shuffled_attention.1), channel_id=1, replica_groups=mesh['row'=8,'block'=8,'core'=2] {'row','block'}, dimensions={0} | all-to-all | bytes 1572864 | tf_op jit(solution)/shard_map/all_to_all | solution.py:462
  117.6 4.1 %residual.1 = (f32[32,64,192]{2,1,0:T(8,128)}, bf16[32,64,192]{2,1,0:T(8,128)(2,1)}) custom-call(bf16[64,48,128]{2,1,0:T(8,128)(2,1)} %all_to_all.11.back_ref, bf16[32,64,192]{2,1,0:T(8,128)(2,1)} %get-tuple-element.14.current_ref, f32[2,3,192]{2,1,0:T(4,128)} %copy.9.gain_ref.refs_6_.refs_7_), custom_call_target="tpu_custom_call" | custom-call | tf_op jit(solution)/shard_map/residual/pallas_call | solution.py:306
  121.7 1.0 fusion.1
  122.7 1.3 collective-permute-start.5
  124.0 1.0 fusion
  125.0 5.5 %collective-permute-start.4 = (bf16[3,64,192]{2,1,0:T(8,128)(2,1)S(1)}, bf16[3,64,192]{2,1,0:T(8,128)(2,1)S(1)}, u32[]{:S(2)}, u32[]{:S(2)}) collective-permute-start(bf16[3,64,192]{2,1,0:T(8,128)(2,1)S(1)} %get-tuple-element.20), channel_id=1, source_target_pairs={{0,16},{16,32},{32,48},{48,64},{64,80},{80,96},{96,112},{1,17},{17... | collective-permute-start | bytes 221192 | tf_op jit(solution)/shard_map/ppermute | solution.py:441
  130.5 0.0 collective-permute-done.5.refs_3_
  130.5 1.8 %collective-permute-done.4.refs_2_ = bf16[3,64,192]{2,1,0:T(8,128)(2,1)S(1)} collective-permute-done((bf16[3,64,192]{2,1,0:T(8,128)(2,1)S(1)}, bf16[3,64,192]{2,1,0:T(8,128)(2,1)S(1)}, u32[]{:S(2)}, u32[]{:S(2)}) %collective-permute-start.4) | collective-permute-done | bytes 73760 | tf_op jit(solution)/shard_map/ppermute | solution.py:441
  132.4 3.2 %collective-permute-start.6 = (bf16[38,8,192]{2,1,0:T(8,128)(2,1)S(1)}, bf16[38,8,192]{2,1,0:T(8,128)(2,1)S(1)}, u32[]{:S(2)}, u32[]{:S(2)}) collective-permute-start(bf16[38,8,192]{2,1,0:T(8,128)(2,1)S(1)} %pad_maximum_fusion.2), channel_id=1, source_target_pairs={{0,1},{1,2},{2,3},{3,4},{4,5},{5,6},{6,7},{7,8},{8,9},{9,10},{10,1... | collective-permute-start | bytes 350216 | tf_op jit(solution)/shard_map/ppermute | solution.py:441
  135.6 1.9 %collective-permute-start.7 = (bf16[38,8,192]{2,1,0:T(8,128)(2,1)S(1)}, bf16[38,8,192]{2,1,0:T(8,128)(2,1)S(1)}, u32[]{:S(2)}, u32[]{:S(2)}) collective-permute-start(bf16[38,8,192]{2,1,0:T(8,128)(2,1)S(1)} %pad_maximum_fusion.3), channel_id=1, source_target_pairs={{1,0},{2,1},{3,2},{4,3},{5,4},{6,5},{7,6},{8,7},{9,8},{10,9},{11,1... | collective-permute-start | bytes 350216 | tf_op jit(solution)/shard_map/ppermute | solution.py:441
  137.6 0.2 collective-permute-done.6.refs_4_
  137.8 4.4 %collective-permute-done.7.refs_5_ = bf16[38,8,192]{2,1,0:T(8,128)(2,1)S(1)} collective-permute-done((bf16[38,8,192]{2,1,0:T(8,128)(2,1)S(1)}, bf16[38,8,192]{2,1,0:T(8,128)(2,1)S(1)}, u32[]{:S(2)}, u32[]{:S(2)}) %collective-permute-start.7) | collective-permute-done | bytes 116768 | tf_op jit(solution)/shard_map/ppermute | solution.py:441
  142.2 0.7 copy-done.4
  142.9 11.9 %finish_layer.3 = bf16[32,64,192]{2,1,0:T(8,128)(2,1)} custom-call(f32[32,64,192]{2,1,0:T(8,128)} %get-tuple-element.15.refs_0_, bf16[32,64,192]{2,1,0:T(8,128)(2,1)} %get-tuple-element.16.refs_1_, bf16[3,64,192]{2,1,0:T(8,128)(2,1)} %copy-done.8, bf16[3,64,192]{2,1,0:T(8,128)(2,1)} %copy-done.6, bf16[38,8,192]{2,1,0:T(8,128)(2,1)} %copy-done.2, ...), custom_call_target="tpu_custom_call" | custom-call | tf_op jit(solution)/shard_map/finish_layer/pallas_call | solution.py:411
  (27 shorter events, 0.2 us)
Async XLA Ops:
  0.0 34.0 %copy-start.9 = (f32[2,49,192]{2,0,1:T(2,128)S(1)}, f32[2,49,192]{2,0,1:T(2,128)}, u32[]{:S(2)}) copy-start(f32[2,49,192]{2,0,1:T(2,128)} %param.13) | copy-start | bytes 225796
  0.0 34.6 %copy-start = (bf16[2,768,192]{1,2,0:T(8,128)(2,1)S(1)}, bf16[2,768,192]{1,2,0:T(8,128)(2,1)}, u32[]{:S(2)}) copy-start(bf16[2,768,192]{1,2,0:T(8,128)(2,1)} %param.15) | copy-start | bytes 1769476
  16.8 8.6 %collective-permute-start.1 = (bf16[3,64,192]{2,1,0:T(8,128)(2,1)S(1)}, bf16[3,64,192]{2,1,0:T(8,128)(2,1)S(1)}, u32[]{:S(2)}, u32[]{:S(2)}) collective-permute-start(bf16[3,64,192]{2,1,0:T(8,128)(2,1)S(1)} %get-tuple-element.23), channel_id=1, source_target_pairs={{16,0},{32,16},{48,32},{64,48},{80,64},{96,80},{112,96},{17,1},{33... | collective-permute-start | bytes 221192 | tf_op jit(solution)/shard_map/ppermute | solution.py:441
  18.1 9.7 %collective-permute-start = (bf16[3,64,192]{2,1,0:T(8,128)(2,1)S(1)}, bf16[3,64,192]{2,1,0:T(8,128)(2,1)S(1)}, u32[]{:S(2)}, u32[]{:S(2)}) collective-permute-start(bf16[3,64,192]{2,1,0:T(8,128)(2,1)S(1)} %get-tuple-element.24), channel_id=1, source_target_pairs={{0,16},{16,32},{32,48},{48,64},{64,80},{80,96},{96,112},{1,17},{17... | collective-permute-start | bytes 221192 | tf_op jit(solution)/shard_map/ppermute | solution.py:441
  25.4 13.2 %copy-start.5 = (bf16[3,64,192]{2,1,0:T(8,128)(2,1)}, bf16[3,64,192]{2,1,0:T(8,128)(2,1)S(1)}, u32[]{:S(2)}) copy-start(bf16[3,64,192]{2,1,0:T(8,128)(2,1)S(1)} %collective-permute-done.1.refs_3_) | copy-start | bytes 221188
  27.8 10.8 %copy-start.7 = (bf16[3,64,192]{2,1,0:T(8,128)(2,1)}, bf16[3,64,192]{2,1,0:T(8,128)(2,1)S(1)}, u32[]{:S(2)}) copy-start(bf16[3,64,192]{2,1,0:T(8,128)(2,1)S(1)} %collective-permute-done.refs_2_) | copy-start | bytes 221188
  27.9 8.0 %collective-permute-start.2 = (bf16[38,8,192]{2,1,0:T(8,128)(2,1)S(1)}, bf16[38,8,192]{2,1,0:T(8,128)(2,1)S(1)}, u32[]{:S(2)}, u32[]{:S(2)}) collective-permute-start(bf16[38,8,192]{2,1,0:T(8,128)(2,1)S(1)} %pad_maximum_fusion), channel_id=1, source_target_pairs={{0,1},{1,2},{2,3},{3,4},{4,5},{5,6},{6,7},{7,8},{8,9},{9,10},{10,1... | collective-permute-start | bytes 350216 | tf_op jit(solution)/shard_map/ppermute | solution.py:441
  32.0 6.5 %collective-permute-start.3 = (bf16[38,8,192]{2,1,0:T(8,128)(2,1)S(1)}, bf16[38,8,192]{2,1,0:T(8,128)(2,1)S(1)}, u32[]{:S(2)}, u32[]{:S(2)}) collective-permute-start(bf16[38,8,192]{2,1,0:T(8,128)(2,1)S(1)} %pad_maximum_fusion.1), channel_id=1, source_target_pairs={{1,0},{2,1},{3,2},{4,3},{5,4},{6,5},{7,6},{8,7},{9,8},{10,9},{11,1... | collective-permute-start | bytes 350216 | tf_op jit(solution)/shard_map/ppermute | solution.py:441
  35.8 2.8 %copy-start.1 = (bf16[38,8,192]{2,1,0:T(8,128)(2,1)}, bf16[38,8,192]{2,1,0:T(8,128)(2,1)S(1)}, u32[]{:S(2)}) copy-start(bf16[38,8,192]{2,1,0:T(8,128)(2,1)S(1)} %collective-permute-done.2.refs_4_) | copy-start | bytes 350212
  38.6 0.7 copy-start.3
  122.7 7.8 %collective-permute-start.5 = (bf16[3,64,192]{2,1,0:T(8,128)(2,1)S(1)}, bf16[3,64,192]{2,1,0:T(8,128)(2,1)S(1)}, u32[]{:S(2)}, u32[]{:S(2)}) collective-permute-start(bf16[3,64,192]{2,1,0:T(8,128)(2,1)S(1)} %get-tuple-element.19), channel_id=1, source_target_pairs={{16,0},{32,16},{48,32},{64,48},{80,64},{96,80},{112,96},{17,1},{33... | collective-permute-start | bytes 221192 | tf_op jit(solution)/shard_map/ppermute | solution.py:441
  125.0 7.4 %collective-permute-start.4 = (bf16[3,64,192]{2,1,0:T(8,128)(2,1)S(1)}, bf16[3,64,192]{2,1,0:T(8,128)(2,1)S(1)}, u32[]{:S(2)}, u32[]{:S(2)}) collective-permute-start(bf16[3,64,192]{2,1,0:T(8,128)(2,1)S(1)} %get-tuple-element.20), channel_id=1, source_target_pairs={{0,16},{16,32},{32,48},{48,64},{64,80},{80,96},{96,112},{1,17},{17... | collective-permute-start | bytes 221192 | tf_op jit(solution)/shard_map/ppermute | solution.py:441
  130.5 11.7 %copy-start.6 = (bf16[3,64,192]{2,1,0:T(8,128)(2,1)}, bf16[3,64,192]{2,1,0:T(8,128)(2,1)S(1)}, u32[]{:S(2)}) copy-start(bf16[3,64,192]{2,1,0:T(8,128)(2,1)S(1)} %collective-permute-done.5.refs_3_) | copy-start | bytes 221188
  132.4 9.8 %copy-start.8 = (bf16[3,64,192]{2,1,0:T(8,128)(2,1)}, bf16[3,64,192]{2,1,0:T(8,128)(2,1)S(1)}, u32[]{:S(2)}) copy-start(bf16[3,64,192]{2,1,0:T(8,128)(2,1)S(1)} %collective-permute-done.4.refs_2_) | copy-start | bytes 221188
  132.4 5.4 %collective-permute-start.6 = (bf16[38,8,192]{2,1,0:T(8,128)(2,1)S(1)}, bf16[38,8,192]{2,1,0:T(8,128)(2,1)S(1)}, u32[]{:S(2)}, u32[]{:S(2)}) collective-permute-start(bf16[38,8,192]{2,1,0:T(8,128)(2,1)S(1)} %pad_maximum_fusion.2), channel_id=1, source_target_pairs={{0,1},{1,2},{2,3},{3,4},{4,5},{5,6},{6,7},{7,8},{8,9},{9,10},{10,1... | collective-permute-start | bytes 350216 | tf_op jit(solution)/shard_map/ppermute | solution.py:441
  135.6 6.5 %collective-permute-start.7 = (bf16[38,8,192]{2,1,0:T(8,128)(2,1)S(1)}, bf16[38,8,192]{2,1,0:T(8,128)(2,1)S(1)}, u32[]{:S(2)}, u32[]{:S(2)}) collective-permute-start(bf16[38,8,192]{2,1,0:T(8,128)(2,1)S(1)} %pad_maximum_fusion.3), channel_id=1, source_target_pairs={{1,0},{2,1},{3,2},{4,3},{5,4},{6,5},{7,6},{8,7},{9,8},{10,9},{11,1... | collective-permute-start | bytes 350216 | tf_op jit(solution)/shard_map/ppermute | solution.py:441
  137.8 4.4 %copy-start.2 = (bf16[38,8,192]{2,1,0:T(8,128)(2,1)}, bf16[38,8,192]{2,1,0:T(8,128)(2,1)S(1)}, u32[]{:S(2)}) copy-start(bf16[38,8,192]{2,1,0:T(8,128)(2,1)S(1)} %collective-permute-done.6.refs_4_) | copy-start | bytes 350212
  142.2 0.7 copy-start.4
where the time goes:
time: 157 us; the launch traced here: 155 us
  Pallas kernels  58.5 us (37%)
  blocking collectives  49.1 us (31%)
  starting transfers between devices  25.5 us (16%)
  waiting for transfers between devices  11.6 us (7%)
  local copies, waits for them, and re-layouts  9.75 us (6%)
    all_to_all x1, blocking collectives, on_device(): got = lax.all_to_all(outgoing, members, 0, 0, tiled=True)  27.8 us
    ppermute x8, starting transfers between devices, shift(): return lax.ppermute(value, axes, pairs)  25.5 us
    pallas_call x2, Pallas kernels, finish_layer(): pl.pallas_call(functools.partial(finish_kernel, send), grid=(steps,), in_...  24.8 us
    all_to_all x1, blocking collectives, on_device(): back = lax.all_to_all(branch, members, 0, 0, tiled=True)  21.3 us
    pallas_call x1, Pallas kernels, shuffled_attention(): pl.pallas_call(shuffled_kernel, grid=(1,), in_specs=[block, whole(D, 3 *...  16.4 us
    pallas_call x1, Pallas kernels, plain_attention(): pl.pallas_call(plain_kernel, grid=(height // WS,), in_specs=[block, whole...  13.2 us
    ppermute x8, waiting for transfers between devices, shift(): return lax.ppermute(value, axes, pairs)  11.6 us
    unnamed x24, local copies, waits for them, and re-layouts  5.85 us
  transfers between devices with their start and end apart: 8, of which 5 were waited for; matrix products, arithmetic and copies ran while one was open for 3% of the time, Pallas kernels for 0%

commit v1 on v0

v1 whole, which is shorter than its diff:
```python
import functools
import jax
import jax.numpy as jnp
from jax import lax
from jax.experimental import pallas as pl
from jax.experimental.pallas import tpu as pltpu
from jax.sharding import Mesh, PartitionSpec as P

D = 192
HEADS = 6
HID = 768
WS = 8
KS = 7
HEAD = 32
AREA = WS * WS
PAD = 256
LANES = 128
HALO = KS // 2
TOGETHER = 4
WINDOW_ROWS = AREA + 8
PIECE_ROWS = 24
RETURN_ROWS = 40
RING = 80
SEGMENT = 16
EPSILON = 1e-05

f32 = jnp.float32
bf16 = jnp.bfloat16


def layer_norm(values, gain):
    centre = jnp.mean(values, axis=-1, keepdims=True)
    centred = values - centre
    spread = jnp.mean(centred * centred, axis=-1, keepdims=True)
    return centred * lax.rsqrt(spread + EPSILON) * gain


def mxu(a, b):
    return jnp.dot(a, b, preferred_element_type=f32)


def prepare_attention(table_ref, qkv_ref, bias_s, rows_s, qkv_s):
    table = table_ref[0]
    high = table.astype(bf16)
    rest = table - high.astype(f32)
    middle = rest.astype(bf16)
    low = (rest - middle.astype(f32)).astype(bf16)
    entries = (2 * WS - 1) ** 2
    lane = lax.broadcasted_iota(jnp.int32, (entries, WS * LANES), 1)
    entry = lax.broadcasted_iota(jnp.int32, (entries, WS * LANES), 0)
    target = (
        (2 * WS - 2 - ((lane & (LANES - 1)) >> 3)) * (2 * WS - 1)
        + (lane >> 7)
        - (lane & 7)
        + WS
        - 1
    )
    chosen = jnp.where(entry == target, 1.0, 0.0).astype(bf16)
    spread = mxu(high, chosen) + mxu(middle, chosen) + mxu(low, chosen)
    for place in range(WS):
        rows_s[place, 0:HEADS, :] = spread[:, place * LANES : (place + 1) * LANES]
    first = lax.broadcasted_iota(jnp.int32, (WS, LANES), 1) < AREA
    for group in range(HEADS // 2):
        left = rows_s[:, 2 * group, :]
        right = rows_s[:, 2 * group + 1, :]
        for row in range(WS):
            shift = LANES - (WS - 1 - row) * WS
            piece = jnp.where(
                first,
                pltpu.roll(left, shift % LANES, 1),
                pltpu.roll(right, (shift + AREA) % LANES, 1),
            )
            bias_s[group * AREA + row * WS : group * AREA + (row + 1) * WS, :] = piece
    weights = qkv_ref[0].astype(f32)
    gap = jnp.zeros((D, PAD - D), f32)
    qkv_s[...] = jnp.concatenate(
        [
            weights[:, 0:D],
            gap,
            weights[:, D : 2 * D],
            gap,
            weights[:, 2 * D : 3 * D],
            gap,
        ],
        axis=1,
    ).astype(bf16)


def attention_masks():
    lane = lax.broadcasted_iota(jnp.int32, (1, PAD), 1)
    groups = [
        jnp.where((lane >> 6) == g, 1.0, 0.0).astype(bf16) for g in range(HEADS // 2)
    ]
    parities = [
        jnp.where(((lane >> 5) & 1) == h, 1.0, 0.0).astype(bf16) for h in range(2)
    ]
    rows = lax.broadcasted_iota(jnp.int32, (LANES, LANES), 0) >> 6
    cols = lax.broadcasted_iota(jnp.int32, (LANES, LANES), 1) >> 6
    summing = jnp.where(rows == cols, 1.0, 0.0).astype(bf16)
    return groups, parities, summing


def attend(projected, bias, masks):
    groups, parities, summing = masks
    count = projected.shape[0] // AREA
    window = lambda n, t: projected[n * AREA : (n + 1) * AREA, t * PAD : (t + 1) * PAD]
    spread = lambda x, ms: jnp.concatenate([x * m for m in ms], axis=0)
    scores = [
        lax.dot_general(
            spread(window(n, 0), groups),
            spread(window(n, 1), parities),
            (((1,), (1,)), ((), ())),
            preferred_element_type=f32,
        )
        for n in range(count)
    ]
    weights = [jnp.exp(x * HEAD ** (-0.5) + bias) for x in scores]
    totals = [mxu(x.astype(bf16), summing) for x in weights]
    weights = [(x / y).astype(bf16) for x, y in zip(weights, totals)]
    mixed = [mxu(x, spread(window(n, 2), parities)) for n, x in enumerate(weights)]
    lane = lax.broadcasted_iota(jnp.int32, (AREA, PAD), 1) >> 6
    return [
        jnp.where(
            lane == 0, x[0:AREA], jnp.where(lane == 1, x[AREA : 2 * AREA], x[2 * AREA :])
        )[:, 0:D].astype(bf16)
        for x in mixed
    ]


def attention(current, gain, qkv, proj, bias, masks, together):
    normed = layer_norm(current, gain).astype(bf16)
    projected = mxu(normed, qkv).astype(bf16)
    outs = []
    for start in range(0, current.shape[0], together * AREA):
        outs += attend(projected[start : start + together * AREA], bias, masks)
    return current + mxu(jnp.concatenate(outs, axis=0), proj)


def plain_kernel(
    x_ref, gain_ref, qkv_ref, proj_ref, table_ref, sum_ref, normed_ref, bias_s, rows_s, qkv_s
):
    @pl.when(pl.program_id(0) == 0)
    def _():
        prepare_attention(table_ref, qkv_ref, bias_s, rows_s, qkv_s)

    cols = x_ref.shape[1]
    count = cols // WS
    grid = x_ref[...].astype(f32)
    current = jnp.concatenate(
        [grid[:, j * WS : (j + 1) * WS, :].reshape(AREA, D) for j in range(count)], axis=0
    )
    after = attention(
        current,
        gain_ref[0, 0:1, :],
        qkv_s[...],
        proj_ref[0],
        bias_s[...],
        attention_masks(),
        TOGETHER,
    )
    normed_two = layer_norm(after, gain_ref[0, 1:2, :])

    def spatial(value):
        return jnp.concatenate(
            [value[j * AREA : (j + 1) * AREA].reshape(WS, WS, D) for j in range(count)], axis=1
        )

    sum_ref[...] = spatial(after)
    normed_ref[...] = spatial(normed_two).astype(bf16)


def attention_scratch():
    return [
        pltpu.VMEM((HEADS // 2 * AREA, LANES), f32),
        pltpu.VMEM((WS, WS, LANES), f32),
        pltpu.VMEM((D, 3 * PAD), bf16),
    ]


def plain_attention(tokens, norm_gain, qkv_weight, proj_weight, bias_table, layer):
    height, width = tokens.shape[:2]
    whole = lambda *shape: pl.BlockSpec(
        (1, *shape), lambda i: (layer,) + (0,) * len(shape)
    )
    block = pl.BlockSpec((WS, width, D), lambda i: (i, 0, 0))
    return pl.pallas_call(
        plain_kernel,
        grid=(height // WS,),
        in_specs=[
            block,
            whole(3, D),
            whole(D, 3 * D),
            whole(D, D),
            whole(HEADS, (2 * WS - 1) ** 2),
        ],
        out_specs=[block, block],
        out_shape=[
            jax.ShapeDtypeStruct(tokens.shape, f32),
            jax.ShapeDtypeStruct(tokens.shape, bf16),
        ],
        scratch_shapes=attention_scratch(),
        name="plain_attention",
    )(tokens, norm_gain, qkv_weight, proj_weight, bias_table)


def low_half(value):
    lane = lax.broadcasted_iota(jnp.int32, value.shape, value.ndim - 1)
    return jnp.where(lane < D - LANES, value, 0.0)


def join_halves(first, second):
    lane = lax.broadcasted_iota(jnp.int32, first.shape, 1)
    return jnp.where(lane < D - LANES, first, pltpu.roll(second, D - LANES, 1))


def shuffled_kernel(
    got_ref, gain_ref, qkv_ref, proj_ref, table_ref, out_ref, bias_s, rows_s, qkv_s, window_s, piece_s
):
    prepare_attention(table_ref, qkv_ref, bias_s, rows_s, qkv_s)
    blocks = WS * 2

    def gather(a, carry):
        for c in range(blocks):
            piece = got_ref[a * blocks + c].astype(f32)
            upper = piece[SEGMENT:]
            upper = jnp.concatenate(
                [low_half(upper), low_half(pltpu.roll(upper, D - LANES, 1))], axis=0
            )
            place = pl.ds(
                (c % 2) * SEGMENT * WINDOW_ROWS + a * WS + c // 2, SEGMENT, stride=WINDOW_ROWS
            )
            window_s[0, place, :] = piece[:SEGMENT]
            window_s[1, place, :] = upper
        return carry

    lax.fori_loop(0, WS, gather, 0)
    masks = attention_masks()

    def windows(c, carry):
        starts = [
            pl.multiple_of((c * TOGETHER + n) * WINDOW_ROWS, 8) for n in range(TOGETHER)
        ]
        current = jnp.concatenate(
            [
                jnp.concatenate(
                    [window_s[t, pl.ds(start, AREA), :] for start in starts], axis=0
                )
                for t in range(2)
            ],
            axis=1,
        )[:, 0:D]
        after = attention(
            current, gain_ref[0, 0:1, :], qkv_s[...], proj_ref[0], bias_s[...], masks, TOGETHER
        )
        for n, start in enumerate(starts):
            window_s[0, pl.ds(start, AREA), :] = after[n * AREA : (n + 1) * AREA, 0:LANES]
            window_s[1, pl.ds(start, AREA), 0 : D - LANES] = after[
                n * AREA : (n + 1) * AREA, LANES:D
            ]
        return carry

    lax.fori_loop(0, 2 * SEGMENT // TOGETHER, windows, 0)

    below = lax.axis_index("row") < WS // 2
    beside = lax.axis_index("block") < WS // 2
    row_step = jnp.where(below, 1, -1)
    row_window = jnp.where(below, 0, 3)
    col_window = jnp.where(beside, 0, 3)

    def scatter(a, carry):
        other_a = a + row_step
        row_keep = jnp.where((other_a >= 0) & (other_a < WS), 1.0, 0.0).astype(f32)
        other_a = jnp.clip(other_a, 0, WS - 1)
        for c in range(blocks):
            b, core = c // 2, c % 2
            other_b = b + (jnp.where(beside, 1, 0) if core else jnp.where(beside, 0, -1))
            col_keep = jnp.where((other_b >= 0) & (other_b < WS), 1.0, 0.0).astype(f32)
            other_b = jnp.clip(other_b, 0, WS - 1)
            base = core * SEGMENT
            other = (1 - core) * SEGMENT
            main = pl.ds(base * WINDOW_ROWS + a * WS + b, SEGMENT, stride=WINDOW_ROWS)
            row = pl.ds(
                (base + row_window * 4) * WINDOW_ROWS + other_a * WS + b, 4, stride=WINDOW_ROWS
            )
            col = pl.ds(
                (other + col_window) * WINDOW_ROWS + a * WS + other_b, 4, stride=4 * WINDOW_ROWS
            )
            corner = pl.ds(
                (other + row_window * 4 + col_window) * WINDOW_ROWS + other_a * WS + other_b, 1
            )
            keep = row_keep * col_keep
            piece_s[0:16] = window_s[0, main, :]
            piece_s[16:20] = window_s[0, row, :] * row_keep
            piece_s[20:24] = window_s[0, col, :] * col_keep
            upper = window_s[1, main, :]
            piece_s[24:32] = join_halves(upper[0:8], upper[8:16])
            piece_s[32:36] = join_halves(
                window_s[1, row, :] * row_keep, window_s[1, col, :] * col_keep
            )
            piece_s[36:37] = window_s[0, corner, :] * keep
            piece_s[37:38] = window_s[1, corner, :] * keep
            out_ref[a * blocks + c] = piece_s[...].astype(bf16)
        return carry

    piece_s[...] = jnp.zeros_like(piece_s)
    lax.fori_loop(0, WS, scatter, 0)


def shuffled_attention(got, norm_gain, qkv_weight, proj_weight, bias_table, layer):
    whole = lambda *shape: pl.BlockSpec(
        (1, *shape), lambda i: (layer,) + (0,) * len(shape)
    )
    shape = (got.shape[0], RETURN_ROWS, LANES)
    return pl.pallas_call(
        shuffled_kernel,
        grid=(1,),
        in_specs=[
            pl.BlockSpec(got.shape, lambda i: (0, 0, 0)),
            whole(3, D),
            whole(D, 3 * D),
            whole(D, D),
            whole(HEADS, (2 * WS - 1) ** 2),
        ],
        out_specs=pl.BlockSpec(shape, lambda i: (0, 0, 0)),
        out_shape=jax.ShapeDtypeStruct(shape, bf16),
        scratch_shapes=attention_scratch()
        + [
            pltpu.VMEM((2, 2 * SEGMENT * WINDOW_ROWS, LANES), f32),
            pltpu.VMEM((RETURN_ROWS, LANES), f32),
        ],
        name="shuffled_attention",
    )(got, norm_gain, qkv_weight, proj_weight, bias_table)


def broadcast_taps(taps_ref, taps_s):
    for t in range(KS * KS):
        taps_s[t] = jnp.broadcast_to(taps_ref[0, t : t + 1, :], (16, D)).astype(bf16)


def convolve_row(padded_s, taps_s, row, width):
    total = None
    for v in range(KS):
        part = None
        for u in range(KS):
            x = padded_s[row + u].reshape(-1, 16, D)
            term = x * taps_s[u * KS + v][None]
            part = term if part is None else part + term
        part = part.reshape(-1, D).astype(f32)
        shift = v - HALO
        if shift < 0:
            part = jnp.concatenate([part[RING + shift :], part[: width + shift]], axis=0)
        else:
            part = part[shift : shift + width]
        total = part if total is None else total + part
    return total


def feed_forward(after, gain, up, down):
    normed = layer_norm(after, gain).astype(bf16)
    raised = mxu(normed, up)
    hidden = (0.5 * raised * (1.0 + lax.erf(raised * 0.5**0.5))).astype(bf16)
    return (after + mxu(hidden, down)).astype(bf16)


def first_kernel(
    sum_ref,
    normed_ref,
    top_ref,
    bottom_ref,
    left_ref,
    right_ref,
    gain_ref,
    taps_ref,
    up_ref,
    down_ref,
    send_ref,
    padded_s,
    after_s,
    taps_s,
    piece_s,
):
    step = pl.program_id(0)
    height, width, _ = normed_ref.shape
    repeats, rows = sum_ref.shape[:2]

    @pl.when(step == 0)
    def _():
        def place(r, middle):
            padded_s[r] = jnp.concatenate(
                [middle.astype(f32), right_ref[r].astype(f32), left_ref[r].astype(f32)], axis=0
            ).astype(bf16)

        for r in range(HALO):
            place(r, top_ref[r])
            place(height + HALO + r, bottom_ref[r])

        def body(r, carry):
            place(r + HALO, normed_ref[r])
            return carry

        lax.fori_loop(0, height, body, 0)
        broadcast_taps(taps_ref, taps_s)

    def row(j, carry):
        m, q = j // rows, j % rows
        total = sum_ref[m, q] + convolve_row(
            padded_s, taps_s, m * WS + step * rows + q, width
        )
        after_s[pl.ds(pl.multiple_of(j * width, width), width), :] = total
        return carry

    lax.fori_loop(0, repeats * rows, row, 0)
    outcome = feed_forward(after_s[...], gain_ref[0, 2:3, :], up_ref[0], down_ref[0]).astype(f32)
    for m in range(repeats):
        for q in range(rows):
            for n in range(width // SEGMENT):
                start = (m * rows + q) * width + n * SEGMENT
                value = outcome[start : start + SEGMENT]
                place = pl.ds((q * SEGMENT + m * 4 + n) * PIECE_ROWS, SEGMENT)
                piece_s[0, place, :] = value[:, 0:LANES]
                piece_s[1, place, 0 : D - LANES] = value[:, LANES:D]
    for q in range(rows):
        for c in range(SEGMENT):
            place = pl.ds(q * SEGMENT * PIECE_ROWS + c, SEGMENT, stride=PIECE_ROWS)
            upper = piece_s[1, place, :]
            send_ref[q * SEGMENT + c] = jnp.concatenate(
                [piece_s[0, place, :], join_halves(upper[0:8], upper[8:16])], axis=0
            ).astype(bf16)


def first_finish(after, normed, halo, norm_gain, conv_weight, up_weight, down_weight, layer, group):
    height, width = normed.shape[:2]
    repeats = height // WS
    rows = WS // repeats
    whole = lambda *shape: pl.BlockSpec(
        (1, *shape), lambda i: (layer,) + (0,) * len(shape)
    )
    full = lambda a: pl.BlockSpec(a.shape, lambda i: (0,) * a.ndim)
    return pl.pallas_call(
        first_kernel,
        grid=(WS // rows,),
        in_specs=[
            pl.BlockSpec((repeats, rows, width, D), lambda i: (0, i, 0, 0)),
            full(normed),
            *[full(h) for h in halo],
            whole(3, D),
            whole(KS * KS, D),
            whole(D, HID),
            whole(HID, D),
        ],
        out_specs=pl.BlockSpec((rows * SEGMENT, PIECE_ROWS, LANES), lambda i: (i, 0, 0)),
        out_shape=jax.ShapeDtypeStruct((group, PIECE_ROWS, LANES), bf16),
        scratch_shapes=[
            pltpu.VMEM((height + 2 * HALO, RING, D), bf16),
            pltpu.VMEM((repeats * rows * width, D), f32),
            pltpu.VMEM((KS * KS, 16, D), bf16),
            pltpu.VMEM((2, rows * SEGMENT * PIECE_ROWS, LANES), f32),
        ],
        name="first_finish",
    )(
        after.reshape(repeats, WS, width, D),
        normed,
        *halo,
        norm_gain,
        conv_weight,
        up_weight,
        down_weight,
    )


def second_kernel(
    back_ref,
    gain_ref,
    taps_ref,
    up_ref,
    down_ref,
    out_ref,
    padded_s,
    sum_s,
    after_s,
    taps_s,
    piece_s,
):
    step = pl.program_id(0)
    rows, width, _ = out_ref.shape
    height = sum_s.shape[0]
    repeats = height // WS

    @pl.when(step == 0)
    def _():
        broadcast_taps(taps_ref, taps_s)

        def build(r, n, target, keep):
            pieces = []
            for m in range(width // SEGMENT + 1):
                if n < 4 and m < 4:
                    low, high, half = 4 * n + m, 24 + (4 * n + m) % 8, (4 * n + m) // 8
                elif m < 4:
                    low, high, half = 16 + m, 32 + m, 0
                elif n < 4:
                    low, high, half = 20 + n, 32 + n, 1
                else:
                    low, high, half = 36, 37, 0
                at = lambda k: piece_s[pl.ds(k, SEGMENT, stride=RETURN_ROWS), :]
                upper = at(high)
                if half:
                    upper = pltpu.roll(upper, D - LANES, 1)
                pieces.append(jnp.concatenate([at(low), upper], axis=1)[:, 0:D])
            value = jnp.concatenate(pieces, axis=0)
            if keep:
                sum_s[target - HALO] = value[0:width]
            padded_s[target] = layer_norm(value, gain_ref[0, 1:2, :]).astype(bf16)

        def body(r, carry):
            def load(c, carry):
                piece_s[pl.ds(pl.multiple_of(c * RETURN_ROWS, 8), RETURN_ROWS), :] = back_ref[
                    r * SEGMENT + c
                ].astype(f32)
                return carry

            lax.fori_loop(0, SEGMENT, load, 0, unroll=True)
            for n in range(repeats):
                build(r, n, HALO + r + WS * n, True)

            @pl.when(r < HALO)
            def _():
                build(r, repeats, HALO + height + r, False)

            @pl.when(r >= WS - HALO)
            def _():
                build(r, repeats, HALO + r - WS, False)

            return carry

        lax.fori_loop(0, WS, body, 0)

    def row(j, carry):
        r = step * rows + j
        total = sum_s[r] + convolve_row(padded_s, taps_s, r, width)
        after_s[pl.ds(pl.multiple_of(j * width, width), width), :] = total
        return carry

    lax.fori_loop(0, rows, row, 0)
    outcome = feed_forward(after_s[...], gain_ref[0, 2:3, :], up_ref[0], down_ref[0])
    out_ref[...] = outcome.reshape(rows, width, D)


def second_finish(back, shape, norm_gain, conv_weight, up_weight, down_weight, layer):
    height, width = shape[:2]
    whole = lambda *shape: pl.BlockSpec(
        (1, *shape), lambda i: (layer,) + (0,) * len(shape)
    )
    return pl.pallas_call(
        second_kernel,
        grid=(height // WS,),
        in_specs=[
            pl.BlockSpec(back.shape, lambda i: (0, 0, 0)),
            whole(3, D),
            whole(KS * KS, D),
            whole(D, HID),
            whole(HID, D),
        ],
        out_specs=pl.BlockSpec((WS, width, D), lambda i: (i, 0, 0)),
        out_shape=jax.ShapeDtypeStruct(shape, bf16),
        scratch_shapes=[
            pltpu.VMEM((height + 2 * HALO, RING, D), bf16),
            pltpu.VMEM((height, width, D), f32),
            pltpu.VMEM((WS * width, D), f32),
            pltpu.VMEM((KS * KS, 16, D), bf16),
            pltpu.VMEM((SEGMENT * RETURN_ROWS, LANES), f32),
        ],
        name="second_finish",
    )(back, norm_gain, conv_weight, up_weight, down_weight)


def halo_of(normed):
    height, width = normed.shape[:2]

    def shift(value, axes, forward):
        count = lax.axis_size(axes)
        pairs = [(i, i + 1) if forward else (i + 1, i) for i in range(count - 1)]
        return lax.ppermute(value, axes, pairs)

    top = shift(normed[height - HALO :], "row", True)
    bottom = shift(normed[:HALO], "row", False)
    columns = lambda part: jnp.concatenate([part(top), part(normed), part(bottom)], axis=0)
    left = shift(columns(lambda a: a[:, width - WS :]), ("block", "core"), True)
    right = shift(columns(lambda a: a[:, :WS]), ("block", "core"), False)
    return top, bottom, left, right


def on_device(
    tokens, norm_gain, qkv_weight, proj_weight, bias_table, conv_weight, up_weight, down_weight
):
    members = ("row", "block", "core")
    after, normed = plain_attention(tokens, norm_gain, qkv_weight, proj_weight, bias_table, 0)
    outgoing = first_finish(
        after,
        normed,
        halo_of(normed),
        norm_gain,
        conv_weight,
        up_weight,
        down_weight,
        0,
        lax.axis_size(members),
    )
    got = lax.all_to_all(outgoing, members, 0, 0, tiled=True)
    branch = shuffled_attention(got, norm_gain, qkv_weight, proj_weight, bias_table, 1)
    back = lax.all_to_all(branch, members, 0, 0, tiled=True)
    return second_finish(back, tokens.shape, norm_gain, conv_weight, up_weight, down_weight, 1)


def solution(mesh):
    split = Mesh(
        mesh.devices.reshape(mesh.shape["row"], mesh.shape["col"] // 2, 2), ("row", "block", "core")
    )
    spec = P("row", ("block", "core"), None)
    return jax.shard_map(
        on_device, mesh=split, in_specs=(spec,) + (P(),) * 7, out_specs=spec, check_vma=False
    )
```

time: 157 us -> 133 us (0.85)
  starting transfers between devices: 25.5 us -> 13.6 us
  Pallas kernels: 58.5 us -> 50.9 us
  waiting for transfers between devices: 11.6 us -> 5.18 us
  blocking collectives: 49.1 us -> 55.4 us
  local copies, waits for them, and re-layouts: 9.75 us -> 7.08 us
    ppermute x8 -> x4, starting transfers between devices: 25.5 us -> 13.6 us  [shift(): return lax.ppermute(value, axes, pairs)]
    ppermute x8 -> x4, waiting for transfers between devices: 11.6 us -> 5.18 us  [shift(): return lax.ppermute(value, axes, pairs)]
    all_to_all x1, blocking collectives: 21.3 us -> 27.7 us  [on_device(): back = lax.all_to_all(branch, members, 0, 0, tiled=True)]
    pallas_call x4 -> x3, Pallas kernels: 45.3 us -> 41.4 us  [the longest x1 15 us: second_finish(): pl.pallas_call(second_kernel, grid=(height // WS,), in_specs=[pl.BlockSpe...]
    pallas_call x1, Pallas kernels: 13.2 us -> 9.45 us  [plain_attention(): pl.pallas_call(plain_kernel, grid=(height // WS,), in_specs=[block, whole...]
    unnamed x24 -> x16, local copies, waits for them, and re-layouts: 5.85 us -> 5.07 us
  transfers between devices with their start and end apart: 8 -> 4, of which waited for: 5 -> 2; matrix products, arithmetic and copies ran while one was open for 3% -> 2% of each run, Pallas kernels for 0% -> 0%
where the time goes in v1:
time: 133 us; the launch traced here: 132 us
  blocking collectives  55.4 us (42%)
  Pallas kernels  50.9 us (38%)
  starting transfers between devices  13.6 us (10%)
  local copies, waits for them, and re-layouts  7.08 us (5%)
  waiting for transfers between devices  5.18 us (4%)
    all_to_all x1, blocking collectives, on_device(): back = lax.all_to_all(branch, members, 0, 0, tiled=True)  27.7 us
    all_to_all x1, blocking collectives, on_device(): got = lax.all_to_all(outgoing, members, 0, 0, tiled=True)  27.7 us
    pallas_call x1, Pallas kernels, second_finish(): pl.pallas_call(second_kernel, grid=(height // WS,), in_specs=[pl.BlockSpe...  15 us
    pallas_call x1, Pallas kernels, shuffled_attention(): pl.pallas_call(shuffled_kernel, grid=(1,), in_specs=[pl.BlockSpec(got.sha...  13.9 us
    ppermute x4, starting transfers between devices, shift(): return lax.ppermute(value, axes, pairs)  13.6 us
    pallas_call x1, Pallas kernels, first_finish(): pl.pallas_call(first_kernel, grid=(WS // rows,), in_specs=[pl.BlockSpec((...  12.5 us
    pallas_call x1, Pallas kernels, plain_attention(): pl.pallas_call(plain_kernel, grid=(height // WS,), in_specs=[block, whole...  9.45 us
    ppermute x4, waiting for transfers between devices, shift(): return lax.ppermute(value, axes, pairs)  5.18 us
  transfers between devices with their start and end apart: 4, of which 2 were waited for; matrix products, arithmetic and copies ran while one was open for 2% of the time, Pallas kernels for 0%

profile of v1, /device:TPU:1, one launch (start us, length us, event | category | flops | bytes accessed | tf_op | source)
XLA Modules:
  0.0 132.3 jit_solution(15687261772241085896)
XLA Ops:
  0.0 1.3 copy.9.gain_ref
  1.3 1.3 copy.10.table_ref
  2.6 0.0 copy-start.5
  2.6 9.5 %plain_attention.1 = (f32[32,64,192]{2,1,0:T(8,128)}, bf16[32,64,192]{2,1,0:T(8,128)(2,1)}) custom-call(bf16[32,64,192]{2,1,0:T(8,128)(2,1)} %x_ref.1, f32[2,3,192]{2,1,0:T(4,128)} %copy.9.gain_ref, bf16[2,192,576]{2,1,0:T(8,128)(2,1)} %qkv_ref.3, bf16[2,192,192]{2,1,0:T(8,128)(2,1)} %proj_ref.3, f32[2,6,225]{2,1,0:T(8,128)} %copy.10.table_ref), custom_call_target="tpu_custom_call" | custom-call | tf_op jit(solution)/shard_map/plain_attention/pallas_call | solution.py:186
  12.1 0.0 copy-start
  12.1 1.0 fusion.1
  13.1 1.3 collective-permute-start.1
  14.4 6.3 %collective-permute-start = (bf16[3,64,192]{2,1,0:T(8,128)(2,1)S(1)}, bf16[3,64,192]{2,1,0:T(8,128)(2,1)S(1)}, u32[]{:S(2)}, u32[]{:S(2)}) collective-permute-start(bf16[3,64,192]{2,1,0:T(8,128)(2,1)S(1)} %get-tuple-element.12), channel_id=1, source_target_pairs={{0,16},{16,32},{32,48},{48,64},{64,80},{80,96},{96,112},{1,17},{17... | collective-permute-start | bytes 221192 | tf_op jit(solution)/shard_map/ppermute | solution.py:582
  20.7 1.0 fusion
  21.6 0.0 collective-permute-done.1.bottom_ref
  21.7 0.0 copy-start.3
  21.7 2.4 %collective-permute-done.top_ref = bf16[3,64,192]{2,1,0:T(8,128)(2,1)S(1)} collective-permute-done((bf16[3,64,192]{2,1,0:T(8,128)(2,1)S(1)}, bf16[3,64,192]{2,1,0:T(8,128)(2,1)S(1)}, u32[]{:S(2)}, u32[]{:S(2)}) %collective-permute-start) | collective-permute-done | bytes 73760 | tf_op jit(solution)/shard_map/ppermute | solution.py:582
  24.1 0.0 copy-start.4
  24.1 4.1 %collective-permute-start.2 = (bf16[38,8,192]{2,1,0:T(8,128)(2,1)S(1)}, bf16[38,8,192]{2,1,0:T(8,128)(2,1)S(1)}, u32[]{:S(2)}, u32[]{:S(2)}) collective-permute-start(bf16[38,8,192]{2,1,0:T(8,128)(2,1)S(1)} %pad_maximum_fusion), channel_id=1, source_target_pairs={{0,1},{1,2},{2,3},{3,4},{4,5},{5,6},{6,7},{7,8},{8,9},{9,10},{10,1... | collective-permute-start | bytes 350216 | tf_op jit(solution)/shard_map/ppermute | solution.py:582
  28.3 1.9 %collective-permute-start.3 = (bf16[38,8,192]{2,1,0:T(8,128)(2,1)S(1)}, bf16[38,8,192]{2,1,0:T(8,128)(2,1)S(1)}, u32[]{:S(2)}, u32[]{:S(2)}) collective-permute-start(bf16[38,8,192]{2,1,0:T(8,128)(2,1)S(1)} %pad_maximum_fusion.1), channel_id=1, source_target_pairs={{1,0},{2,1},{3,2},{4,3},{5,4},{6,5},{7,6},{8,7},{9,8},{10,9},{11,1... | collective-permute-start | bytes 350216 | tf_op jit(solution)/shard_map/ppermute | solution.py:582
  30.2 0.0 copy-done.5
  30.2 0.6 copy.12.taps_ref
  30.8 0.0 copy-done
  30.8 1.2 copy.13.down_ref
  32.0 0.0 collective-permute-done.2.left_ref
  32.0 0.0 copy-start.1
  32.0 2.8 %collective-permute-done.3.right_ref = bf16[38,8,192]{2,1,0:T(8,128)(2,1)S(1)} collective-permute-done((bf16[38,8,192]{2,1,0:T(8,128)(2,1)S(1)}, bf16[38,8,192]{2,1,0:T(8,128)(2,1)S(1)}, u32[]{:S(2)}, u32[]{:S(2)}) %collective-permute-start.3) | collective-permute-done | bytes 116768 | tf_op jit(solution)/shard_map/ppermute | solution.py:582
  34.8 0.0 copy-start.2
  34.8 0.0 copy-done.3
  34.8 0.0 copy-done.4
  34.8 0.0 copy-done.1
  34.8 0.7 copy-done.2
  35.5 12.5 %first_finish.1 = bf16[128,24,128]{2,1,0:T(8,128)(2,1)} custom-call(f32[4,8,64,192]{3,2,1,0:T(8,128)} %bitcast.1, bf16[32,64,192]{2,1,0:T(8,128)(2,1)} %get-tuple-element.8.normed_ref, bf16[3,64,192]{2,1,0:T(8,128)(2,1)} %copy-done.4, bf16[3,64,192]{2,1,0:T(8,128)(2,1)} %copy-done.3, bf16[38,8,192]{2,1,0:T(8,128)(2,1)} %copy-done.1, ...), custom_call_target="tpu_custom_call" | custom-call | tf_op jit(solution)/shard_map/first_finish/pallas_call | solution.py:439
  48.0 27.7 %all_to_all.10.got_ref = bf16[128,24,128]{2,1,0:T(8,128)(2,1)} all-to-all(bf16[128,24,128]{2,1,0:T(8,128)(2,1)} %first_finish.1), channel_id=1, replica_groups=mesh['row'=8,'block'=8,'core'=2] {'row','block','core'}, dimensions={0} | all-to-all | bytes 1572864 | tf_op jit(solution)/shard_map/all_to_all | solution.py:608
  75.7 13.9 %shuffled_attention.1 = bf16[128,40,128]{2,1,0:T(8,128)(2,1)} custom-call(bf16[128,24,128]{2,1,0:T(8,128)(2,1)} %all_to_all.10.got_ref, f32[2,3,192]{2,1,0:T(4,128)} %copy.9.gain_ref, bf16[2,192,576]{2,1,0:T(8,128)(2,1)} %qkv_ref.3, bf16[2,192,192]{2,1,0:T(8,128)(2,1)} %proj_ref.3, f32[2,6,225]{2,1,0:T(8,128)} %copy.10.table_ref), custom_call_target="tpu_custom_call" | custom-call | tf_op jit(solution)/shard_map/shuffled_attention/pallas_call | solution.py:314
  89.6 27.7 %all_to_all.11.back_ref = bf16[128,40,128]{2,1,0:T(8,128)(2,1)} all-to-all(bf16[128,40,128]{2,1,0:T(8,128)(2,1)} %shuffled_attention.1), channel_id=1, replica_groups=mesh['row'=8,'block'=8,'core'=2] {'row','block','core'}, dimensions={0} | all-to-all | bytes 2621440 | tf_op jit(solution)/shard_map/all_to_all | solution.py:610
  117.3 15.0 %second_finish.1 = bf16[32,64,192]{2,1,0:T(8,128)(2,1)} custom-call(bf16[128,40,128]{2,1,0:T(8,128)(2,1)} %all_to_all.11.back_ref, f32[2,3,192]{2,1,0:T(4,128)} %copy.9.gain_ref, f32[2,49,192]{2,1,0:T(8,128)} %copy.12.taps_ref, bf16[2,192,768]{2,1,0:T(8,128)(2,1)} %up_ref.3, bf16[2,768,192]{2,1,0:T(8,128)(2,1)} %copy.13.down_ref), custom_call_target="tpu_custom_call" | custom-call | tf_op jit(solution)/shard_map/second_finish/pallas_call | solution.py:553
  (4 shorter events, 0.1 us)
Async XLA Ops:
  2.6 27.6 %copy-start.5 = (f32[2,49,192]{2,0,1:T(2,128)S(1)}, f32[2,49,192]{2,0,1:T(2,128)}, u32[]{:S(2)}) copy-start(f32[2,49,192]{2,0,1:T(2,128)} %param.13) | copy-start | bytes 225796
  12.1 18.8 %copy-start = (bf16[2,768,192]{1,2,0:T(8,128)(2,1)S(1)}, bf16[2,768,192]{1,2,0:T(8,128)(2,1)}, u32[]{:S(2)}) copy-start(bf16[2,768,192]{1,2,0:T(8,128)(2,1)} %param.15) | copy-start | bytes 1769476
  13.1 8.6 %collective-permute-start.1 = (bf16[3,64,192]{2,1,0:T(8,128)(2,1)S(1)}, bf16[3,64,192]{2,1,0:T(8,128)(2,1)S(1)}, u32[]{:S(2)}, u32[]{:S(2)}) collective-permute-start(bf16[3,64,192]{2,1,0:T(8,128)(2,1)S(1)} %get-tuple-element.11), channel_id=1, source_target_pairs={{16,0},{32,16},{48,32},{64,48},{80,64},{96,80},{112,96},{17,1},{33... | collective-permute-start | bytes 221192 | tf_op jit(solution)/shard_map/ppermute | solution.py:582
  14.4 9.7 %collective-permute-start = (bf16[3,64,192]{2,1,0:T(8,128)(2,1)S(1)}, bf16[3,64,192]{2,1,0:T(8,128)(2,1)S(1)}, u32[]{:S(2)}, u32[]{:S(2)}) collective-permute-start(bf16[3,64,192]{2,1,0:T(8,128)(2,1)S(1)} %get-tuple-element.12), channel_id=1, source_target_pairs={{0,16},{16,32},{32,48},{48,64},{64,80},{80,96},{96,112},{1,17},{17... | collective-permute-start | bytes 221192 | tf_op jit(solution)/shard_map/ppermute | solution.py:582
  21.7 13.2 %copy-start.3 = (bf16[3,64,192]{2,1,0:T(8,128)(2,1)}, bf16[3,64,192]{2,1,0:T(8,128)(2,1)S(1)}, u32[]{:S(2)}) copy-start(bf16[3,64,192]{2,1,0:T(8,128)(2,1)S(1)} %collective-permute-done.1.bottom_ref) | copy-start | bytes 221188
  24.1 10.8 %copy-start.4 = (bf16[3,64,192]{2,1,0:T(8,128)(2,1)}, bf16[3,64,192]{2,1,0:T(8,128)(2,1)S(1)}, u32[]{:S(2)}) copy-start(bf16[3,64,192]{2,1,0:T(8,128)(2,1)S(1)} %collective-permute-done.top_ref) | copy-start | bytes 221188
  24.1 7.9 %collective-permute-start.2 = (bf16[38,8,192]{2,1,0:T(8,128)(2,1)S(1)}, bf16[38,8,192]{2,1,0:T(8,128)(2,1)S(1)}, u32[]{:S(2)}, u32[]{:S(2)}) collective-permute-start(bf16[38,8,192]{2,1,0:T(8,128)(2,1)S(1)} %pad_maximum_fusion), channel_id=1, source_target_pairs={{0,1},{1,2},{2,3},{3,4},{4,5},{5,6},{6,7},{7,8},{8,9},{9,10},{10,1... | collective-permute-start | bytes 350216 | tf_op jit(solution)/shard_map/ppermute | solution.py:582
  28.3 6.5 %collective-permute-start.3 = (bf16[38,8,192]{2,1,0:T(8,128)(2,1)S(1)}, bf16[38,8,192]{2,1,0:T(8,128)(2,1)S(1)}, u32[]{:S(2)}, u32[]{:S(2)}) collective-permute-start(bf16[38,8,192]{2,1,0:T(8,128)(2,1)S(1)} %pad_maximum_fusion.1), channel_id=1, source_target_pairs={{1,0},{2,1},{3,2},{4,3},{5,4},{6,5},{7,6},{8,7},{9,8},{10,9},{11,1... | collective-permute-start | bytes 350216 | tf_op jit(solution)/shard_map/ppermute | solution.py:582
  32.0 2.8 %copy-start.1 = (bf16[38,8,192]{2,1,0:T(8,128)(2,1)}, bf16[38,8,192]{2,1,0:T(8,128)(2,1)S(1)}, u32[]{:S(2)}) copy-start(bf16[38,8,192]{2,1,0:T(8,128)(2,1)S(1)} %collective-permute-done.2.left_ref) | copy-start | bytes 350212
  34.8 0.7 copy-start.2

commit v2 on v1

--- a/solution.py
+++ b/solution.py
@@ -39,8 +39,8 @@
     return jnp.dot(a, b, preferred_element_type=f32)
 
 
-def prepare_attention(table_ref, qkv_ref, bias_s, rows_s, qkv_s):
-    table = table_ref[0]
+def prepare_attention(layer, table_ref, qkv_ref, bias_s, rows_s, qkv_s):
+    table = table_ref[:, layer, :]
     high = table.astype(bf16)
     rest = table - high.astype(f32)
     middle = rest.astype(bf16)
@@ -71,7 +71,7 @@
                 pltpu.roll(right, (shift + AREA) % LANES, 1),
             )
             bias_s[group * AREA + row * WS : group * AREA + (row + 1) * WS, :] = piece
-    weights = qkv_ref[0].astype(f32)
+    weights = qkv_ref[layer].astype(f32)
     gap = jnp.zeros((D, PAD - D), f32)
     qkv_s[...] = jnp.concatenate(
         [
@@ -136,37 +136,79 @@
     return current + mxu(jnp.concatenate(outs, axis=0), proj)
 
 
-def plain_kernel(
-    x_ref, gain_ref, qkv_ref, proj_ref, table_ref, sum_ref, normed_ref, bias_s, rows_s, qkv_s
+def edge_kernel(
+    first_ref,
+    last_ref,
+    gain_ref,
+    qkv_ref,
+    proj_ref,
+    table_ref,
+    sum_left_ref,
+    sum_right_ref,
+    left_out_ref,
+    right_out_ref,
+    bias_ref,
+    pad_ref,
+    rows_s,
 ):
-    @pl.when(pl.program_id(0) == 0)
-    def _():
-        prepare_attention(table_ref, qkv_ref, bias_s, rows_s, qkv_s)
-
-    cols = x_ref.shape[1]
-    count = cols // WS
-    grid = x_ref[...].astype(f32)
+    prepare_attention(0, table_ref, qkv_ref, bias_ref, rows_s, pad_ref)
+    sides = [side[...].astype(f32).reshape(-1, D) for side in (first_ref, last_ref)]
+    after = attention(
+        jnp.concatenate(sides, axis=0),
+        gain_ref[0, 0:1, :],
+        pad_ref[...],
+        proj_ref[0],
+        bias_ref[...],
+        attention_masks(),
+        TOGETHER,
+    )
+    normed = layer_norm(after, gain_ref[1, 0:1, :])
+    half = after.shape[0] // 2
+    shape = sum_left_ref.shape
+    sum_left_ref[...] = after[:half].reshape(shape)
+    sum_right_ref[...] = after[half:].reshape(shape)
+    left_out_ref[...] = normed[:half].reshape(shape).astype(bf16)
+    right_out_ref[...] = normed[half:].reshape(shape).astype(bf16)
+
+
+def inner_kernel(
+    x_ref,
+    gain_ref,
+    pad_ref,
+    proj_ref,
+    bias_ref,
+    sum_left_ref,
+    sum_right_ref,
+    left_ref,
+    right_ref,
+    sum_ref,
+    normed_ref,
+):
+    rows = pl.ds(pl.program_id(0) * WS, WS)
+    inner = range(1, x_ref.shape[1] // WS - 1)
+    grid = x_ref[rows].astype(f32)
     current = jnp.concatenate(
-        [grid[:, j * WS : (j + 1) * WS, :].reshape(AREA, D) for j in range(count)], axis=0
+        [grid[:, j * WS : (j + 1) * WS, :].reshape(AREA, D) for j in inner], axis=0
     )
     after = attention(
         current,
         gain_ref[0, 0:1, :],
-        qkv_s[...],
+        pad_ref[...],
         proj_ref[0],
-        bias_s[...],
+        bias_ref[...],
         attention_masks(),
-        TOGETHER,
+        len(inner) // 2,
     )
-    normed_two = layer_norm(after, gain_ref[0, 1:2, :])
-
-    def spatial(value):
-        return jnp.concatenate(
-            [value[j * AREA : (j + 1) * AREA].reshape(WS, WS, D) for j in range(count)], axis=1
-        )
-
-    sum_ref[...] = spatial(after)
-    normed_ref[...] = spatial(normed_two).astype(bf16)
+    normed = layer_norm(after, gain_ref[1, 0:1, :])
+
+    def spatial(first, value, last):
+        pieces = [value[n * AREA : (n + 1) * AREA].reshape(WS, WS, D) for n in range(len(inner))]
+        return jnp.concatenate([first, *pieces, last], axis=1)
+
+    sum_ref[rows] = spatial(sum_left_ref[rows], after, sum_right_ref[rows])
+    normed_ref[rows] = spatial(
+        left_ref[rows].astype(f32), normed, right_ref[rows].astype(f32)
+    ).astype(bf16)
 
 
 def attention_scratch():
@@ -177,30 +219,60 @@
     ]
 
 
-def plain_attention(tokens, norm_gain, qkv_weight, proj_weight, bias_table, layer):
-    height, width = tokens.shape[:2]
-    whole = lambda *shape: pl.BlockSpec(
-        (1, *shape), lambda i: (layer,) + (0,) * len(shape)
-    )
-    block = pl.BlockSpec((WS, width, D), lambda i: (i, 0, 0))
+RESIDENT = pl.BlockSpec(memory_space=pltpu.VMEM)
+PARAMS = pltpu.CompilerParams(vmem_limit_bytes=24 << 20)
+
+
+def resident(*arrays):
+    return [pltpu.with_memory_space_constraint(a, pltpu.VMEM) for a in arrays]
+
+
+def work(flops):
+    return pl.CostEstimate(flops=int(flops), transcendentals=0, bytes_accessed=1 << 20)
+
+
+def edge_attention(tokens, gains, qkv_weight, proj_weight, table):
+    side = (tokens.shape[0], WS, D)
+    last = tokens.shape[1] // WS - 1
+    full = lambda a: pl.BlockSpec(a.shape, lambda i: (0,) * a.ndim)
     return pl.pallas_call(
-        plain_kernel,
-        grid=(height // WS,),
+        edge_kernel,
+        grid=(1,),
         in_specs=[
-            block,
-            whole(3, D),
-            whole(D, 3 * D),
-            whole(D, D),
-            whole(HEADS, (2 * WS - 1) ** 2),
+            pl.BlockSpec(side, lambda i: (0, 0, 0)),
+            pl.BlockSpec(side, lambda i: (0, last, 0)),
+            full(gains),
+            full(qkv_weight),
+            full(proj_weight),
+            full(table),
         ],
-        out_specs=[block, block],
+        out_specs=[RESIDENT] * 6,
         out_shape=[
-            jax.ShapeDtypeStruct(tokens.shape, f32),
-            jax.ShapeDtypeStruct(tokens.shape, bf16),
+            pltpu.VMEM(side, f32),
+            pltpu.VMEM(side, f32),
+            pltpu.VMEM(side, bf16),
+            pltpu.VMEM(side, bf16),
+            pltpu.VMEM((HEADS // 2 * AREA, LANES), f32),
+            pltpu.VMEM((D, 3 * PAD), bf16),
         ],
-        scratch_shapes=attention_scratch(),
-        name="plain_attention",
-    )(tokens, norm_gain, qkv_weight, proj_weight, bias_table)
+        scratch_shapes=[pltpu.VMEM((WS, WS, LANES), f32)],
+        compiler_params=PARAMS,
+        cost_estimate=work(5e8),
+        name="edge_attention",
+    )(tokens, tokens, gains, qkv_weight, proj_weight, table)
+
+
+def inner_attention(tokens, gains, padded, proj_weight, bias, edges):
+    return pl.pallas_call(
+        inner_kernel,
+        grid=(tokens.shape[0] // WS,),
+        in_specs=[RESIDENT] * 9,
+        out_specs=[RESIDENT] * 2,
+        out_shape=[pltpu.VMEM(tokens.shape, f32), pltpu.VMEM(tokens.shape, bf16)],
+        compiler_params=PARAMS,
+        cost_estimate=work(8e9),
+        name="inner_attention",
+    )(*resident(tokens, gains, padded, proj_weight, bias, *edges))
 
 
 def low_half(value):
@@ -216,7 +288,7 @@
 def shuffled_kernel(
     got_ref, gain_ref, qkv_ref, proj_ref, table_ref, out_ref, bias_s, rows_s, qkv_s, window_s, piece_s
 ):
-    prepare_attention(table_ref, qkv_ref, bias_s, rows_s, qkv_s)
+    prepare_attention(1, table_ref, qkv_ref, bias_s, rows_s, qkv_s)
     blocks = WS * 2
 
     def gather(a, carry):
@@ -250,7 +322,7 @@
             axis=1,
         )[:, 0:D]
         after = attention(
-            current, gain_ref[0, 0:1, :], qkv_s[...], proj_ref[0], bias_s[...], masks, TOGETHER
+            current, gain_ref[0, 1:2, :], qkv_s[...], proj_ref[1], bias_s[...], masks, TOGETHER
         )
         for n, start in enumerate(starts):
             window_s[0, pl.ds(start, AREA), :] = after[n * AREA : (n + 1) * AREA, 0:LANES]
@@ -306,35 +378,30 @@
     lax.fori_loop(0, WS, scatter, 0)
 
 
-def shuffled_attention(got, norm_gain, qkv_weight, proj_weight, bias_table, layer):
-    whole = lambda *shape: pl.BlockSpec(
-        (1, *shape), lambda i: (layer,) + (0,) * len(shape)
-    )
+def shuffled_attention(got, gains, qkv_weight, proj_weight, table):
     shape = (got.shape[0], RETURN_ROWS, LANES)
     return pl.pallas_call(
         shuffled_kernel,
-        grid=(1,),
-        in_specs=[
-            pl.BlockSpec(got.shape, lambda i: (0, 0, 0)),
-            whole(3, D),
-            whole(D, 3 * D),
-            whole(D, D),
-            whole(HEADS, (2 * WS - 1) ** 2),
-        ],
-        out_specs=pl.BlockSpec(shape, lambda i: (0, 0, 0)),
-        out_shape=jax.ShapeDtypeStruct(shape, bf16),
+        in_specs=[RESIDENT] * 5,
+        out_specs=RESIDENT,
+        out_shape=pltpu.VMEM(shape, bf16),
         scratch_shapes=attention_scratch()
         + [
             pltpu.VMEM((2, 2 * SEGMENT * WINDOW_ROWS, LANES), f32),
             pltpu.VMEM((RETURN_ROWS, LANES), f32),
         ],
+        compiler_params=PARAMS,
+        cost_estimate=work(1e10),
         name="shuffled_attention",
-    )(got, norm_gain, qkv_weight, proj_weight, bias_table)
-
-
-def broadcast_taps(taps_ref, taps_s):
+    )(*resident(got, gains, qkv_weight, proj_weight, table))
+
+
+def prepare_finish(layer, taps_ref, down_ref, taps_s, down_s):
     for t in range(KS * KS):
-        taps_s[t] = jnp.broadcast_to(taps_ref[0, t : t + 1, :], (16, D)).astype(bf16)
+        taps_s[t] = jnp.broadcast_to(
+            taps_ref[t, layer : layer + 1, :], (16, D)
+        ).astype(bf16)
+    down_s[...] = down_ref[layer].T
 
 
 def convolve_row(padded_s, taps_s, row, width):
@@ -362,8 +429,77 @@
     return (after + mxu(hidden, down)).astype(bf16)
 
 
-def first_kernel(
+def ring(middle, right, left):
+    return jnp.concatenate(
+        [middle.astype(f32), right.astype(f32), left.astype(f32)], axis=0
+    ).astype(bf16)
+
+
+def middle_kernel(
     sum_ref,
+    normed_ref,
+    left_ref,
+    right_ref,
+    gain_ref,
+    taps_ref,
+    up_ref,
+    down_ref,
+    out_ref,
+    padded_s,
+    after_s,
+    taps_s,
+    down_s,
+):
+    step = pl.program_id(0)
+    rows = WS
+    width = sum_ref.shape[1]
+    first = WS - HALO
+
+    @pl.when(step == 0)
+    def _():
+        def body(r, carry):
+            padded_s[r] = ring(normed_ref[first + r], right_ref[first + r], left_ref[first + r])
+            return carry
+
+        lax.fori_loop(0, padded_s.shape[0], body, 0)
+        prepare_finish(0, taps_ref, down_ref, taps_s, down_s)
+
+    def row(j, carry):
+        total = sum_ref[WS + step * rows + j] + convolve_row(
+            padded_s, taps_s, step * rows + j, width
+        )
+        after_s[pl.ds(pl.multiple_of(j * width, width), width), :] = total
+        return carry
+
+    lax.fori_loop(0, rows, row, 0)
+    outcome = feed_forward(after_s[...], gain_ref[2, 0:1, :], up_ref[0], down_s[...])
+    out_ref[pl.ds(step * rows, rows)] = outcome.reshape(rows, width, D)
+
+
+def middle_finish(after, normed, left, right, gains, taps, up_weight, down_weight):
+    height, width = normed.shape[:2]
+    inner = height - 2 * WS
+    return pl.pallas_call(
+        middle_kernel,
+        grid=(inner // WS,),
+        in_specs=[RESIDENT] * 8,
+        out_specs=RESIDENT,
+        out_shape=pltpu.VMEM((inner, width, D), bf16),
+        scratch_shapes=[
+            pltpu.VMEM((inner + 2 * HALO, RING, D), bf16),
+            pltpu.VMEM((WS * width, D), f32),
+            pltpu.VMEM((KS * KS, 16, D), bf16),
+            pltpu.VMEM((HID, D), bf16),
+        ],
+        compiler_params=PARAMS,
+        cost_estimate=work(8e9),
+        name="middle_finish",
+    )(*resident(after, normed, left, right, gains, taps, up_weight, down_weight))
+
+
+def outer_kernel(
+    sum_ref,
+    middle_ref,
     normed_ref,
     top_ref,
     bottom_ref,
@@ -377,45 +513,46 @@
     padded_s,
     after_s,
     taps_s,
+    down_s,
     piece_s,
 ):
     step = pl.program_id(0)
     height, width, _ = normed_ref.shape
-    repeats, rows = sum_ref.shape[:2]
+    rows = WS // 2
+    repeats = height // WS
 
     @pl.when(step == 0)
     def _():
-        def place(r, middle):
-            padded_s[r] = jnp.concatenate(
-                [middle.astype(f32), right_ref[r].astype(f32), left_ref[r].astype(f32)], axis=0
-            ).astype(bf16)
-
         for r in range(HALO):
-            place(r, top_ref[r])
-            place(height + HALO + r, bottom_ref[r])
+            padded_s[r] = top_ref[r]
+            padded_s[height + HALO + r] = bottom_ref[r]
 
         def body(r, carry):
-            place(r + HALO, normed_ref[r])
+            padded_s[r + HALO] = ring(normed_ref[r], right_ref[r], left_ref[r])
             return carry
 
-        lax.fori_loop(0, height, body, 0)
-        broadcast_taps(taps_ref, taps_s)
+        lax.fori_loop(0, WS + HALO, body, 0)
+        lax.fori_loop(height - WS - HALO, height, body, 0)
+        prepare_finish(0, taps_ref, down_ref, taps_s, down_s)
 
     def row(j, carry):
-        m, q = j // rows, j % rows
-        total = sum_ref[m, q] + convolve_row(
-            padded_s, taps_s, m * WS + step * rows + q, width
-        )
+        part, q = j // rows, j % rows
+        r = part * (height - WS) + step * rows + q
+        total = sum_ref[r] + convolve_row(padded_s, taps_s, r, width)
         after_s[pl.ds(pl.multiple_of(j * width, width), width), :] = total
         return carry
 
-    lax.fori_loop(0, repeats * rows, row, 0)
-    outcome = feed_forward(after_s[...], gain_ref[0, 2:3, :], up_ref[0], down_ref[0]).astype(f32)
+    lax.fori_loop(0, 2 * rows, row, 0)
+    outcome = feed_forward(after_s[...], gain_ref[2, 0:1, :], up_ref[0], down_s[...]).astype(f32)
     for m in range(repeats):
         for q in range(rows):
+            if m in (0, repeats - 1):
+                start = ((m > 0) * rows + q) * width
+                line = outcome[start : start + width]
+            else:
+                line = middle_ref[(m - 1) * WS + step * rows + q].astype(f32)
             for n in range(width // SEGMENT):
-                start = (m * rows + q) * width + n * SEGMENT
-                value = outcome[start : start + SEGMENT]
+                value = line[n * SEGMENT : (n + 1) * SEGMENT]
                 place = pl.ds((q * SEGMENT + m * 4 + n) * PIECE_ROWS, SEGMENT)
                 piece_s[0, place, :] = value[:, 0:LANES]
                 piece_s[1, place, 0 : D - LANES] = value[:, LANES:D]
@@ -423,48 +560,46 @@
         for c in range(SEGMENT):
             place = pl.ds(q * SEGMENT * PIECE_ROWS + c, SEGMENT, stride=PIECE_ROWS)
             upper = piece_s[1, place, :]
-            send_ref[q * SEGMENT + c] = jnp.concatenate(
+            send_ref[(step * rows + q) * SEGMENT + c] = jnp.concatenate(
                 [piece_s[0, place, :], join_halves(upper[0:8], upper[8:16])], axis=0
             ).astype(bf16)
 
 
-def first_finish(after, normed, halo, norm_gain, conv_weight, up_weight, down_weight, layer, group):
+def outer_finish(
+    after, middle, normed, top, bottom, left, right, gains, taps, up_weight, down_weight, group
+):
     height, width = normed.shape[:2]
-    repeats = height // WS
-    rows = WS // repeats
-    whole = lambda *shape: pl.BlockSpec(
-        (1, *shape), lambda i: (layer,) + (0,) * len(shape)
-    )
-    full = lambda a: pl.BlockSpec(a.shape, lambda i: (0,) * a.ndim)
+    rows = WS // 2
     return pl.pallas_call(
-        first_kernel,
+        outer_kernel,
         grid=(WS // rows,),
-        in_specs=[
-            pl.BlockSpec((repeats, rows, width, D), lambda i: (0, i, 0, 0)),
-            full(normed),
-            *[full(h) for h in halo],
-            whole(3, D),
-            whole(KS * KS, D),
-            whole(D, HID),
-            whole(HID, D),
-        ],
-        out_specs=pl.BlockSpec((rows * SEGMENT, PIECE_ROWS, LANES), lambda i: (i, 0, 0)),
-        out_shape=jax.ShapeDtypeStruct((group, PIECE_ROWS, LANES), bf16),
+        in_specs=[RESIDENT] * 11,
+        out_specs=RESIDENT,
+        out_shape=pltpu.VMEM((group, PIECE_ROWS, LANES), bf16),
         scratch_shapes=[
             pltpu.VMEM((height + 2 * HALO, RING, D), bf16),
-            pltpu.VMEM((repeats * rows * width, D), f32),
+            pltpu.VMEM((2 * rows * width, D), f32),
             pltpu.VMEM((KS * KS, 16, D), bf16),
+            pltpu.VMEM((HID, D), bf16),
             pltpu.VMEM((2, rows * SEGMENT * PIECE_ROWS, LANES), f32),
         ],
-        name="first_finish",
+        compiler_params=PARAMS,
+        cost_estimate=work(8e9),
+        name="outer_finish",
     )(
-        after.reshape(repeats, WS, width, D),
-        normed,
-        *halo,
-        norm_gain,
-        conv_weight,
-        up_weight,
-        down_weight,
+        *resident(
+            after,
+            middle,
+            normed,
+            top,
+            bottom,
+            left,
+            right,
+            gains,
+            taps,
+            up_weight,
+            down_weight,
+        )
     )
 
 
@@ -479,6 +614,7 @@
     sum_s,
     after_s,
     taps_s,
+    down_s,
     piece_s,
 ):
     step = pl.program_id(0)
@@ -488,7 +624,7 @@
 
     @pl.when(step == 0)
     def _():
-        broadcast_taps(taps_ref, taps_s)
+        prepare_finish(1, taps_ref, down_ref, taps_s, down_s)
 
         def build(r, n, target, keep):
             pieces = []
@@ -509,7 +645,7 @@
             value = jnp.concatenate(pieces, axis=0)
             if keep:
                 sum_s[target - HALO] = value[0:width]
-            padded_s[target] = layer_norm(value, gain_ref[0, 1:2, :]).astype(bf16)
+            padded_s[target] = layer_norm(value, gain_ref[1, 1:2, :]).astype(bf16)
 
         def body(r, carry):
             def load(c, carry):
@@ -541,25 +677,16 @@
         return carry
 
     lax.fori_loop(0, rows, row, 0)
-    outcome = feed_forward(after_s[...], gain_ref[0, 2:3, :], up_ref[0], down_ref[0])
+    outcome = feed_forward(after_s[...], gain_ref[2, 1:2, :], up_ref[1], down_s[...])
     out_ref[...] = outcome.reshape(rows, width, D)
 
 
-def second_finish(back, shape, norm_gain, conv_weight, up_weight, down_weight, layer):
+def second_finish(back, shape, gains, taps, up_weight, down_weight):
     height, width = shape[:2]
-    whole = lambda *shape: pl.BlockSpec(
-        (1, *shape), lambda i: (layer,) + (0,) * len(shape)
-    )
     return pl.pallas_call(
         second_kernel,
         grid=(height // WS,),
-        in_specs=[
-            pl.BlockSpec(back.shape, lambda i: (0, 0, 0)),
-            whole(3, D),
-            whole(KS * KS, D),
-            whole(D, HID),
-            whole(HID, D),
-        ],
+        in_specs=[RESIDENT] * 5,
         out_specs=pl.BlockSpec((WS, width, D), lambda i: (i, 0, 0)),
         out_shape=jax.ShapeDtypeStruct(shape, bf16),
         scratch_shapes=[
@@ -567,48 +694,57 @@
             pltpu.VMEM((height, width, D), f32),
             pltpu.VMEM((WS * width, D), f32),
             pltpu.VMEM((KS * KS, 16, D), bf16),
+            pltpu.VMEM((HID, D), bf16),
             pltpu.VMEM((SEGMENT * RETURN_ROWS, LANES), f32),
         ],
+        compiler_params=PARAMS,
+        cost_estimate=work(1e10),
         name="second_finish",
-    )(back, norm_gain, conv_weight, up_weight, down_weight)
-
-
-def halo_of(normed):
-    height, width = normed.shape[:2]
-
-    def shift(value, axes, forward):
-        count = lax.axis_size(axes)
-        pairs = [(i, i + 1) if forward else (i + 1, i) for i in range(count - 1)]
-        return lax.ppermute(value, axes, pairs)
-
-    top = shift(normed[height - HALO :], "row", True)
-    bottom = shift(normed[:HALO], "row", False)
-    columns = lambda part: jnp.concatenate([part(top), part(normed), part(bottom)], axis=0)
-    left = shift(columns(lambda a: a[:, width - WS :]), ("block", "core"), True)
-    right = shift(columns(lambda a: a[:, :WS]), ("block", "core"), False)
-    return top, bottom, left, right
+    )(*resident(back, gains, taps, up_weight, down_weight))
+
+
+def shift(value, axes, forward):
+    count = lax.axis_size(axes)
+    pairs = [(i, i + 1) if forward else (i + 1, i) for i in range(count - 1)]
+    return lax.ppermute(value, axes, pairs)
 
 
 def on_device(
     tokens, norm_gain, qkv_weight, proj_weight, bias_table, conv_weight, up_weight, down_weight
 ):
     members = ("row", "block", "core")
-    after, normed = plain_attention(tokens, norm_gain, qkv_weight, proj_weight, bias_table, 0)
-    outgoing = first_finish(
+    columns = ("block", "core")
+    gains = norm_gain.transpose(1, 0, 2)
+    table = bias_table.transpose(1, 0, 2)
+    taps = conv_weight.transpose(1, 0, 2)
+    down_weight = down_weight.transpose(0, 2, 1)
+    *edges, bias, padded = edge_attention(tokens, gains, qkv_weight, proj_weight, table)
+    left = shift(edges[3], columns, True)
+    right = shift(edges[2], columns, False)
+    after, normed = inner_attention(tokens, gains, padded, proj_weight, bias, edges)
+    around = lambda rows: jnp.concatenate([normed[rows], right[rows], left[rows]], axis=1)
+    height = tokens.shape[0]
+    top = shift(around(slice(height - HALO, height)), "row", True)
+    bottom = shift(around(slice(0, HALO)), "row", False)
+    middle = middle_finish(after, normed, left, right, gains, taps, up_weight, down_weight)
+    outgoing = outer_finish(
         after,
+        middle,
         normed,
-        halo_of(normed),
-        norm_gain,
-        conv_weight,
+        top,
+        bottom,
+        left,
+        right,
+        gains,
+        taps,
         up_weight,
         down_weight,
-        0,
         lax.axis_size(members),
     )
     got = lax.all_to_all(outgoing, members, 0, 0, tiled=True)
-    branch = shuffled_attention(got, norm_gain, qkv_weight, proj_weight, bias_table, 1)
+    branch = shuffled_attention(got, gains, qkv_weight, proj_weight, table)
     back = lax.all_to_all(branch, members, 0, 0, tiled=True)
-    return second_finish(back, tokens.shape, norm_gain, conv_weight, up_weight, down_weight, 1)
+    return second_finish(back, tokens.shape, gains, taps, up_weight, down_weight)
 
 
 def solution(mesh):

time: 133 us -> 117 us (0.88)
  Pallas kernels: 50.9 us -> 44 us
  waiting for transfers between devices: 5.18 us -> 1.97 us
  local copies, waits for them, and re-layouts: 7.08 us -> 4.64 us
  blocking collectives: 55.4 us -> 53.1 us
    pallas_call x4 -> x6, Pallas kernels: 50.9 us -> 44 us  [the longest x1 13.6 us: second_finish(): pl.pallas_call(second_kernel, grid=(height // WS,), in_specs=[RESIDENT] *...]
    ppermute x4, waiting for transfers between devices: 5.18 us -> 1.97 us  [shift(): return lax.ppermute(value, axes, pairs)]
    slice x4 -> x3, local copies, waits for them, and re-layouts: 2.01 us -> 0.02 us  [the longest x1 0.02 us: on_device(): normed[rows]]
    unnamed x16 -> x24, local copies, waits for them, and re-layouts: 5.07 us -> 4.62 us
  transfers between devices with their start and end apart: 4 -> 4, of which waited for: 2 -> 1; matrix products, arithmetic and copies ran while one was open for 2% -> 0% of each run, Pallas kernels for 0% -> 10%
where the time goes in v2:
time: 117 us
  blocking collectives  53.1 us (45%)
  Pallas kernels  44 us (38%)
  starting transfers between devices  13 us (11%)
  local copies, waits for them, and re-layouts  4.64 us (4%)
  waiting for transfers between devices  1.97 us (2%)
    all_to_all x1, blocking collectives, on_device(): got = lax.all_to_all(outgoing, members, 0, 0, tiled=True)  26.7 us
    all_to_all x1, blocking collectives, on_device(): back = lax.all_to_all(branch, members, 0, 0, tiled=True)  26.4 us
    pallas_call x1, Pallas kernels, second_finish(): pl.pallas_call(second_kernel, grid=(height // WS,), in_specs=[RESIDENT] *...  13.6 us
    ppermute x4, starting transfers between devices, shift(): return lax.ppermute(value, axes, pairs)  13 us
    pallas_call x1, Pallas kernels, shuffled_attention(): pl.pallas_call(shuffled_kernel, in_specs=[RESIDENT] * 5, out_specs=RESIDE...  11.7 us
    pallas_call x1, Pallas kernels, inner_attention(): pl.pallas_call(inner_kernel, grid=(tokens.shape[0] // WS,), in_specs=[RES...  6.7 us
    pallas_call x1, Pallas kernels, outer_finish(): pl.pallas_call(outer_kernel, grid=(WS // rows,), in_specs=[RESIDENT] * 11...  5.21 us
    pallas_call x1, Pallas kernels, middle_finish(): pl.pallas_call(middle_kernel, grid=(inner // WS,), in_specs=[RESIDENT] *...  4.86 us
  transfers between devices with their start and end apart: 4, of which 1 were waited for; matrix products, arithmetic and copies ran while one was open for 0% of the time, Pallas kernels for 10%

profile of v2, /device:TPU:1, one launch (start us, length us, event | category | flops | bytes accessed | tf_op | source)
XLA Modules:
  0.0 116.9 jit_solution(5930519135321765274)
XLA Ops:
  0.0 1.2 %copy-done = bf16[32,64,192]{2,1,0:T(8,128)(2,1)S(1)} copy-done((bf16[32,64,192]{2,1,0:T(8,128)(2,1)S(1)}, bf16[32,64,192]{2,1,0:T(8,128)(2,1)}, u32[]{:S(2)}) %copy-start) | copy-done | bytes 786456
  1.2 1.0 copy-done.1
  2.3 0.9 copy-done.3
  3.2 0.7 copy-done.5
  3.9 0.7 copy-done.7
  4.6 2.0 %edge_attention.1 = (f32[32,8,192]{2,1,0:T(8,128)S(1)}, f32[32,8,192]{2,1,0:T(8,128)S(1)}, bf16[32,8,192]{2,1,0:T(8,128)(2,1)S(1)}, bf16[32,8,192]{2,1,0:T(8,128...) custom-call(bf16[32,64,192]{2,1,0:T(8,128)(2,1)S(1)} %copy-done, bf16[32,64,192]{2,1,0:T(8,128)(2,1)S(1)} %copy-done, ...), custom_call_target="tpu_custom_call" | custom-call | flops 500000000 | bytes 1048576 | tf_op jit(solution)/shard_map/edge_attention/pallas_call | solution.py:238
  6.5 3.3 %collective-permute-start.1 = (bf16[32,8,192]{2,1,0:T(8,128)(2,1)S(1)}, bf16[32,8,192]{2,1,0:T(8,128)(2,1)S(1)}, u32[]{:S(2)}, u32[]{:S(2)}) collective-permute-start(bf16[32,8,192]{2,1,0:T(8,128)(2,1)S(1)} %get-tuple-element.17.left_ref), channel_id=1, source_target_pairs={{1,0},{2,1},{3,2},{4,3},{5,4},{6,5},{7,6},{8,7},{9,8},{10,9},{11,1... | collective-permute-start | bytes 294920 | tf_op jit(solution)/shard_map/ppermute | solution.py:709
  9.8 3.6 %collective-permute-start = (bf16[32,8,192]{2,1,0:T(8,128)(2,1)S(1)}, bf16[32,8,192]{2,1,0:T(8,128)(2,1)S(1)}, u32[]{:S(2)}, u32[]{:S(2)}) collective-permute-start(bf16[32,8,192]{2,1,0:T(8,128)(2,1)S(1)} %get-tuple-element.18.right_ref), channel_id=1, source_target_pairs={{0,1},{1,2},{2,3},{3,4},{4,5},{5,6},{6,7},{7,8},{8,9},{9,10},{10,1... | collective-permute-start | bytes 294920 | tf_op jit(solution)/shard_map/ppermute | solution.py:709
  13.4 0.0 copy-done.4
  13.4 0.0 copy-start.8
  13.4 0.0 copy-start.9
  13.4 0.0 copy-start.10
  13.5 0.0 copy-start.11
  13.5 6.7 %inner_attention.1 = (f32[32,64,192]{2,1,0:T(8,128)S(1)}, bf16[32,64,192]{2,1,0:T(8,128)(2,1)S(1)}) custom-call(bf16[32,64,192]{2,1,0:T(8,128)(2,1)S(1)} %copy-done, f32[3,2,192]{2,1,0:T(2,128)S(1)} %bitcast.7, bf16[192,768]{1,0:T(8,128)(2,1)S(1)} %get-tuple-element.13.pad_ref, bf16[2,192,192]{2,1,0:T(8,128)(2,1)S(1)} %copy-done.4, ...), custom_call_target="tpu_custom_call" | custom-call | flops 8000000000 | bytes 1048576 | tf_op jit(solution)/shard_map/inner_attention/pallas_call | solution.py:266
  20.2 0.0 collective-permute-done.1.right_ref
  20.2 0.0 collective-permute-done.left_ref
  20.3 4.8 %collective-permute-start.2 = (bf16[3,80,192]{2,1,0:T(8,128)(2,1)S(1)}, bf16[3,80,192]{2,1,0:T(8,128)(2,1)S(1)}, u32[]{:S(2)}, u32[]{:S(2)}) collective-permute-start(bf16[3,80,192]{2,1,0:T(8,128)(2,1)S(1)} %pad_maximum_fusion), channel_id=1, source_target_pairs={{0,16},{16,32},{32,48},{48,64},{64,80},{80,96},{96,112},{1,17},{17... | collective-permute-start | bytes 276488 | tf_op jit(solution)/shard_map/ppermute | solution.py:709
  25.1 1.3 %collective-permute-start.3 = (bf16[3,80,192]{2,1,0:T(8,128)(2,1)S(1)}, bf16[3,80,192]{2,1,0:T(8,128)(2,1)S(1)}, u32[]{:S(2)}, u32[]{:S(2)}) collective-permute-start(bf16[3,80,192]{2,1,0:T(8,128)(2,1)S(1)} %pad_maximum_fusion.1), channel_id=1, source_target_pairs={{16,0},{32,16},{48,32},{64,48},{80,64},{96,80},{112,96},{17,1},{33... | collective-permute-start | bytes 276488 | tf_op jit(solution)/shard_map/ppermute | solution.py:709
  26.4 0.0 copy-done.8
  26.4 0.0 copy-done.9
  26.5 0.0 copy-done.10
  26.5 4.9 %middle_finish.1.middle_ref = bf16[16,64,192]{2,1,0:T(8,128)(2,1)S(1)} custom-call(f32[32,64,192]{2,1,0:T(8,128)S(1)} %get-tuple-element.19.sum_ref, bf16[32,64,192]{2,1,0:T(8,128)(2,1)S(1)} %get-tuple-element.20.normed_ref, bf16[32,8,192]{2,1,0:T(8,128)(2,1)S(1)} %collective-permute-done.left_ref, bf16[32,8,192]{2,1,0:T(8,128)(2,1)S(1)} %collective-permute-done.1.right_ref, ...), custom_call_target="tpu_custom_call" | custom-call | flops 8000000000 | bytes 1048576 | tf_op jit(solution)/shard_map/middle_finish/pallas_call | solution.py:482
  31.3 0.0 collective-permute-done.2.top_ref
  31.4 2.0 %collective-permute-done.3.bottom_ref = bf16[3,80,192]{2,1,0:T(8,128)(2,1)S(1)} collective-permute-done((bf16[3,80,192]{2,1,0:T(8,128)(2,1)S(1)}, bf16[3,80,192]{2,1,0:T(8,128)(2,1)S(1)}, u32[]{:S(2)}, u32[]{:S(2)}) %collective-permute-start.3) | collective-permute-done | bytes 92192 | tf_op jit(solution)/shard_map/ppermute | solution.py:709
  33.3 5.2 %outer_finish.1 = bf16[128,24,128]{2,1,0:T(8,128)(2,1)S(1)} custom-call(f32[32,64,192]{2,1,0:T(8,128)S(1)} %get-tuple-element.19.sum_ref, bf16[16,64,192]{2,1,0:T(8,128)(2,1)S(1)} %middle_finish.1.middle_ref, bf16[32,64,192]{2,1,0:T(8,128)(2,1)S(1)} %get-tuple-element.20.normed_ref, bf16[3,80,192]{2,1,0:T(8,128)(2,1)S(1)} %collective-permute-done.2.top_ref, ...), custom_call_target="tpu_custom_call" | custom-call | flops 8000000000 | bytes 1048576 | tf_op jit(solution)/shard_map/outer_finish/pallas_call | solution.py:573
  38.5 0.0 copy-start.2
  38.5 0.0 copy-start.6
  38.6 26.7 %all_to_all.10.got_ref = bf16[128,24,128]{2,1,0:T(8,128)(2,1)S(1)} all-to-all(bf16[128,24,128]{2,1,0:T(8,128)(2,1)S(1)} %outer_finish.1), channel_id=1, replica_groups=mesh['row'=8,'block'=8,'core'=2] {'row','block','core'}, dimensions={0} | all-to-all | bytes 1572864 | tf_op jit(solution)/shard_map/all_to_all | solution.py:744
  65.2 0.0 copy-done.6
  65.2 11.7 %shuffled_attention.1 = bf16[128,40,128]{2,1,0:T(8,128)(2,1)S(1)} custom-call(bf16[128,24,128]{2,1,0:T(8,128)(2,1)S(1)} %all_to_all.10.got_ref, f32[3,2,192]{2,1,0:T(2,128)S(1)} %bitcast.10, bf16[2,192,576]{2,1,0:T(8,128)(2,1)S(1)} %copy-done.2, bf16[2,192,192]{2,1,0:T(8,128)(2,1)S(1)} %copy-done.4, f32[6,2,225]{2,1,0:T(2,128)S(1)} %bitcast.5), custom_call_target="tpu_custom_call" | custom-call | flops 10000000000 | bytes 1048576 | tf_op jit(solution)/shard_map/shuffled_attention/pallas_call | solution.py:383
  76.9 26.4 %all_to_all.11.back_ref = bf16[128,40,128]{2,1,0:T(8,128)(2,1)S(1)} all-to-all(bf16[128,40,128]{2,1,0:T(8,128)(2,1)S(1)} %shuffled_attention.1), channel_id=1, replica_groups=mesh['row'=8,'block'=8,'core'=2] {'row','block','core'}, dimensions={0} | all-to-all | bytes 2621440 | tf_op jit(solution)/shard_map/all_to_all | solution.py:746
  103.3 13.6 %second_finish.1 = bf16[32,64,192]{2,1,0:T(8,128)(2,1)} custom-call(bf16[128,40,128]{2,1,0:T(8,128)(2,1)S(1)} %all_to_all.11.back_ref, f32[3,2,192]{2,1,0:T(2,128)S(1)} %bitcast.11, f32[49,2,192]{2,1,0:T(2,128)S(1)} %bitcast.17, bf16[2,192,768]{2,1,0:T(8,128)(2,1)S(1)} %copy-done.9, bf16[2,192,768]{2,1,0:T(8,128)(2,1)S(1)} %bitcast.14), custom_call_target="tpu_custom_call" | custom-call | flops 10000000000 | bytes 1048576 | tf_op jit(solution)/shard_map/second_finish/pallas_call | solution.py:686
  (13 shorter events, 0.1 us)
Async XLA Ops:
  0.0 1.2 %copy-start = (bf16[32,64,192]{2,1,0:T(8,128)(2,1)S(1)}, bf16[32,64,192]{2,1,0:T(8,128)(2,1)}, u32[]{:S(2)}) copy-start(bf16[32,64,192]{2,1,0:T(8,128)(2,1)} %x_ref.1) | copy-start | bytes 2359300
  1.2 1.0 copy-start.1
  2.3 0.9 copy-start.3
  3.2 0.7 copy-start.5
  3.9 0.7 copy-start.7
  4.6 8.8 %copy-start.4 = (bf16[2,192,192]{2,1,0:T(8,128)(2,1)S(1)}, bf16[2,192,192]{2,1,0:T(8,128)(2,1)}, u32[]{:S(2)}) copy-start(bf16[2,192,192]{2,1,0:T(8,128)(2,1)} %proj_ref.5) | copy-start | bytes 442372
  6.5 13.6 %collective-permute-start.1 = (bf16[32,8,192]{2,1,0:T(8,128)(2,1)S(1)}, bf16[32,8,192]{2,1,0:T(8,128)(2,1)S(1)}, u32[]{:S(2)}, u32[]{:S(2)}) collective-permute-start(bf16[32,8,192]{2,1,0:T(8,128)(2,1)S(1)} %get-tuple-element.17.left_ref), channel_id=1, source_target_pairs={{1,0},{2,1},{3,2},{4,3},{5,4},{6,5},{7,6},{8,7},{9,8},{10,9},{11,1... | collective-permute-start | bytes 294920 | tf_op jit(solution)/shard_map/ppermute | solution.py:709
  9.8 10.4 %collective-permute-start = (bf16[32,8,192]{2,1,0:T(8,128)(2,1)S(1)}, bf16[32,8,192]{2,1,0:T(8,128)(2,1)S(1)}, u32[]{:S(2)}, u32[]{:S(2)}) collective-permute-start(bf16[32,8,192]{2,1,0:T(8,128)(2,1)S(1)} %get-tuple-element.18.right_ref), channel_id=1, source_target_pairs={{0,1},{1,2},{2,3},{3,4},{4,5},{5,6},{6,7},{7,8},{8,9},{9,10},{10,1... | collective-permute-start | bytes 294920 | tf_op jit(solution)/shard_map/ppermute | solution.py:709
  13.4 13.0 %copy-start.8 = (f32[2,3,192]{2,0,1:T(2,128)S(1)}, f32[2,3,192]{2,0,1:T(2,128)}, u32[]{:S(2)}) copy-start(f32[2,3,192]{2,0,1:T(2,128)} %param.9) | copy-start | bytes 13828
  13.4 13.0 %copy-start.9 = (bf16[2,192,768]{2,1,0:T(8,128)(2,1)S(1)}, bf16[2,192,768]{2,1,0:T(8,128)(2,1)}, u32[]{:S(2)}) copy-start(bf16[2,192,768]{2,1,0:T(8,128)(2,1)} %up_ref.5) | copy-start | bytes 1769476
  13.4 13.0 %copy-start.10 = (bf16[2,768,192]{1,2,0:T(8,128)(2,1)S(1)}, bf16[2,768,192]{1,2,0:T(8,128)(2,1)}, u32[]{:S(2)}) copy-start(bf16[2,768,192]{1,2,0:T(8,128)(2,1)} %param.15) | copy-start | bytes 1769476
  13.5 13.0 %copy-start.11 = (f32[2,49,192]{2,0,1:T(2,128)S(1)}, f32[2,49,192]{2,0,1:T(2,128)}, u32[]{:S(2)}) copy-start(f32[2,49,192]{2,0,1:T(2,128)} %param.13) | copy-start | bytes 225796
  20.3 11.1 %collective-permute-start.2 = (bf16[3,80,192]{2,1,0:T(8,128)(2,1)S(1)}, bf16[3,80,192]{2,1,0:T(8,128)(2,1)S(1)}, u32[]{:S(2)}, u32[]{:S(2)}) collective-permute-start(bf16[3,80,192]{2,1,0:T(8,128)(2,1)S(1)} %pad_maximum_fusion), channel_id=1, source_target_pairs={{0,16},{16,32},{32,48},{48,64},{64,80},{80,96},{96,112},{1,17},{17... | collective-permute-start | bytes 276488 | tf_op jit(solution)/shard_map/ppermute | solution.py:709
  25.1 8.2 %collective-permute-start.3 = (bf16[3,80,192]{2,1,0:T(8,128)(2,1)S(1)}, bf16[3,80,192]{2,1,0:T(8,128)(2,1)S(1)}, u32[]{:S(2)}, u32[]{:S(2)}) collective-permute-start(bf16[3,80,192]{2,1,0:T(8,128)(2,1)S(1)} %pad_maximum_fusion.1), channel_id=1, source_target_pairs={{16,0},{32,16},{48,32},{64,48},{80,64},{96,80},{112,96},{17,1},{33... | collective-permute-start | bytes 276488 | tf_op jit(solution)/shard_map/ppermute | solution.py:709
  38.5 26.7 %copy-start.2 = (bf16[2,192,576]{2,1,0:T(8,128)(2,1)S(1)}, bf16[2,192,576]{2,1,0:T(8,128)(2,1)}, u32[]{:S(2)}) copy-start(bf16[2,192,576]{2,1,0:T(8,128)(2,1)} %qkv_ref.3) | copy-start | bytes 1327108
  38.5 26.7 %copy-start.6 = (f32[2,6,225]{2,0,1:T(2,128)S(1)}, f32[2,6,225]{2,0,1:T(2,128)}, u32[]{:S(2)}) copy-start(f32[2,6,225]{2,0,1:T(2,128)} %param.12) | copy-start | bytes 32404

commit v3 on v2

--- a/solution.py
+++ b/solution.py
@@ -16,10 +16,12 @@
 PAD = 256
 LANES = 128
 HALO = KS // 2
-TOGETHER = 4
-WINDOW_ROWS = AREA + 8
+TOGETHER = 16
+WINDOW_ROWS = AREA + 4
 PIECE_ROWS = 24
+PIECE_STRIDE = PIECE_ROWS + 4
 RETURN_ROWS = 40
+RETURN_STRIDE = RETURN_ROWS + 4
 RING = 80
 SEGMENT = 16
 EPSILON = 1e-05
@@ -184,11 +186,17 @@
     sum_ref,
     normed_ref,
 ):
-    rows = pl.ds(pl.program_id(0) * WS, WS)
+    high = 4 * WS
+    rows = pl.ds(pl.program_id(0) * high, high)
     inner = range(1, x_ref.shape[1] // WS - 1)
     grid = x_ref[rows].astype(f32)
+    places = [(i, j) for i in range(high // WS) for j in inner]
     current = jnp.concatenate(
-        [grid[:, j * WS : (j + 1) * WS, :].reshape(AREA, D) for j in inner], axis=0
+        [
+            grid[i * WS : (i + 1) * WS, j * WS : (j + 1) * WS, :].reshape(AREA, D)
+            for i, j in places
+        ],
+        axis=0,
     )
     after = attention(
         current,
@@ -197,13 +205,19 @@
         proj_ref[0],
         bias_ref[...],
         attention_masks(),
-        len(inner) // 2,
+        len(places),
     )
     normed = layer_norm(after, gain_ref[1, 0:1, :])
 
     def spatial(first, value, last):
-        pieces = [value[n * AREA : (n + 1) * AREA].reshape(WS, WS, D) for n in range(len(inner))]
-        return jnp.concatenate([first, *pieces, last], axis=1)
+        pieces = [
+            value[n * AREA : (n + 1) * AREA].reshape(WS, WS, D) for n in range(len(places))
+        ]
+        lines = [
+            jnp.concatenate(pieces[i * len(inner) : (i + 1) * len(inner)], axis=1)
+            for i in range(high // WS)
+        ]
+        return jnp.concatenate([first, jnp.concatenate(lines, axis=0), last], axis=1)
 
     sum_ref[rows] = spatial(sum_left_ref[rows], after, sum_right_ref[rows])
     normed_ref[rows] = spatial(
@@ -259,13 +273,18 @@
         compiler_params=PARAMS,
         cost_estimate=work(5e8),
         name="edge_attention",
-    )(tokens, tokens, gains, qkv_weight, proj_weight, table)
+    )(
+        *[
+            pltpu.with_memory_space_constraint(a, pltpu.HBM)
+            for a in (tokens, tokens, gains, qkv_weight, proj_weight, table)
+        ]
+    )
 
 
 def inner_attention(tokens, gains, padded, proj_weight, bias, edges):
     return pl.pallas_call(
         inner_kernel,
-        grid=(tokens.shape[0] // WS,),
+        grid=(tokens.shape[0] // (4 * WS),),
         in_specs=[RESIDENT] * 9,
         out_specs=[RESIDENT] * 2,
         out_shape=[pltpu.VMEM(tokens.shape, f32), pltpu.VMEM(tokens.shape, bf16)],
@@ -309,9 +328,7 @@
     masks = attention_masks()
 
     def windows(c, carry):
-        starts = [
-            pl.multiple_of((c * TOGETHER + n) * WINDOW_ROWS, 8) for n in range(TOGETHER)
-        ]
+        starts = [(c * TOGETHER + n) * WINDOW_ROWS for n in range(TOGETHER)]
         current = jnp.concatenate(
             [
                 jnp.concatenate(
@@ -404,7 +421,7 @@
     down_s[...] = down_ref[layer].T
 
 
-def convolve_row(padded_s, taps_s, row, width):
+def convolve_row(padded_s, taps_s, shift_s, row, width):
     total = None
     for v in range(KS):
         part = None
@@ -413,11 +430,17 @@
             term = x * taps_s[u * KS + v][None]
             part = term if part is None else part + term
         part = part.reshape(-1, D).astype(f32)
-        shift = v - HALO
-        if shift < 0:
-            part = jnp.concatenate([part[RING + shift :], part[: width + shift]], axis=0)
+        if v == HALO:
+            part = part[:width]
         else:
-            part = part[shift : shift + width]
+            pieces = []
+            for n, value in enumerate((part[:, :LANES], part[:, LANES:])):
+                lanes = slice(0, value.shape[1])
+                shift_s[v, n, SEGMENT : SEGMENT + RING, lanes] = value
+                shift_s[v, n, WS:SEGMENT, lanes] = value[RING - WS :]
+                start = SEGMENT + v - HALO
+                pieces.append(shift_s[v, n, start : start + width, :])
+            part = jnp.concatenate(pieces, axis=1)[:, 0:D]
         total = part if total is None else total + part
     return total
 
@@ -448,10 +471,11 @@
     padded_s,
     after_s,
     taps_s,
+    shift_s,
     down_s,
 ):
     step = pl.program_id(0)
-    rows = WS
+    rows = 2 * WS
     width = sum_ref.shape[1]
     first = WS - HALO
 
@@ -466,7 +490,7 @@
 
     def row(j, carry):
         total = sum_ref[WS + step * rows + j] + convolve_row(
-            padded_s, taps_s, step * rows + j, width
+            padded_s, taps_s, shift_s, step * rows + j, width
         )
         after_s[pl.ds(pl.multiple_of(j * width, width), width), :] = total
         return carry
@@ -481,14 +505,15 @@
     inner = height - 2 * WS
     return pl.pallas_call(
         middle_kernel,
-        grid=(inner // WS,),
+        grid=(inner // (2 * WS),),
         in_specs=[RESIDENT] * 8,
         out_specs=RESIDENT,
         out_shape=pltpu.VMEM((inner, width, D), bf16),
         scratch_shapes=[
             pltpu.VMEM((inner + 2 * HALO, RING, D), bf16),
-            pltpu.VMEM((WS * width, D), f32),
+            pltpu.VMEM((2 * WS * width, D), f32),
             pltpu.VMEM((KS * KS, 16, D), bf16),
+            pltpu.VMEM((KS, 2, SEGMENT + RING, LANES), f32),
             pltpu.VMEM((HID, D), bf16),
         ],
         compiler_params=PARAMS,
@@ -513,12 +538,13 @@
     padded_s,
     after_s,
     taps_s,
+    shift_s,
     down_s,
     piece_s,
 ):
     step = pl.program_id(0)
     height, width, _ = normed_ref.shape
-    rows = WS // 2
+    rows = WS
     repeats = height // WS
 
     @pl.when(step == 0)
@@ -538,7 +564,7 @@
     def row(j, carry):
         part, q = j // rows, j % rows
         r = part * (height - WS) + step * rows + q
-        total = sum_ref[r] + convolve_row(padded_s, taps_s, r, width)
+        total = sum_ref[r] + convolve_row(padded_s, taps_s, shift_s, r, width)
         after_s[pl.ds(pl.multiple_of(j * width, width), width), :] = total
         return carry
 
@@ -553,12 +579,12 @@
                 line = middle_ref[(m - 1) * WS + step * rows + q].astype(f32)
             for n in range(width // SEGMENT):
                 value = line[n * SEGMENT : (n + 1) * SEGMENT]
-                place = pl.ds((q * SEGMENT + m * 4 + n) * PIECE_ROWS, SEGMENT)
+                place = pl.ds((q * SEGMENT + m * 4 + n) * PIECE_STRIDE, SEGMENT)
                 piece_s[0, place, :] = value[:, 0:LANES]
                 piece_s[1, place, 0 : D - LANES] = value[:, LANES:D]
     for q in range(rows):
         for c in range(SEGMENT):
-            place = pl.ds(q * SEGMENT * PIECE_ROWS + c, SEGMENT, stride=PIECE_ROWS)
+            place = pl.ds(q * SEGMENT * PIECE_STRIDE + c, SEGMENT, stride=PIECE_STRIDE)
             upper = piece_s[1, place, :]
             send_ref[(step * rows + q) * SEGMENT + c] = jnp.concatenate(
                 [piece_s[0, place, :], join_halves(upper[0:8], upper[8:16])], axis=0
@@ -569,7 +595,7 @@
     after, middle, normed, top, bottom, left, right, gains, taps, up_weight, down_weight, group
 ):
     height, width = normed.shape[:2]
-    rows = WS // 2
+    rows = WS
     return pl.pallas_call(
         outer_kernel,
         grid=(WS // rows,),
@@ -580,8 +606,9 @@
             pltpu.VMEM((height + 2 * HALO, RING, D), bf16),
             pltpu.VMEM((2 * rows * width, D), f32),
             pltpu.VMEM((KS * KS, 16, D), bf16),
+            pltpu.VMEM((KS, 2, SEGMENT + RING, LANES), f32),
             pltpu.VMEM((HID, D), bf16),
-            pltpu.VMEM((2, rows * SEGMENT * PIECE_ROWS, LANES), f32),
+            pltpu.VMEM((2, rows * SEGMENT * PIECE_STRIDE, LANES), f32),
         ],
         compiler_params=PARAMS,
         cost_estimate=work(8e9),
@@ -614,6 +641,7 @@
     sum_s,
     after_s,
     taps_s,
+    shift_s,
     down_s,
     piece_s,
 ):
@@ -626,7 +654,7 @@
     def _():
         prepare_finish(1, taps_ref, down_ref, taps_s, down_s)
 
-        def build(r, n, target, keep):
+        def line(n):
             pieces = []
             for m in range(width // SEGMENT + 1):
                 if n < 4 and m < 4:
@@ -637,42 +665,35 @@
                     low, high, half = 20 + n, 32 + n, 1
                 else:
                     low, high, half = 36, 37, 0
-                at = lambda k: piece_s[pl.ds(k, SEGMENT, stride=RETURN_ROWS), :]
+                at = lambda k: piece_s[pl.ds(k, SEGMENT, stride=RETURN_STRIDE), :]
                 upper = at(high)
                 if half:
                     upper = pltpu.roll(upper, D - LANES, 1)
                 pieces.append(jnp.concatenate([at(low), upper], axis=1)[:, 0:D])
-            value = jnp.concatenate(pieces, axis=0)
-            if keep:
-                sum_s[target - HALO] = value[0:width]
-            padded_s[target] = layer_norm(value, gain_ref[1, 1:2, :]).astype(bf16)
+            return jnp.concatenate(pieces, axis=0)
 
         def body(r, carry):
-            def load(c, carry):
-                piece_s[pl.ds(pl.multiple_of(c * RETURN_ROWS, 8), RETURN_ROWS), :] = back_ref[
+            for c in range(SEGMENT):
+                piece_s[c * RETURN_STRIDE : c * RETURN_STRIDE + RETURN_ROWS, :] = back_ref[
                     r * SEGMENT + c
                 ].astype(f32)
-                return carry
-
-            lax.fori_loop(0, SEGMENT, load, 0, unroll=True)
+            lines = [line(n) for n in range(repeats + 1)]
+            normed = layer_norm(jnp.concatenate(lines, axis=0), gain_ref[1, 1:2, :]).astype(bf16)
             for n in range(repeats):
-                build(r, n, HALO + r + WS * n, True)
-
-            @pl.when(r < HALO)
-            def _():
-                build(r, repeats, HALO + height + r, False)
-
-            @pl.when(r >= WS - HALO)
-            def _():
-                build(r, repeats, HALO + r - WS, False)
-
+                sum_s[r + WS * n] = lines[n][0:width]
+                padded_s[HALO + r + WS * n] = normed[n * RING : (n + 1) * RING]
+            spare = height + 2 * HALO
+            target = jnp.where(
+                r < HALO, HALO + height + r, jnp.where(r >= WS - HALO, HALO + r - WS, spare)
+            )
+            padded_s[target] = normed[repeats * RING :]
             return carry
 
         lax.fori_loop(0, WS, body, 0)
 
     def row(j, carry):
         r = step * rows + j
-        total = sum_s[r] + convolve_row(padded_s, taps_s, r, width)
+        total = sum_s[r] + convolve_row(padded_s, taps_s, shift_s, r, width)
         after_s[pl.ds(pl.multiple_of(j * width, width), width), :] = total
         return carry
 
@@ -685,17 +706,18 @@
     height, width = shape[:2]
     return pl.pallas_call(
         second_kernel,
-        grid=(height // WS,),
+        grid=(height // (2 * WS),),
         in_specs=[RESIDENT] * 5,
-        out_specs=pl.BlockSpec((WS, width, D), lambda i: (i, 0, 0)),
+        out_specs=pl.BlockSpec((2 * WS, width, D), lambda i: (i, 0, 0)),
         out_shape=jax.ShapeDtypeStruct(shape, bf16),
         scratch_shapes=[
-            pltpu.VMEM((height + 2 * HALO, RING, D), bf16),
+            pltpu.VMEM((height + 2 * HALO + 1, RING, D), bf16),
             pltpu.VMEM((height, width, D), f32),
-            pltpu.VMEM((WS * width, D), f32),
+            pltpu.VMEM((2 * WS * width, D), f32),
             pltpu.VMEM((KS * KS, 16, D), bf16),
+            pltpu.VMEM((KS, 2, SEGMENT + RING, LANES), f32),
             pltpu.VMEM((HID, D), bf16),
-            pltpu.VMEM((SEGMENT * RETURN_ROWS, LANES), f32),
+            pltpu.VMEM((SEGMENT * RETURN_STRIDE, LANES), f32),
         ],
         compiler_params=PARAMS,
         cost_estimate=work(1e10),

time: 117 us -> 104 us (0.89)
  Pallas kernels: 44 us -> 34.4 us
  local copies, waits for them, and re-layouts: 4.64 us -> 0.07 us
    pallas_call x3, Pallas kernels: 25.2 us -> 19.1 us  [the longest x1 11.3 us: second_finish(): pl.pallas_call(second_kernel, grid=(height // (2 * WS),), in_specs=[RESID...]
    unnamed x24 -> x16, local copies, waits for them, and re-layouts: 4.62 us -> 0.04 us
    pallas_call x1, Pallas kernels: 11.7 us -> 7.77 us  [shuffled_attention(): pl.pallas_call(shuffled_kernel, in_specs=[RESIDENT] * 5, out_specs=RESIDE...]
  transfers between devices with their start and end apart: 4 -> 4, of which waited for: 1 -> 1; matrix products, arithmetic and copies ran while one was open for 0% -> 0% of each run, Pallas kernels for 10% -> 8%
where the time goes in v3:
time: 104 us
  blocking collectives  53.6 us (52%)
  Pallas kernels  34.4 us (33%)
  starting transfers between devices  13 us (12%)
  waiting for transfers between devices  2.47 us (2%)
    all_to_all x1, blocking collectives, on_device(): got = lax.all_to_all(outgoing, members, 0, 0, tiled=True)  27.2 us
    all_to_all x1, blocking collectives, on_device(): back = lax.all_to_all(branch, members, 0, 0, tiled=True)  26.4 us
    ppermute x4, starting transfers between devices, shift(): return lax.ppermute(value, axes, pairs)  13 us
    pallas_call x1, Pallas kernels, second_finish(): pl.pallas_call(second_kernel, grid=(height // (2 * WS),), in_specs=[RESID...  11.3 us
    pallas_call x1, Pallas kernels, shuffled_attention(): pl.pallas_call(shuffled_kernel, in_specs=[RESIDENT] * 5, out_specs=RESIDE...  7.77 us
    pallas_call x1, Pallas kernels, outer_finish(): pl.pallas_call(outer_kernel, grid=(WS // rows,), in_specs=[RESIDENT] * 11...  4.5 us
    pallas_call x1, Pallas kernels, middle_finish(): pl.pallas_call(middle_kernel, grid=(inner // (2 * WS),), in_specs=[RESIDE...  4.36 us
    pallas_call x1, Pallas kernels, inner_attention(): pl.pallas_call(inner_kernel, grid=(tokens.shape[0] // (4 * WS),), in_spec...  3.48 us
  transfers between devices with their start and end apart: 4, of which 1 were waited for; matrix products, arithmetic and copies ran while one was open for 0% of the time, Pallas kernels for 8%

profile of v3, /device:TPU:1, one launch (start us, length us, event | category | flops | bytes accessed | tf_op | source)
XLA Modules:
  0.0 103.8 jit_solution(17579325242801636052)
XLA Ops:
  0.0 0.0 copy-start
  0.0 0.0 copy-start.2
  0.0 0.0 copy-start.4
  0.0 3.0 %edge_attention.1 = (f32[32,8,192]{2,1,0:T(8,128)S(1)}, f32[32,8,192]{2,1,0:T(8,128)S(1)}, bf16[32,8,192]{2,1,0:T(8,128)(2,1)S(1)}, bf16[32,8,192]{2,1,0:T(8,128...) custom-call(bf16[32,64,192]{2,1,0:T(8,128)(2,1)} %x_ref.1, bf16[32,64,192]{2,1,0:T(8,128)(2,1)} %x_ref.1, ...), custom_call_target="tpu_custom_call" | custom-call | flops 500000000 | bytes 1048576 | tf_op jit(solution)/shard_map/edge_attention/pallas_call | solution.py:252
  3.1 3.3 %collective-permute-start.1 = (bf16[32,8,192]{2,1,0:T(8,128)(2,1)S(1)}, bf16[32,8,192]{2,1,0:T(8,128)(2,1)S(1)}, u32[]{:S(2)}, u32[]{:S(2)}) collective-permute-start(bf16[32,8,192]{2,1,0:T(8,128)(2,1)S(1)} %get-tuple-element.17.left_ref), channel_id=1, source_target_pairs={{1,0},{2,1},{3,2},{4,3},{5,4},{6,5},{7,6},{8,7},{9,8},{10,9},{11,1... | collective-permute-start | bytes 294920 | tf_op jit(solution)/shard_map/ppermute | solution.py:731
  6.4 3.6 %collective-permute-start = (bf16[32,8,192]{2,1,0:T(8,128)(2,1)S(1)}, bf16[32,8,192]{2,1,0:T(8,128)(2,1)S(1)}, u32[]{:S(2)}, u32[]{:S(2)}) collective-permute-start(bf16[32,8,192]{2,1,0:T(8,128)(2,1)S(1)} %get-tuple-element.18.right_ref), channel_id=1, source_target_pairs={{0,1},{1,2},{2,3},{3,4},{4,5},{5,6},{6,7},{7,8},{8,9},{9,10},{10,1... | collective-permute-start | bytes 294920 | tf_op jit(solution)/shard_map/ppermute | solution.py:731
  9.9 0.0 copy-done
  9.9 0.0 copy-done.2
  10.0 0.0 copy-done.4
  10.0 0.0 copy-start.5
  10.0 0.0 copy-start.6
  10.0 0.0 copy-start.7
  10.0 3.5 %inner_attention.1 = (f32[32,64,192]{2,1,0:T(8,128)S(1)}, bf16[32,64,192]{2,1,0:T(8,128)(2,1)S(1)}) custom-call(bf16[32,64,192]{2,1,0:T(8,128)(2,1)S(1)} %copy-done, f32[3,2,192]{2,1,0:T(2,128)S(1)} %bitcast.7, bf16[192,768]{1,0:T(8,128)(2,1)S(1)} %get-tuple-element.13.pad_ref, bf16[2,192,192]{2,1,0:T(8,128)(2,1)S(1)} %copy-done.2, ...), custom_call_target="tpu_custom_call" | custom-call | flops 8000000000 | bytes 1048576 | tf_op jit(solution)/shard_map/inner_attention/pallas_call | solution.py:285
  13.5 0.0 collective-permute-done.1.right_ref
  13.5 0.0 collective-permute-done.left_ref
  13.6 4.8 %collective-permute-start.2 = (bf16[3,80,192]{2,1,0:T(8,128)(2,1)S(1)}, bf16[3,80,192]{2,1,0:T(8,128)(2,1)S(1)}, u32[]{:S(2)}, u32[]{:S(2)}) collective-permute-start(bf16[3,80,192]{2,1,0:T(8,128)(2,1)S(1)} %pad_maximum_fusion), channel_id=1, source_target_pairs={{0,16},{16,32},{32,48},{48,64},{64,80},{80,96},{96,112},{1,17},{17... | collective-permute-start | bytes 276488 | tf_op jit(solution)/shard_map/ppermute | solution.py:731
  18.4 1.3 %collective-permute-start.3 = (bf16[3,80,192]{2,1,0:T(8,128)(2,1)S(1)}, bf16[3,80,192]{2,1,0:T(8,128)(2,1)S(1)}, u32[]{:S(2)}, u32[]{:S(2)}) collective-permute-start(bf16[3,80,192]{2,1,0:T(8,128)(2,1)S(1)} %pad_maximum_fusion.1), channel_id=1, source_target_pairs={{16,0},{32,16},{48,32},{64,48},{80,64},{96,80},{112,96},{17,1},{33... | collective-permute-start | bytes 276488 | tf_op jit(solution)/shard_map/ppermute | solution.py:731
  19.7 0.0 copy-done.5
  19.8 0.0 copy-done.6
  19.8 0.0 copy-done.7
  19.8 4.4 %middle_finish.1.middle_ref = bf16[16,64,192]{2,1,0:T(8,128)(2,1)S(1)} custom-call(f32[32,64,192]{2,1,0:T(8,128)S(1)} %get-tuple-element.19.sum_ref, bf16[32,64,192]{2,1,0:T(8,128)(2,1)S(1)} %get-tuple-element.20.normed_ref, bf16[32,8,192]{2,1,0:T(8,128)(2,1)S(1)} %collective-permute-done.left_ref, bf16[32,8,192]{2,1,0:T(8,128)(2,1)S(1)} %collective-permute-done.1.right_ref, ...), custom_call_target="tpu_custom_call" | custom-call | flops 8000000000 | bytes 1048576 | tf_op jit(solution)/shard_map/middle_finish/pallas_call | solution.py:506
  24.1 0.0 collective-permute-done.2.top_ref
  24.1 2.5 %collective-permute-done.3.bottom_ref = bf16[3,80,192]{2,1,0:T(8,128)(2,1)S(1)} collective-permute-done((bf16[3,80,192]{2,1,0:T(8,128)(2,1)S(1)}, bf16[3,80,192]{2,1,0:T(8,128)(2,1)S(1)}, u32[]{:S(2)}, u32[]{:S(2)}) %collective-permute-start.3) | collective-permute-done | bytes 92192 | tf_op jit(solution)/shard_map/ppermute | solution.py:731
  26.6 4.5 %outer_finish.1 = bf16[128,24,128]{2,1,0:T(8,128)(2,1)S(1)} custom-call(f32[32,64,192]{2,1,0:T(8,128)S(1)} %get-tuple-element.19.sum_ref, bf16[16,64,192]{2,1,0:T(8,128)(2,1)S(1)} %middle_finish.1.middle_ref, bf16[32,64,192]{2,1,0:T(8,128)(2,1)S(1)} %get-tuple-element.20.normed_ref, bf16[3,80,192]{2,1,0:T(8,128)(2,1)S(1)} %collective-permute-done.2.top_ref, ...), custom_call_target="tpu_custom_call" | custom-call | flops 8000000000 | bytes 1048576 | tf_op jit(solution)/shard_map/outer_finish/pallas_call | solution.py:599
  31.1 0.0 copy-start.1
  31.1 0.0 copy-start.3
  31.1 27.2 %all_to_all.10.got_ref = bf16[128,24,128]{2,1,0:T(8,128)(2,1)S(1)} all-to-all(bf16[128,24,128]{2,1,0:T(8,128)(2,1)S(1)} %outer_finish.1), channel_id=1, replica_groups=mesh['row'=8,'block'=8,'core'=2] {'row','block','core'}, dimensions={0} | all-to-all | bytes 1572864 | tf_op jit(solution)/shard_map/all_to_all | solution.py:766
  58.3 0.0 copy-done.1
  58.3 0.0 copy-done.3
  58.3 7.8 %shuffled_attention.1 = bf16[128,40,128]{2,1,0:T(8,128)(2,1)S(1)} custom-call(bf16[128,24,128]{2,1,0:T(8,128)(2,1)S(1)} %all_to_all.10.got_ref, f32[3,2,192]{2,1,0:T(2,128)S(1)} %bitcast.10, bf16[2,192,576]{2,1,0:T(8,128)(2,1)S(1)} %copy-done.1, bf16[2,192,192]{2,1,0:T(8,128)(2,1)S(1)} %copy-done.2, f32[6,2,225]{2,1,0:T(2,128)S(1)} %bitcast.5), custom_call_target="tpu_custom_call" | custom-call | flops 10000000000 | bytes 1048576 | tf_op jit(solution)/shard_map/shuffled_attention/pallas_call | solution.py:400
  66.1 26.4 %all_to_all.11.back_ref = bf16[128,40,128]{2,1,0:T(8,128)(2,1)S(1)} all-to-all(bf16[128,40,128]{2,1,0:T(8,128)(2,1)S(1)} %shuffled_attention.1), channel_id=1, replica_groups=mesh['row'=8,'block'=8,'core'=2] {'row','block','core'}, dimensions={0} | all-to-all | bytes 2621440 | tf_op jit(solution)/shard_map/all_to_all | solution.py:768
  92.5 11.3 %second_finish.1 = bf16[32,64,192]{2,1,0:T(8,128)(2,1)} custom-call(bf16[128,40,128]{2,1,0:T(8,128)(2,1)S(1)} %all_to_all.11.back_ref, f32[3,2,192]{2,1,0:T(2,128)S(1)} %bitcast.11, f32[49,2,192]{2,1,0:T(2,128)S(1)} %bitcast.17, bf16[2,192,768]{2,1,0:T(8,128)(2,1)S(1)} %copy-done.5, bf16[2,192,768]{2,1,0:T(8,128)(2,1)S(1)} %bitcast.14), custom_call_target="tpu_custom_call" | custom-call | flops 10000000000 | bytes 1048576 | tf_op jit(solution)/shard_map/second_finish/pallas_call | solution.py:707
  (5 shorter events, 0.1 us)
Async XLA Ops:
  0.0 9.9 %copy-start = (bf16[32,64,192]{2,1,0:T(8,128)(2,1)S(1)}, bf16[32,64,192]{2,1,0:T(8,128)(2,1)}, u32[]{:S(2)}) copy-start(bf16[32,64,192]{2,1,0:T(8,128)(2,1)} %x_ref.1) | copy-start | bytes 2359300
  0.0 9.9 %copy-start.2 = (bf16[2,192,192]{2,1,0:T(8,128)(2,1)S(1)}, bf16[2,192,192]{2,1,0:T(8,128)(2,1)}, u32[]{:S(2)}) copy-start(bf16[2,192,192]{2,1,0:T(8,128)(2,1)} %proj_ref.5) | copy-start | bytes 442372
  0.0 9.9 %copy-start.4 = (f32[2,3,192]{2,0,1:T(2,128)S(1)}, f32[2,3,192]{2,0,1:T(2,128)}, u32[]{:S(2)}) copy-start(f32[2,3,192]{2,0,1:T(2,128)} %param.9) | copy-start | bytes 13828
  3.1 10.4 %collective-permute-start.1 = (bf16[32,8,192]{2,1,0:T(8,128)(2,1)S(1)}, bf16[32,8,192]{2,1,0:T(8,128)(2,1)S(1)}, u32[]{:S(2)}, u32[]{:S(2)}) collective-permute-start(bf16[32,8,192]{2,1,0:T(8,128)(2,1)S(1)} %get-tuple-element.17.left_ref), channel_id=1, source_target_pairs={{1,0},{2,1},{3,2},{4,3},{5,4},{6,5},{7,6},{8,7},{9,8},{10,9},{11,1... | collective-permute-start | bytes 294920 | tf_op jit(solution)/shard_map/ppermute | solution.py:731
  6.4 7.2 %collective-permute-start = (bf16[32,8,192]{2,1,0:T(8,128)(2,1)S(1)}, bf16[32,8,192]{2,1,0:T(8,128)(2,1)S(1)}, u32[]{:S(2)}, u32[]{:S(2)}) collective-permute-start(bf16[32,8,192]{2,1,0:T(8,128)(2,1)S(1)} %get-tuple-element.18.right_ref), channel_id=1, source_target_pairs={{0,1},{1,2},{2,3},{3,4},{4,5},{5,6},{6,7},{7,8},{8,9},{9,10},{10,1... | collective-permute-start | bytes 294920 | tf_op jit(solution)/shard_map/ppermute | solution.py:731
  10.0 9.8 %copy-start.5 = (bf16[2,192,768]{2,1,0:T(8,128)(2,1)S(1)}, bf16[2,192,768]{2,1,0:T(8,128)(2,1)}, u32[]{:S(2)}) copy-start(bf16[2,192,768]{2,1,0:T(8,128)(2,1)} %up_ref.5) | copy-start | bytes 1769476
  10.0 9.8 %copy-start.6 = (bf16[2,768,192]{1,2,0:T(8,128)(2,1)S(1)}, bf16[2,768,192]{1,2,0:T(8,128)(2,1)}, u32[]{:S(2)}) copy-start(bf16[2,768,192]{1,2,0:T(8,128)(2,1)} %param.15) | copy-start | bytes 1769476
  10.0 9.8 %copy-start.7 = (f32[2,49,192]{2,0,1:T(2,128)S(1)}, f32[2,49,192]{2,0,1:T(2,128)}, u32[]{:S(2)}) copy-start(f32[2,49,192]{2,0,1:T(2,128)} %param.13) | copy-start | bytes 225796
  13.6 10.6 %collective-permute-start.2 = (bf16[3,80,192]{2,1,0:T(8,128)(2,1)S(1)}, bf16[3,80,192]{2,1,0:T(8,128)(2,1)S(1)}, u32[]{:S(2)}, u32[]{:S(2)}) collective-permute-start(bf16[3,80,192]{2,1,0:T(8,128)(2,1)S(1)} %pad_maximum_fusion), channel_id=1, source_target_pairs={{0,16},{16,32},{32,48},{48,64},{64,80},{80,96},{96,112},{1,17},{17... | collective-permute-start | bytes 276488 | tf_op jit(solution)/shard_map/ppermute | solution.py:731
  18.4 8.2 %collective-permute-start.3 = (bf16[3,80,192]{2,1,0:T(8,128)(2,1)S(1)}, bf16[3,80,192]{2,1,0:T(8,128)(2,1)S(1)}, u32[]{:S(2)}, u32[]{:S(2)}) collective-permute-start(bf16[3,80,192]{2,1,0:T(8,128)(2,1)S(1)} %pad_maximum_fusion.1), channel_id=1, source_target_pairs={{16,0},{32,16},{48,32},{64,48},{80,64},{96,80},{112,96},{17,1},{33... | collective-permute-start | bytes 276488 | tf_op jit(solution)/shard_map/ppermute | solution.py:731
  31.1 27.2 %copy-start.1 = (bf16[2,192,576]{2,1,0:T(8,128)(2,1)S(1)}, bf16[2,192,576]{2,1,0:T(8,128)(2,1)}, u32[]{:S(2)}) copy-start(bf16[2,192,576]{2,1,0:T(8,128)(2,1)} %qkv_ref.3) | copy-start | bytes 1327108
  31.1 27.2 %copy-start.3 = (f32[2,6,225]{2,0,1:T(2,128)S(1)}, f32[2,6,225]{2,0,1:T(2,128)}, u32[]{:S(2)}) copy-start(f32[2,6,225]{2,0,1:T(2,128)} %param.12) | copy-start | bytes 32404

commit v4 on v3

--- a/solution.py
+++ b/solution.py
@@ -725,10 +725,18 @@
     )(*resident(back, gains, taps, up_weight, down_weight))
 
 
-def shift(value, axes, forward):
+def swap(first, last, axes):
     count = lax.axis_size(axes)
-    pairs = [(i, i + 1) if forward else (i + 1, i) for i in range(count - 1)]
-    return lax.ppermute(value, axes, pairs)
+    even = lax.axis_index(axes) % 2 == 0
+    results = []
+    for start in range(2):
+        pairs = [
+            pair for i in range(start, count - 1, 2) for pair in ((i, i + 1), (i + 1, i))
+        ]
+        facing = jnp.where(even, last, first) if start == 0 else jnp.where(even, first, last)
+        results.append(lax.ppermute(facing, axes, pairs))
+    partner, other = results
+    return jnp.where(even, other, partner), jnp.where(even, partner, other)
 
 
 def on_device(
@@ -741,13 +749,11 @@
     taps = conv_weight.transpose(1, 0, 2)
     down_weight = down_weight.transpose(0, 2, 1)
     *edges, bias, padded = edge_attention(tokens, gains, qkv_weight, proj_weight, table)
-    left = shift(edges[3], columns, True)
-    right = shift(edges[2], columns, False)
+    left, right = swap(edges[2], edges[3], columns)
     after, normed = inner_attention(tokens, gains, padded, proj_weight, bias, edges)
     around = lambda rows: jnp.concatenate([normed[rows], right[rows], left[rows]], axis=1)
     height = tokens.shape[0]
-    top = shift(around(slice(height - HALO, height)), "row", True)
-    bottom = shift(around(slice(0, HALO)), "row", False)
+    top, bottom = swap(around(slice(0, HALO)), around(slice(height - HALO, height)), "row")
     middle = middle_finish(after, normed, left, right, gains, taps, up_weight, down_weight)
     outgoing = outer_finish(
         after,

time: 104 us -> 101 us (0.971)
  starting transfers between devices: 13 us -> 8.67 us
  local copies, waits for them, and re-layouts: 0.07 us -> 2.96 us
  waiting for transfers between devices: 2.47 us -> 0.01 us
    ppermute x4, starting transfers between devices: 13 us -> 8.67 us  [swap(): results.append(lax.ppermute(facing, axes, pairs))]
    unnamed x16 -> x20, local copies, waits for them, and re-layouts: 0.04 us -> 2.94 us
    ppermute x4, waiting for transfers between devices: 2.47 us -> 0.01 us  [swap(): results.append(lax.ppermute(facing, axes, pairs))]
    all_to_all x1, blocking collectives: 27.2 us -> 28.2 us  [on_device(): got = lax.all_to_all(outgoing, members, 0, 0, tiled=True)]
  transfers between devices with their start and end apart: 4 -> 4, of which waited for: 1 -> 0; matrix products, arithmetic and copies ran while one was open for 0% -> 0% of each run, Pallas kernels for 8% -> 8%
where the time goes in v4:
time: 101 us
  blocking collectives  54.6 us (54%)
  Pallas kernels  34.4 us (34%)
  starting transfers between devices  8.67 us (9%)
  local copies, waits for them, and re-layouts  2.96 us (3%)
    all_to_all x1, blocking collectives, on_device(): got = lax.all_to_all(outgoing, members, 0, 0, tiled=True)  28.2 us
    all_to_all x1, blocking collectives, on_device(): back = lax.all_to_all(branch, members, 0, 0, tiled=True)  26.4 us
    pallas_call x1, Pallas kernels, second_finish(): pl.pallas_call(second_kernel, grid=(height // (2 * WS),), in_specs=[RESID...  11.3 us
    ppermute x4, starting transfers between devices, swap(): results.append(lax.ppermute(facing, axes, pairs))  8.67 us
    pallas_call x1, Pallas kernels, shuffled_attention(): pl.pallas_call(shuffled_kernel, in_specs=[RESIDENT] * 5, out_specs=RESIDE...  7.75 us
    pallas_call x1, Pallas kernels, outer_finish(): pl.pallas_call(outer_kernel, grid=(WS // rows,), in_specs=[RESIDENT] * 11...  4.5 us
    pallas_call x1, Pallas kernels, middle_finish(): pl.pallas_call(middle_kernel, grid=(inner // (2 * WS),), in_specs=[RESIDE...  4.31 us
    pallas_call x1, Pallas kernels, inner_attention(): pl.pallas_call(inner_kernel, grid=(tokens.shape[0] // (4 * WS),), in_spec...  3.48 us
  transfers between devices with their start and end apart: 4, of which 0 were waited for; matrix products, arithmetic and copies ran while one was open for 0% of the time, Pallas kernels for 8%

profile of v4, /device:TPU:1, one launch (start us, length us, event | category | flops | bytes accessed | tf_op | source)
XLA Modules:
  0.0 101.0 jit_solution(3520908644305251460)
XLA Ops:
  0.0 0.0 copy-start
  0.0 3.0 %edge_attention.1 = (f32[32,8,192]{2,1,0:T(8,128)S(1)}, f32[32,8,192]{2,1,0:T(8,128)S(1)}, bf16[32,8,192]{2,1,0:T(8,128)(2,1)S(1)}, bf16[32,8,192]{2,1,0:T(8,128...) custom-call(bf16[32,64,192]{2,1,0:T(8,128)(2,1)} %x_ref.1, bf16[32,64,192]{2,1,0:T(8,128)(2,1)} %x_ref.1, ...), custom_call_target="tpu_custom_call" | custom-call | flops 500000000 | bytes 1048576 | tf_op jit(solution)/shard_map/edge_attention/pallas_call | solution.py:252
  3.1 1.5 %collective-permute-start.1 = (bf16[32,8,192]{2,1,0:T(8,128)(2,1)S(1)}, bf16[32,8,192]{2,1,0:T(8,128)(2,1)S(1)}, u32[]{:S(2)}, u32[]{:S(2)}) collective-permute-start(bf16[32,8,192]{2,1,0:T(8,128)(2,1)S(1)} %get-tuple-element.25), channel_id=1, source_target_pairs={{0,1},{1,0},{2,3},{3,2},{4,5},{5,4},{6,7},{7,6},{8,9},{9,8},{10,11... | collective-permute-start | bytes 294920 | tf_op jit(solution)/shard_map/ppermute | solution.py:737
  4.6 3.6 %collective-permute-start = (bf16[32,8,192]{2,1,0:T(8,128)(2,1)S(1)}, bf16[32,8,192]{2,1,0:T(8,128)(2,1)S(1)}, u32[]{:S(2)}, u32[]{:S(2)}) collective-permute-start(bf16[32,8,192]{2,1,0:T(8,128)(2,1)S(1)} %get-tuple-element.26), channel_id=1, source_target_pairs={{1,2},{2,1},{3,4},{4,3},{5,6},{6,5},{7,8},{8,7},{9,10},{10,9},{11,... | collective-permute-start | bytes 294920 | tf_op jit(solution)/shard_map/ppermute | solution.py:737
  8.1 0.0 copy-done
  8.1 0.0 copy-done.2
  8.1 0.0 copy-done.4
  8.2 3.5 %inner_attention.1 = (f32[32,64,192]{2,1,0:T(8,128)S(1)}, bf16[32,64,192]{2,1,0:T(8,128)(2,1)S(1)}) custom-call(bf16[32,64,192]{2,1,0:T(8,128)(2,1)S(1)} %copy-done, f32[3,2,192]{2,1,0:T(2,128)S(1)} %bitcast.7, bf16[192,768]{1,0:T(8,128)(2,1)S(1)} %get-tuple-element.13.pad_ref, bf16[2,192,192]{2,1,0:T(8,128)(2,1)S(1)} %copy-done.2, ...), custom_call_target="tpu_custom_call" | custom-call | flops 8000000000 | bytes 1048576 | tf_op jit(solution)/shard_map/inner_attention/pallas_call | solution.py:285
  11.6 0.0 copy-start.8
  11.7 1.3 %copy-done.8 = f32[32,64,192]{2,1,0:T(8,128)} copy-done((f32[32,64,192]{2,1,0:T(8,128)}, f32[32,64,192]{2,1,0:T(8,128)S(1)}, u32[]{:S(2)}) %copy-start.8) | copy-done | bytes 1572888
  13.0 0.0 collective-permute-done.1
  13.0 0.0 collective-permute-done
  13.1 0.1 broadcast_select_fusion.6
  13.2 3.0 %collective-permute-start.3 = (bf16[3,80,192]{2,1,0:T(8,128)(2,1)S(1)}, bf16[3,80,192]{2,1,0:T(8,128)(2,1)S(1)}, u32[]{:S(2)}, u32[]{:S(2)}) collective-permute-start(bf16[3,80,192]{2,1,0:T(8,128)(2,1)S(1)} %get-tuple-element.29), channel_id=1, source_target_pairs={{0,16},{16,0},{32,48},{48,32},{64,80},{80,64},{96,112},{112,96},{1... | collective-permute-start | bytes 276488 | tf_op jit(solution)/shard_map/ppermute | solution.py:737
  16.1 0.7 collective-permute-start.2
  16.8 0.0 copy-done.5
  16.8 0.0 copy-done.6
  16.8 0.0 copy-done.7
  16.8 0.0 copy-start.9
  16.9 1.6 %copy-done.9 = f32[32,64,192]{2,1,0:T(8,128)S(1)} copy-done((f32[32,64,192]{2,1,0:T(8,128)S(1)}, f32[32,64,192]{2,1,0:T(8,128)}, u32[]{:S(2)}) %copy-start.9) | copy-done | bytes 1572888
  18.4 4.3 %middle_finish.1.middle_ref = bf16[16,64,192]{2,1,0:T(8,128)(2,1)S(1)} custom-call(f32[32,64,192]{2,1,0:T(8,128)S(1)} %copy-done.9, bf16[32,64,192]{2,1,0:T(8,128)(2,1)S(1)} %get-tuple-element.20.normed_ref, bf16[32,8,192]{2,1,0:T(8,128)(2,1)S(1)} %get-tuple-element.24.left_ref, bf16[32,8,192]{2,1,0:T(8,128)(2,1)S(1)} %get-tuple-element.23.right_ref, ...), custom_call_target="tpu_custom_call" | custom-call | flops 8000000000 | bytes 1048576 | tf_op jit(solution)/shard_map/middle_finish/pallas_call | solution.py:506
  22.7 0.0 collective-permute-done.3
  22.8 0.0 collective-permute-done.2
  22.8 4.5 %outer_finish.1 = bf16[128,24,128]{2,1,0:T(8,128)(2,1)S(1)} custom-call(f32[32,64,192]{2,1,0:T(8,128)S(1)} %copy-done.9, bf16[16,64,192]{2,1,0:T(8,128)(2,1)S(1)} %middle_finish.1.middle_ref, bf16[32,64,192]{2,1,0:T(8,128)(2,1)S(1)} %get-tuple-element.20.normed_ref, bf16[3,80,192]{2,1,0:T(8,128)(2,1)S(1)} %get-tuple-element.28.top_ref, ...), custom_call_target="tpu_custom_call" | custom-call | flops 8000000000 | bytes 1048576 | tf_op jit(solution)/shard_map/outer_finish/pallas_call | solution.py:599
  27.3 0.0 copy-start.1
  27.3 0.0 copy-start.3
  27.3 28.2 %all_to_all.10.got_ref = bf16[128,24,128]{2,1,0:T(8,128)(2,1)S(1)} all-to-all(bf16[128,24,128]{2,1,0:T(8,128)(2,1)S(1)} %outer_finish.1), channel_id=1, replica_groups=mesh['row'=8,'block'=8,'core'=2] {'row','block','core'}, dimensions={0} | all-to-all | bytes 1572864 | tf_op jit(solution)/shard_map/all_to_all | solution.py:772
  55.6 0.0 copy-done.1
  55.6 0.0 copy-done.3
  55.6 7.8 %shuffled_attention.1 = bf16[128,40,128]{2,1,0:T(8,128)(2,1)S(1)} custom-call(bf16[128,24,128]{2,1,0:T(8,128)(2,1)S(1)} %all_to_all.10.got_ref, f32[3,2,192]{2,1,0:T(2,128)S(1)} %bitcast.10, bf16[2,192,576]{2,1,0:T(8,128)(2,1)S(1)} %copy-done.1, bf16[2,192,192]{2,1,0:T(8,128)(2,1)S(1)} %copy-done.2, f32[6,2,225]{2,1,0:T(2,128)S(1)} %bitcast.5), custom_call_target="tpu_custom_call" | custom-call | flops 10000000000 | bytes 1048576 | tf_op jit(solution)/shard_map/shuffled_attention/pallas_call | solution.py:400
  63.3 26.4 %all_to_all.11.back_ref = bf16[128,40,128]{2,1,0:T(8,128)(2,1)S(1)} all-to-all(bf16[128,40,128]{2,1,0:T(8,128)(2,1)S(1)} %shuffled_attention.1), channel_id=1, replica_groups=mesh['row'=8,'block'=8,'core'=2] {'row','block','core'}, dimensions={0} | all-to-all | bytes 2621440 | tf_op jit(solution)/shard_map/all_to_all | solution.py:774
  89.7 11.3 %second_finish.1 = bf16[32,64,192]{2,1,0:T(8,128)(2,1)} custom-call(bf16[128,40,128]{2,1,0:T(8,128)(2,1)S(1)} %all_to_all.11.back_ref, f32[3,2,192]{2,1,0:T(2,128)S(1)} %bitcast.11, f32[49,2,192]{2,1,0:T(2,128)S(1)} %bitcast.17, bf16[2,192,768]{2,1,0:T(8,128)(2,1)S(1)} %copy-done.5, bf16[2,192,768]{2,1,0:T(8,128)(2,1)S(1)} %bitcast.14), custom_call_target="tpu_custom_call" | custom-call | flops 10000000000 | bytes 1048576 | tf_op jit(solution)/shard_map/second_finish/pallas_call | solution.py:707
  (10 shorter events, 0.1 us)
Async XLA Ops:
  0.0 8.1 %copy-start = (bf16[32,64,192]{2,1,0:T(8,128)(2,1)S(1)}, bf16[32,64,192]{2,1,0:T(8,128)(2,1)}, u32[]{:S(2)}) copy-start(bf16[32,64,192]{2,1,0:T(8,128)(2,1)} %x_ref.1) | copy-start | bytes 2359300
  0.0 8.1 %copy-start.2 = (bf16[2,192,192]{2,1,0:T(8,128)(2,1)S(1)}, bf16[2,192,192]{2,1,0:T(8,128)(2,1)}, u32[]{:S(2)}) copy-start(bf16[2,192,192]{2,1,0:T(8,128)(2,1)} %proj_ref.5) | copy-start | bytes 442372
  0.0 8.1 %copy-start.4 = (f32[2,3,192]{2,0,1:T(2,128)S(1)}, f32[2,3,192]{2,0,1:T(2,128)}, u32[]{:S(2)}) copy-start(f32[2,3,192]{2,0,1:T(2,128)} %param.9) | copy-start | bytes 13828
  3.1 9.9 %collective-permute-start.1 = (bf16[32,8,192]{2,1,0:T(8,128)(2,1)S(1)}, bf16[32,8,192]{2,1,0:T(8,128)(2,1)S(1)}, u32[]{:S(2)}, u32[]{:S(2)}) collective-permute-start(bf16[32,8,192]{2,1,0:T(8,128)(2,1)S(1)} %get-tuple-element.25), channel_id=1, source_target_pairs={{0,1},{1,0},{2,3},{3,2},{4,5},{5,4},{6,7},{7,6},{8,9},{9,8},{10,11... | collective-permute-start | bytes 294920 | tf_op jit(solution)/shard_map/ppermute | solution.py:737
  4.6 8.5 %collective-permute-start = (bf16[32,8,192]{2,1,0:T(8,128)(2,1)S(1)}, bf16[32,8,192]{2,1,0:T(8,128)(2,1)S(1)}, u32[]{:S(2)}, u32[]{:S(2)}) collective-permute-start(bf16[32,8,192]{2,1,0:T(8,128)(2,1)S(1)} %get-tuple-element.26), channel_id=1, source_target_pairs={{1,2},{2,1},{3,4},{4,3},{5,6},{6,5},{7,8},{8,7},{9,10},{10,9},{11,... | collective-permute-start | bytes 294920 | tf_op jit(solution)/shard_map/ppermute | solution.py:737
  11.6 1.3 %copy-start.8 = (f32[32,64,192]{2,1,0:T(8,128)}, f32[32,64,192]{2,1,0:T(8,128)S(1)}, u32[]{:S(2)}) copy-start(f32[32,64,192]{2,1,0:T(8,128)S(1)} %get-tuple-element.19.sum_ref) | copy-start | bytes 4718596
  13.0 3.8 %copy-start.5 = (bf16[2,192,768]{2,1,0:T(8,128)(2,1)S(1)}, bf16[2,192,768]{2,1,0:T(8,128)(2,1)}, u32[]{:S(2)}) copy-start(bf16[2,192,768]{2,1,0:T(8,128)(2,1)} %up_ref.5) | copy-start | bytes 1769476
  13.0 3.8 %copy-start.6 = (bf16[2,768,192]{1,2,0:T(8,128)(2,1)S(1)}, bf16[2,768,192]{1,2,0:T(8,128)(2,1)}, u32[]{:S(2)}) copy-start(bf16[2,768,192]{1,2,0:T(8,128)(2,1)} %param.15) | copy-start | bytes 1769476
  13.0 3.9 %copy-start.7 = (f32[2,49,192]{2,0,1:T(2,128)S(1)}, f32[2,49,192]{2,0,1:T(2,128)}, u32[]{:S(2)}) copy-start(f32[2,49,192]{2,0,1:T(2,128)} %param.13) | copy-start | bytes 225796
  13.2 9.6 %collective-permute-start.3 = (bf16[3,80,192]{2,1,0:T(8,128)(2,1)S(1)}, bf16[3,80,192]{2,1,0:T(8,128)(2,1)S(1)}, u32[]{:S(2)}, u32[]{:S(2)}) collective-permute-start(bf16[3,80,192]{2,1,0:T(8,128)(2,1)S(1)} %get-tuple-element.29), channel_id=1, source_target_pairs={{0,16},{16,0},{32,48},{48,32},{64,80},{80,64},{96,112},{112,96},{1... | collective-permute-start | bytes 276488 | tf_op jit(solution)/shard_map/ppermute | solution.py:737
  16.1 6.6 %collective-permute-start.2 = (bf16[3,80,192]{2,1,0:T(8,128)(2,1)S(1)}, bf16[3,80,192]{2,1,0:T(8,128)(2,1)S(1)}, u32[]{:S(2)}, u32[]{:S(2)}) collective-permute-start(bf16[3,80,192]{2,1,0:T(8,128)(2,1)S(1)} %get-tuple-element.30), channel_id=1, source_target_pairs={{16,32},{32,16},{48,64},{64,48},{80,96},{96,80},{17,33},{33,17},{4... | collective-permute-start | bytes 276488 | tf_op jit(solution)/shard_map/ppermute | solution.py:737
  16.8 1.6 %copy-start.9 = (f32[32,64,192]{2,1,0:T(8,128)S(1)}, f32[32,64,192]{2,1,0:T(8,128)}, u32[]{:S(2)}) copy-start(f32[32,64,192]{2,1,0:T(8,128)} %copy-done.8) | copy-start | bytes 4718596
  27.3 28.3 %copy-start.1 = (bf16[2,192,576]{2,1,0:T(8,128)(2,1)S(1)}, bf16[2,192,576]{2,1,0:T(8,128)(2,1)}, u32[]{:S(2)}) copy-start(bf16[2,192,576]{2,1,0:T(8,128)(2,1)} %qkv_ref.3) | copy-start | bytes 1327108
  27.3 28.3 %copy-start.3 = (f32[2,6,225]{2,0,1:T(2,128)S(1)}, f32[2,6,225]{2,0,1:T(2,128)}, u32[]{:S(2)}) copy-start(f32[2,6,225]{2,0,1:T(2,128)} %param.12) | copy-start | bytes 32404

commit v5 on v3

--- a/solution.py
+++ b/solution.py
@@ -149,6 +149,8 @@
     sum_right_ref,
     left_out_ref,
     right_out_ref,
+    facing_ref,
+    behind_ref,
     bias_ref,
     pad_ref,
     rows_s,
@@ -169,8 +171,13 @@
     shape = sum_left_ref.shape
     sum_left_ref[...] = after[:half].reshape(shape)
     sum_right_ref[...] = after[half:].reshape(shape)
-    left_out_ref[...] = normed[:half].reshape(shape).astype(bf16)
-    right_out_ref[...] = normed[half:].reshape(shape).astype(bf16)
+    left = normed[:half].reshape(shape)
+    right = normed[half:].reshape(shape)
+    left_out_ref[...] = left.astype(bf16)
+    right_out_ref[...] = right.astype(bf16)
+    even = lax.axis_index("core") == 0
+    facing_ref[...] = jnp.where(even, right, left).astype(bf16)
+    behind_ref[...] = jnp.where(even, left, right).astype(bf16)
 
 
 def inner_kernel(
@@ -260,10 +267,12 @@
             full(proj_weight),
             full(table),
         ],
-        out_specs=[RESIDENT] * 6,
+        out_specs=[RESIDENT] * 8,
         out_shape=[
             pltpu.VMEM(side, f32),
             pltpu.VMEM(side, f32),
+            pltpu.VMEM(side, bf16),
+            pltpu.VMEM(side, bf16),
             pltpu.VMEM(side, bf16),
             pltpu.VMEM(side, bf16),
             pltpu.VMEM((HEADS // 2 * AREA, LANES), f32),
@@ -522,12 +531,47 @@
     )(*resident(after, normed, left, right, gains, taps, up_weight, down_weight))
 
 
+def turn_kernel(
+    normed_ref, partner_ref, other_ref, left_ref, right_ref, facing_ref, behind_ref
+):
+    height = normed_ref.shape[0]
+    even = lax.axis_index("core") == 0
+    partner = partner_ref[...].astype(f32)
+    other = other_ref[...].astype(f32)
+    left_ref[...] = jnp.where(even, other, partner).astype(bf16)
+    right_ref[...] = jnp.where(even, partner, other).astype(bf16)
+    even = lax.axis_index("row") % 2 == 0
+    for r in range(HALO):
+        first = ring(normed_ref[r], right_ref[r], left_ref[r]).astype(f32)
+        n = height - HALO + r
+        last = ring(normed_ref[n], right_ref[n], left_ref[n]).astype(f32)
+        facing_ref[r] = jnp.where(even, last, first).astype(bf16)
+        behind_ref[r] = jnp.where(even, first, last).astype(bf16)
+
+
+def turn(normed, partner, other):
+    rows = (HALO, RING, D)
+    return pl.pallas_call(
+        turn_kernel,
+        in_specs=[RESIDENT] * 3,
+        out_specs=[RESIDENT] * 4,
+        out_shape=[
+            pltpu.VMEM(partner.shape, bf16),
+            pltpu.VMEM(partner.shape, bf16),
+            pltpu.VMEM(rows, bf16),
+            pltpu.VMEM(rows, bf16),
+        ],
+        compiler_params=PARAMS,
+        name="turn",
+    )(*resident(normed, partner, other))
+
+
 def outer_kernel(
     sum_ref,
     middle_ref,
     normed_ref,
-    top_ref,
-    bottom_ref,
+    partner_ref,
+    other_ref,
     left_ref,
     right_ref,
     gain_ref,
@@ -549,9 +593,12 @@
 
     @pl.when(step == 0)
     def _():
+        even = lax.axis_index("row") % 2 == 0
         for r in range(HALO):
-            padded_s[r] = top_ref[r]
-            padded_s[height + HALO + r] = bottom_ref[r]
+            partner = partner_ref[r].astype(f32)
+            other = other_ref[r].astype(f32)
+            padded_s[r] = jnp.where(even, other, partner).astype(bf16)
+            padded_s[height + HALO + r] = jnp.where(even, partner, other).astype(bf16)
 
         def body(r, carry):
             padded_s[r + HALO] = ring(normed_ref[r], right_ref[r], left_ref[r])
@@ -725,10 +772,13 @@
     )(*resident(back, gains, taps, up_weight, down_weight))
 
 
-def shift(value, axes, forward):
+def swap(facing, behind, axes):
     count = lax.axis_size(axes)
-    pairs = [(i, i + 1) if forward else (i + 1, i) for i in range(count - 1)]
-    return lax.ppermute(value, axes, pairs)
+
+    def pairs(start):
+        return [pair for i in range(start, count - 1, 2) for pair in ((i, i + 1), (i + 1, i))]
+
+    return lax.ppermute(facing, axes, pairs(0)), lax.ppermute(behind, axes, pairs(1))
 
 
 def on_device(
@@ -740,21 +790,18 @@
     table = bias_table.transpose(1, 0, 2)
     taps = conv_weight.transpose(1, 0, 2)
     down_weight = down_weight.transpose(0, 2, 1)
-    *edges, bias, padded = edge_attention(tokens, gains, qkv_weight, proj_weight, table)
-    left = shift(edges[3], columns, True)
-    right = shift(edges[2], columns, False)
+    *edges, facing, behind, bias, padded = edge_attention(tokens, gains, qkv_weight, proj_weight, table)
+    partner, other = swap(facing, behind, columns)
     after, normed = inner_attention(tokens, gains, padded, proj_weight, bias, edges)
-    around = lambda rows: jnp.concatenate([normed[rows], right[rows], left[rows]], axis=1)
-    height = tokens.shape[0]
-    top = shift(around(slice(height - HALO, height)), "row", True)
-    bottom = shift(around(slice(0, HALO)), "row", False)
+    left, right, facing, behind = turn(normed, partner, other)
+    partner, other = swap(facing, behind, "row")
     middle = middle_finish(after, normed, left, right, gains, taps, up_weight, down_weight)
     outgoing = outer_finish(
         after,
         middle,
         normed,
-        top,
-        bottom,
+        partner,
+        other,
         left,
         right,
         gains,

time: 104 us -> 99.7 us (0.959)
  starting transfers between devices: 13 us -> 8.67 us
  waiting for transfers between devices: 2.47 us -> 0.01 us
  blocking collectives: 53.6 us -> 56 us
    ppermute x4, starting transfers between devices: 13 us -> 8.67 us  [the longest x2 4.45 us: swap(): lax.ppermute(facing, axes, pairs(0))]
    ppermute x4, waiting for transfers between devices: 2.47 us -> 0.01 us  [the longest x2 0.01 us: swap(): lax.ppermute(behind, axes, pairs(1))]
    all_to_all x1, blocking collectives: 27.2 us -> 29.6 us  [on_device(): got = lax.all_to_all(outgoing, members, 0, 0, tiled=True)]
  transfers between devices with their start and end apart: 4 -> 4, of which waited for: 1 -> 0; matrix products, arithmetic and copies ran while one was open for 0% -> 0% of each run, Pallas kernels for 8% -> 8%
where the time goes in v5:
time: 99.7 us; the launch traced here: 99.5 us
  blocking collectives  56 us (56%)
  Pallas kernels  34.6 us (35%)
  starting transfers between devices  8.67 us (9%)
    all_to_all x1, blocking collectives, on_device(): got = lax.all_to_all(outgoing, members, 0, 0, tiled=True)  29.6 us
    all_to_all x1, blocking collectives, on_device(): back = lax.all_to_all(branch, members, 0, 0, tiled=True)  26.4 us
    pallas_call x1, Pallas kernels, second_finish(): pl.pallas_call(second_kernel, grid=(height // (2 * WS),), in_specs=[RESID...  11.3 us
    pallas_call x1, Pallas kernels, shuffled_attention(): pl.pallas_call(shuffled_kernel, in_specs=[RESIDENT] * 5, out_specs=RESIDE...  7.76 us
    pallas_call x1, Pallas kernels, outer_finish(): pl.pallas_call(outer_kernel, grid=(WS // rows,), in_specs=[RESIDENT] * 11...  4.58 us
    ppermute x2, starting transfers between devices, swap(): lax.ppermute(facing, axes, pairs(0))  4.45 us
    pallas_call x1, Pallas kernels, middle_finish(): pl.pallas_call(middle_kernel, grid=(inner // (2 * WS),), in_specs=[RESIDE...  4.36 us
    ppermute x2, starting transfers between devices, swap(): lax.ppermute(behind, axes, pairs(1))  4.22 us
  transfers between devices with their start and end apart: 4, of which 0 were waited for; matrix products, arithmetic and copies ran while one was open for 0% of the time, Pallas kernels for 8%

profile of v5, /device:TPU:1, one launch (start us, length us, event | category | flops | bytes accessed | tf_op | source)
XLA Modules:
  0.0 99.5 jit_solution(15249716053306659897)
XLA Ops:
  0.0 0.0 copy-start
  0.0 0.0 copy-start.2
  0.0 3.0 %edge_attention.1 = (f32[32,8,192]{2,1,0:T(8,128)S(1)}, f32[32,8,192]{2,1,0:T(8,128)S(1)}, bf16[32,8,192]{2,1,0:T(8,128)(2,1)S(1)}, bf16[32,8,192]{2,1,0:T(8,128...) custom-call(bf16[32,64,192]{2,1,0:T(8,128)(2,1)} %x_ref.1, ...), custom_call_target="tpu_custom_call" | custom-call | flops 500000000 | bytes 1048576 | tf_op jit(solution)/shard_map/edge_attention/pallas_call | solution.py:259
  3.1 1.5 %collective-permute-start = (bf16[32,8,192]{2,1,0:T(8,128)(2,1)S(1)}, bf16[32,8,192]{2,1,0:T(8,128)(2,1)S(1)}, u32[]{:S(2)}, u32[]{:S(2)}) collective-permute-start(bf16[32,8,192]{2,1,0:T(8,128)(2,1)S(1)} %get-tuple-element.27), channel_id=1, source_target_pairs={{0,1},{1,0},{2,3},{3,2},{4,5},{5,4},{6,7},{7,6},{8,9},{9,8},{10,11... | collective-permute-start | bytes 294920 | tf_op jit(solution)/shard_map/ppermute | solution.py:781
  4.5 3.6 %collective-permute-start.1 = (bf16[32,8,192]{2,1,0:T(8,128)(2,1)S(1)}, bf16[32,8,192]{2,1,0:T(8,128)(2,1)S(1)}, u32[]{:S(2)}, u32[]{:S(2)}) collective-permute-start(bf16[32,8,192]{2,1,0:T(8,128)(2,1)S(1)} %get-tuple-element.28), channel_id=1, source_target_pairs={{1,2},{2,1},{3,4},{4,3},{5,6},{6,5},{7,8},{8,7},{9,10},{10,9},{11,... | collective-permute-start | bytes 294920 | tf_op jit(solution)/shard_map/ppermute | solution.py:781
  8.1 0.0 copy-done
  8.1 0.0 copy-done.2
  8.1 0.0 copy-done.4
  8.1 3.4 %inner_attention.1 = (f32[32,64,192]{2,1,0:T(8,128)S(1)}, bf16[32,64,192]{2,1,0:T(8,128)(2,1)S(1)}) custom-call(bf16[32,64,192]{2,1,0:T(8,128)(2,1)S(1)} %copy-done, f32[3,2,192]{2,1,0:T(2,128)S(1)} %bitcast.7, bf16[192,768]{1,0:T(8,128)(2,1)S(1)} %get-tuple-element.19.pad_ref, bf16[2,192,192]{2,1,0:T(8,128)(2,1)S(1)} %copy-done.2, ...), custom_call_target="tpu_custom_call" | custom-call | flops 8000000000 | bytes 1048576 | tf_op jit(solution)/shard_map/inner_attention/pallas_call | solution.py:294
  11.6 0.0 copy-start.5
  11.6 0.0 copy-start.6
  11.6 0.0 copy-start.7
  11.6 0.0 collective-permute-done.partner_ref
  11.6 0.0 collective-permute-done.1.other_ref
  11.6 0.1 turn.1
  11.8 3.0 %collective-permute-start.2 = (bf16[3,80,192]{2,1,0:T(8,128)(2,1)S(1)}, bf16[3,80,192]{2,1,0:T(8,128)(2,1)S(1)}, u32[]{:S(2)}, u32[]{:S(2)}) collective-permute-start(bf16[3,80,192]{2,1,0:T(8,128)(2,1)S(1)} %get-tuple-element.31), channel_id=1, source_target_pairs={{0,16},{16,0},{32,48},{48,32},{64,80},{80,64},{96,112},{112,96},{1... | collective-permute-start | bytes 276488 | tf_op jit(solution)/shard_map/ppermute | solution.py:781
  14.8 0.7 collective-permute-start.3
  15.4 0.0 copy-done.5
  15.4 0.0 copy-done.6
  15.4 0.0 copy-done.7
  15.5 4.4 %middle_finish.1.middle_ref = bf16[16,64,192]{2,1,0:T(8,128)(2,1)S(1)} custom-call(f32[32,64,192]{2,1,0:T(8,128)S(1)} %get-tuple-element.25.sum_ref, bf16[32,64,192]{2,1,0:T(8,128)(2,1)S(1)} %get-tuple-element.26.normed_ref, bf16[32,8,192]{2,1,0:T(8,128)(2,1)S(1)} %get-tuple-element.29.left_ref, bf16[32,8,192]{2,1,0:T(8,128)(2,1)S(1)} %get-tuple-element.30.right_ref, ...), custom_call_target="tpu_custom_call" | custom-call | flops 8000000000 | bytes 1048576 | tf_op jit(solution)/shard_map/middle_finish/pallas_call | solution.py:515
  19.8 0.0 collective-permute-done.2.partner_ref
  19.8 0.0 collective-permute-done.3.other_ref
  19.8 4.6 %outer_finish.1 = bf16[128,24,128]{2,1,0:T(8,128)(2,1)S(1)} custom-call(f32[32,64,192]{2,1,0:T(8,128)S(1)} %get-tuple-element.25.sum_ref, bf16[16,64,192]{2,1,0:T(8,128)(2,1)S(1)} %middle_finish.1.middle_ref, bf16[32,64,192]{2,1,0:T(8,128)(2,1)S(1)} %get-tuple-element.26.normed_ref, bf16[3,80,192]{2,1,0:T(8,128)(2,1)S(1)} %collective-permute-done.2.partner_ref, ...), custom_call_target="tpu_custom_call" | custom-call | flops 8000000000 | bytes 1048576 | tf_op jit(solution)/shard_map/outer_finish/pallas_call | solution.py:646
  24.4 0.0 copy-start.1
  24.4 0.0 copy-start.3
  24.4 29.6 %all_to_all.10.got_ref = bf16[128,24,128]{2,1,0:T(8,128)(2,1)S(1)} all-to-all(bf16[128,24,128]{2,1,0:T(8,128)(2,1)S(1)} %outer_finish.1), channel_id=1, replica_groups=mesh['row'=8,'block'=8,'core'=2] {'row','block','core'}, dimensions={0} | all-to-all | bytes 1572864 | tf_op jit(solution)/shard_map/all_to_all | solution.py:813
  54.1 0.0 copy-done.1
  54.1 0.0 copy-done.3
  54.1 7.8 %shuffled_attention.1 = bf16[128,40,128]{2,1,0:T(8,128)(2,1)S(1)} custom-call(bf16[128,24,128]{2,1,0:T(8,128)(2,1)S(1)} %all_to_all.10.got_ref, f32[3,2,192]{2,1,0:T(2,128)S(1)} %bitcast.10, bf16[2,192,576]{2,1,0:T(8,128)(2,1)S(1)} %copy-done.1, bf16[2,192,192]{2,1,0:T(8,128)(2,1)S(1)} %copy-done.2, f32[6,2,225]{2,1,0:T(2,128)S(1)} %bitcast.5), custom_call_target="tpu_custom_call" | custom-call | flops 10000000000 | bytes 1048576 | tf_op jit(solution)/shard_map/shuffled_attention/pallas_call | solution.py:409
  61.8 26.4 %all_to_all.11.back_ref = bf16[128,40,128]{2,1,0:T(8,128)(2,1)S(1)} all-to-all(bf16[128,40,128]{2,1,0:T(8,128)(2,1)S(1)} %shuffled_attention.1), channel_id=1, replica_groups=mesh['row'=8,'block'=8,'core'=2] {'row','block','core'}, dimensions={0} | all-to-all | bytes 2621440 | tf_op jit(solution)/shard_map/all_to_all | solution.py:815
  88.2 11.3 %second_finish.1 = bf16[32,64,192]{2,1,0:T(8,128)(2,1)} custom-call(bf16[128,40,128]{2,1,0:T(8,128)(2,1)S(1)} %all_to_all.11.back_ref, f32[3,2,192]{2,1,0:T(2,128)S(1)} %bitcast.11, f32[49,2,192]{2,1,0:T(2,128)S(1)} %bitcast.17, bf16[2,192,768]{2,1,0:T(8,128)(2,1)S(1)} %copy-done.5, bf16[2,192,768]{2,1,0:T(8,128)(2,1)S(1)} %bitcast.14), custom_call_target="tpu_custom_call" | custom-call | flops 10000000000 | bytes 1048576 | tf_op jit(solution)/shard_map/second_finish/pallas_call | solution.py:754
  (1 shorter events, 0.0 us)
Async XLA Ops:
  0.0 8.1 %copy-start = (bf16[32,64,192]{2,1,0:T(8,128)(2,1)S(1)}, bf16[32,64,192]{2,1,0:T(8,128)(2,1)}, u32[]{:S(2)}) copy-start(bf16[32,64,192]{2,1,0:T(8,128)(2,1)} %x_ref.1) | copy-start | bytes 2359300
  0.0 8.1 %copy-start.2 = (bf16[2,192,192]{2,1,0:T(8,128)(2,1)S(1)}, bf16[2,192,192]{2,1,0:T(8,128)(2,1)}, u32[]{:S(2)}) copy-start(bf16[2,192,192]{2,1,0:T(8,128)(2,1)} %proj_ref.5) | copy-start | bytes 442372
  0.0 8.1 %copy-start.4 = (f32[2,3,192]{2,0,1:T(2,128)S(1)}, f32[2,3,192]{2,0,1:T(2,128)}, u32[]{:S(2)}) copy-start(f32[2,3,192]{2,0,1:T(2,128)} %param.9) | copy-start | bytes 13828
  3.1 8.5 %collective-permute-start = (bf16[32,8,192]{2,1,0:T(8,128)(2,1)S(1)}, bf16[32,8,192]{2,1,0:T(8,128)(2,1)S(1)}, u32[]{:S(2)}, u32[]{:S(2)}) collective-permute-start(bf16[32,8,192]{2,1,0:T(8,128)(2,1)S(1)} %get-tuple-element.27), channel_id=1, source_target_pairs={{0,1},{1,0},{2,3},{3,2},{4,5},{5,4},{6,7},{7,6},{8,9},{9,8},{10,11... | collective-permute-start | bytes 294920 | tf_op jit(solution)/shard_map/ppermute | solution.py:781
  4.5 7.1 %collective-permute-start.1 = (bf16[32,8,192]{2,1,0:T(8,128)(2,1)S(1)}, bf16[32,8,192]{2,1,0:T(8,128)(2,1)S(1)}, u32[]{:S(2)}, u32[]{:S(2)}) collective-permute-start(bf16[32,8,192]{2,1,0:T(8,128)(2,1)S(1)} %get-tuple-element.28), channel_id=1, source_target_pairs={{1,2},{2,1},{3,4},{4,3},{5,6},{6,5},{7,8},{8,7},{9,10},{10,9},{11,... | collective-permute-start | bytes 294920 | tf_op jit(solution)/shard_map/ppermute | solution.py:781
  11.6 3.9 %copy-start.5 = (bf16[2,192,768]{2,1,0:T(8,128)(2,1)S(1)}, bf16[2,192,768]{2,1,0:T(8,128)(2,1)}, u32[]{:S(2)}) copy-start(bf16[2,192,768]{2,1,0:T(8,128)(2,1)} %up_ref.5) | copy-start | bytes 1769476
  11.6 3.9 %copy-start.6 = (bf16[2,768,192]{1,2,0:T(8,128)(2,1)S(1)}, bf16[2,768,192]{1,2,0:T(8,128)(2,1)}, u32[]{:S(2)}) copy-start(bf16[2,768,192]{1,2,0:T(8,128)(2,1)} %param.15) | copy-start | bytes 1769476
  11.6 3.9 %copy-start.7 = (f32[2,49,192]{2,0,1:T(2,128)S(1)}, f32[2,49,192]{2,0,1:T(2,128)}, u32[]{:S(2)}) copy-start(f32[2,49,192]{2,0,1:T(2,128)} %param.13) | copy-start | bytes 225796
  11.8 8.1 %collective-permute-start.2 = (bf16[3,80,192]{2,1,0:T(8,128)(2,1)S(1)}, bf16[3,80,192]{2,1,0:T(8,128)(2,1)S(1)}, u32[]{:S(2)}, u32[]{:S(2)}) collective-permute-start(bf16[3,80,192]{2,1,0:T(8,128)(2,1)S(1)} %get-tuple-element.31), channel_id=1, source_target_pairs={{0,16},{16,0},{32,48},{48,32},{64,80},{80,64},{96,112},{112,96},{1... | collective-permute-start | bytes 276488 | tf_op jit(solution)/shard_map/ppermute | solution.py:781
  14.8 5.1 %collective-permute-start.3 = (bf16[3,80,192]{2,1,0:T(8,128)(2,1)S(1)}, bf16[3,80,192]{2,1,0:T(8,128)(2,1)S(1)}, u32[]{:S(2)}, u32[]{:S(2)}) collective-permute-start(bf16[3,80,192]{2,1,0:T(8,128)(2,1)S(1)} %get-tuple-element.32), channel_id=1, source_target_pairs={{16,32},{32,16},{48,64},{64,48},{80,96},{96,80},{17,33},{33,17},{4... | collective-permute-start | bytes 276488 | tf_op jit(solution)/shard_map/ppermute | solution.py:781
  24.4 29.7 %copy-start.1 = (bf16[2,192,576]{2,1,0:T(8,128)(2,1)S(1)}, bf16[2,192,576]{2,1,0:T(8,128)(2,1)}, u32[]{:S(2)}) copy-start(bf16[2,192,576]{2,1,0:T(8,128)(2,1)} %qkv_ref.3) | copy-start | bytes 1327108
  24.4 29.6 %copy-start.3 = (f32[2,6,225]{2,0,1:T(2,128)S(1)}, f32[2,6,225]{2,0,1:T(2,128)}, u32[]{:S(2)}) copy-start(f32[2,6,225]{2,0,1:T(2,128)} %param.12) | copy-start | bytes 32404

commit v6 on v5

--- a/solution.py
+++ b/solution.py
@@ -16,7 +16,7 @@
 PAD = 256
 LANES = 128
 HALO = KS // 2
-TOGETHER = 16
+TOGETHER = 32
 WINDOW_ROWS = AREA + 4
 PIECE_ROWS = 24
 PIECE_STRIDE = PIECE_ROWS + 4
@@ -333,7 +333,7 @@
             window_s[1, place, :] = upper
         return carry
 
-    lax.fori_loop(0, WS, gather, 0)
+    lax.fori_loop(0, WS, gather, 0, unroll=2)
     masks = attention_masks()
 
     def windows(c, carry):
@@ -401,7 +401,7 @@
         return carry
 
     piece_s[...] = jnp.zeros_like(piece_s)
-    lax.fori_loop(0, WS, scatter, 0)
+    lax.fori_loop(0, WS, scatter, 0, unroll=2)
 
 
 def shuffled_attention(got, gains, qkv_weight, proj_weight, table):
@@ -736,7 +736,7 @@
             padded_s[target] = normed[repeats * RING :]
             return carry
 
-        lax.fori_loop(0, WS, body, 0)
+        lax.fori_loop(0, WS, body, 0, unroll=2)
 
     def row(j, carry):
         r = step * rows + j

time: 99.7 us -> 98.1 us (0.984)
  Pallas kernels: 34.6 us -> 33 us
    pallas_call x1, Pallas kernels: 7.76 us -> 6.41 us  [shuffled_attention(): pl.pallas_call(shuffled_kernel, in_specs=[RESIDENT] * 5, out_specs=RESIDE...]
where the time goes in v6:
time: 98.1 us; the launch traced here: 97.9 us
  blocking collectives  56 us (57%)
  Pallas kernels  33 us (34%)
  starting transfers between devices  8.67 us (9%)
    all_to_all x1, blocking collectives, on_device(): got = lax.all_to_all(outgoing, members, 0, 0, tiled=True)  29.6 us
    all_to_all x1, blocking collectives, on_device(): back = lax.all_to_all(branch, members, 0, 0, tiled=True)  26.4 us
    pallas_call x1, Pallas kernels, second_finish(): pl.pallas_call(second_kernel, grid=(height // (2 * WS),), in_specs=[RESID...  11.1 us
    pallas_call x1, Pallas kernels, shuffled_attention(): pl.pallas_call(shuffled_kernel, in_specs=[RESIDENT] * 5, out_specs=RESIDE...  6.41 us
    pallas_call x1, Pallas kernels, outer_finish(): pl.pallas_call(outer_kernel, grid=(WS // rows,), in_specs=[RESIDENT] * 11...  4.58 us
    ppermute x2, starting transfers between devices, swap(): lax.ppermute(facing, axes, pairs(0))  4.45 us
    pallas_call x1, Pallas kernels, middle_finish(): pl.pallas_call(middle_kernel, grid=(inner // (2 * WS),), in_specs=[RESIDE...  4.36 us
    ppermute x2, starting transfers between devices, swap(): lax.ppermute(behind, axes, pairs(1))  4.22 us
  transfers between devices with their start and end apart: 4, of which 0 were waited for; matrix products, arithmetic and copies ran while one was open for 0% of the time, Pallas kernels for 8%

profile of v6, /device:TPU:1, one launch (start us, length us, event | category | flops | bytes accessed | tf_op | source)
XLA Modules:
  0.0 97.9 jit_solution(9493526091463793242)
XLA Ops:
  0.0 0.0 copy-start
  0.0 0.0 copy-start.2
  0.0 3.0 %edge_attention.1 = (f32[32,8,192]{2,1,0:T(8,128)S(1)}, f32[32,8,192]{2,1,0:T(8,128)S(1)}, bf16[32,8,192]{2,1,0:T(8,128)(2,1)S(1)}, bf16[32,8,192]{2,1,0:T(8,128...) custom-call(bf16[32,64,192]{2,1,0:T(8,128)(2,1)} %x_ref.1, ...), custom_call_target="tpu_custom_call" | custom-call | flops 500000000 | bytes 1048576 | tf_op jit(solution)/shard_map/edge_attention/pallas_call | solution.py:259
  3.1 1.5 %collective-permute-start = (bf16[32,8,192]{2,1,0:T(8,128)(2,1)S(1)}, bf16[32,8,192]{2,1,0:T(8,128)(2,1)S(1)}, u32[]{:S(2)}, u32[]{:S(2)}) collective-permute-start(bf16[32,8,192]{2,1,0:T(8,128)(2,1)S(1)} %get-tuple-element.27), channel_id=1, source_target_pairs={{0,1},{1,0},{2,3},{3,2},{4,5},{5,4},{6,7},{7,6},{8,9},{9,8},{10,11... | collective-permute-start | bytes 294920 | tf_op jit(solution)/shard_map/ppermute | solution.py:781
  4.5 3.6 %collective-permute-start.1 = (bf16[32,8,192]{2,1,0:T(8,128)(2,1)S(1)}, bf16[32,8,192]{2,1,0:T(8,128)(2,1)S(1)}, u32[]{:S(2)}, u32[]{:S(2)}) collective-permute-start(bf16[32,8,192]{2,1,0:T(8,128)(2,1)S(1)} %get-tuple-element.28), channel_id=1, source_target_pairs={{1,2},{2,1},{3,4},{4,3},{5,6},{6,5},{7,8},{8,7},{9,10},{10,9},{11,... | collective-permute-start | bytes 294920 | tf_op jit(solution)/shard_map/ppermute | solution.py:781
  8.1 0.0 copy-done
  8.1 0.0 copy-done.2
  8.1 0.0 copy-done.4
  8.1 3.4 %inner_attention.1 = (f32[32,64,192]{2,1,0:T(8,128)S(1)}, bf16[32,64,192]{2,1,0:T(8,128)(2,1)S(1)}) custom-call(bf16[32,64,192]{2,1,0:T(8,128)(2,1)S(1)} %copy-done, f32[3,2,192]{2,1,0:T(2,128)S(1)} %bitcast.7, bf16[192,768]{1,0:T(8,128)(2,1)S(1)} %get-tuple-element.19.pad_ref, bf16[2,192,192]{2,1,0:T(8,128)(2,1)S(1)} %copy-done.2, ...), custom_call_target="tpu_custom_call" | custom-call | flops 8000000000 | bytes 1048576 | tf_op jit(solution)/shard_map/inner_attention/pallas_call | solution.py:294
  11.6 0.0 copy-start.5
  11.6 0.0 copy-start.6
  11.6 0.0 copy-start.7
  11.6 0.0 collective-permute-done.partner_ref
  11.6 0.0 collective-permute-done.1.other_ref
  11.6 0.1 turn.1
  11.8 3.0 %collective-permute-start.2 = (bf16[3,80,192]{2,1,0:T(8,128)(2,1)S(1)}, bf16[3,80,192]{2,1,0:T(8,128)(2,1)S(1)}, u32[]{:S(2)}, u32[]{:S(2)}) collective-permute-start(bf16[3,80,192]{2,1,0:T(8,128)(2,1)S(1)} %get-tuple-element.31), channel_id=1, source_target_pairs={{0,16},{16,0},{32,48},{48,32},{64,80},{80,64},{96,112},{112,96},{1... | collective-permute-start | bytes 276488 | tf_op jit(solution)/shard_map/ppermute | solution.py:781
  14.8 0.7 collective-permute-start.3
  15.4 0.0 copy-done.5
  15.4 0.0 copy-done.6
  15.4 0.0 copy-done.7
  15.5 4.4 %middle_finish.1.middle_ref = bf16[16,64,192]{2,1,0:T(8,128)(2,1)S(1)} custom-call(f32[32,64,192]{2,1,0:T(8,128)S(1)} %get-tuple-element.25.sum_ref, bf16[32,64,192]{2,1,0:T(8,128)(2,1)S(1)} %get-tuple-element.26.normed_ref, bf16[32,8,192]{2,1,0:T(8,128)(2,1)S(1)} %get-tuple-element.29.left_ref, bf16[32,8,192]{2,1,0:T(8,128)(2,1)S(1)} %get-tuple-element.30.right_ref, ...), custom_call_target="tpu_custom_call" | custom-call | flops 8000000000 | bytes 1048576 | tf_op jit(solution)/shard_map/middle_finish/pallas_call | solution.py:515
  19.8 0.0 collective-permute-done.2.partner_ref
  19.8 0.0 collective-permute-done.3.other_ref
  19.8 4.6 %outer_finish.1 = bf16[128,24,128]{2,1,0:T(8,128)(2,1)S(1)} custom-call(f32[32,64,192]{2,1,0:T(8,128)S(1)} %get-tuple-element.25.sum_ref, bf16[16,64,192]{2,1,0:T(8,128)(2,1)S(1)} %middle_finish.1.middle_ref, bf16[32,64,192]{2,1,0:T(8,128)(2,1)S(1)} %get-tuple-element.26.normed_ref, bf16[3,80,192]{2,1,0:T(8,128)(2,1)S(1)} %collective-permute-done.2.partner_ref, ...), custom_call_target="tpu_custom_call" | custom-call | flops 8000000000 | bytes 1048576 | tf_op jit(solution)/shard_map/outer_finish/pallas_call | solution.py:646
  24.4 0.0 copy-start.1
  24.4 0.0 copy-start.3
  24.4 29.6 %all_to_all.10.got_ref = bf16[128,24,128]{2,1,0:T(8,128)(2,1)S(1)} all-to-all(bf16[128,24,128]{2,1,0:T(8,128)(2,1)S(1)} %outer_finish.1), channel_id=1, replica_groups=mesh['row'=8,'block'=8,'core'=2] {'row','block','core'}, dimensions={0} | all-to-all | bytes 1572864 | tf_op jit(solution)/shard_map/all_to_all | solution.py:813
  54.1 0.0 copy-done.1
  54.1 0.0 copy-done.3
  54.1 6.4 %shuffled_attention.1 = bf16[128,40,128]{2,1,0:T(8,128)(2,1)S(1)} custom-call(bf16[128,24,128]{2,1,0:T(8,128)(2,1)S(1)} %all_to_all.10.got_ref, f32[3,2,192]{2,1,0:T(2,128)S(1)} %bitcast.10, bf16[2,192,576]{2,1,0:T(8,128)(2,1)S(1)} %copy-done.1, bf16[2,192,192]{2,1,0:T(8,128)(2,1)S(1)} %copy-done.2, f32[6,2,225]{2,1,0:T(2,128)S(1)} %bitcast.5), custom_call_target="tpu_custom_call" | custom-call | flops 10000000000 | bytes 1048576 | tf_op jit(solution)/shard_map/shuffled_attention/pallas_call | solution.py:409
  60.5 26.4 %all_to_all.11.back_ref = bf16[128,40,128]{2,1,0:T(8,128)(2,1)S(1)} all-to-all(bf16[128,40,128]{2,1,0:T(8,128)(2,1)S(1)} %shuffled_attention.1), channel_id=1, replica_groups=mesh['row'=8,'block'=8,'core'=2] {'row','block','core'}, dimensions={0} | all-to-all | bytes 2621440 | tf_op jit(solution)/shard_map/all_to_all | solution.py:815
  86.9 11.1 %second_finish.1 = bf16[32,64,192]{2,1,0:T(8,128)(2,1)} custom-call(bf16[128,40,128]{2,1,0:T(8,128)(2,1)S(1)} %all_to_all.11.back_ref, f32[3,2,192]{2,1,0:T(2,128)S(1)} %bitcast.11, f32[49,2,192]{2,1,0:T(2,128)S(1)} %bitcast.17, bf16[2,192,768]{2,1,0:T(8,128)(2,1)S(1)} %copy-done.5, bf16[2,192,768]{2,1,0:T(8,128)(2,1)S(1)} %bitcast.14), custom_call_target="tpu_custom_call" | custom-call | flops 10000000000 | bytes 1048576 | tf_op jit(solution)/shard_map/second_finish/pallas_call | solution.py:754
  (1 shorter events, 0.0 us)
Async XLA Ops:
  0.0 8.1 %copy-start = (bf16[32,64,192]{2,1,0:T(8,128)(2,1)S(1)}, bf16[32,64,192]{2,1,0:T(8,128)(2,1)}, u32[]{:S(2)}) copy-start(bf16[32,64,192]{2,1,0:T(8,128)(2,1)} %x_ref.1) | copy-start | bytes 2359300
  0.0 8.1 %copy-start.2 = (bf16[2,192,192]{2,1,0:T(8,128)(2,1)S(1)}, bf16[2,192,192]{2,1,0:T(8,128)(2,1)}, u32[]{:S(2)}) copy-start(bf16[2,192,192]{2,1,0:T(8,128)(2,1)} %proj_ref.5) | copy-start | bytes 442372
  0.0 8.1 %copy-start.4 = (f32[2,3,192]{2,0,1:T(2,128)S(1)}, f32[2,3,192]{2,0,1:T(2,128)}, u32[]{:S(2)}) copy-start(f32[2,3,192]{2,0,1:T(2,128)} %param.9) | copy-start | bytes 13828
  3.1 8.5 %collective-permute-start = (bf16[32,8,192]{2,1,0:T(8,128)(2,1)S(1)}, bf16[32,8,192]{2,1,0:T(8,128)(2,1)S(1)}, u32[]{:S(2)}, u32[]{:S(2)}) collective-permute-start(bf16[32,8,192]{2,1,0:T(8,128)(2,1)S(1)} %get-tuple-element.27), channel_id=1, source_target_pairs={{0,1},{1,0},{2,3},{3,2},{4,5},{5,4},{6,7},{7,6},{8,9},{9,8},{10,11... | collective-permute-start | bytes 294920 | tf_op jit(solution)/shard_map/ppermute | solution.py:781
  4.5 7.1 %collective-permute-start.1 = (bf16[32,8,192]{2,1,0:T(8,128)(2,1)S(1)}, bf16[32,8,192]{2,1,0:T(8,128)(2,1)S(1)}, u32[]{:S(2)}, u32[]{:S(2)}) collective-permute-start(bf16[32,8,192]{2,1,0:T(8,128)(2,1)S(1)} %get-tuple-element.28), channel_id=1, source_target_pairs={{1,2},{2,1},{3,4},{4,3},{5,6},{6,5},{7,8},{8,7},{9,10},{10,9},{11,... | collective-permute-start | bytes 294920 | tf_op jit(solution)/shard_map/ppermute | solution.py:781
  11.6 3.9 %copy-start.5 = (bf16[2,192,768]{2,1,0:T(8,128)(2,1)S(1)}, bf16[2,192,768]{2,1,0:T(8,128)(2,1)}, u32[]{:S(2)}) copy-start(bf16[2,192,768]{2,1,0:T(8,128)(2,1)} %up_ref.5) | copy-start | bytes 1769476
  11.6 3.9 %copy-start.6 = (bf16[2,768,192]{1,2,0:T(8,128)(2,1)S(1)}, bf16[2,768,192]{1,2,0:T(8,128)(2,1)}, u32[]{:S(2)}) copy-start(bf16[2,768,192]{1,2,0:T(8,128)(2,1)} %param.15) | copy-start | bytes 1769476
  11.6 3.9 %copy-start.7 = (f32[2,49,192]{2,0,1:T(2,128)S(1)}, f32[2,49,192]{2,0,1:T(2,128)}, u32[]{:S(2)}) copy-start(f32[2,49,192]{2,0,1:T(2,128)} %param.13) | copy-start | bytes 225796
  11.8 8.1 %collective-permute-start.2 = (bf16[3,80,192]{2,1,0:T(8,128)(2,1)S(1)}, bf16[3,80,192]{2,1,0:T(8,128)(2,1)S(1)}, u32[]{:S(2)}, u32[]{:S(2)}) collective-permute-start(bf16[3,80,192]{2,1,0:T(8,128)(2,1)S(1)} %get-tuple-element.31), channel_id=1, source_target_pairs={{0,16},{16,0},{32,48},{48,32},{64,80},{80,64},{96,112},{112,96},{1... | collective-permute-start | bytes 276488 | tf_op jit(solution)/shard_map/ppermute | solution.py:781
  14.8 5.1 %collective-permute-start.3 = (bf16[3,80,192]{2,1,0:T(8,128)(2,1)S(1)}, bf16[3,80,192]{2,1,0:T(8,128)(2,1)S(1)}, u32[]{:S(2)}, u32[]{:S(2)}) collective-permute-start(bf16[3,80,192]{2,1,0:T(8,128)(2,1)S(1)} %get-tuple-element.32), channel_id=1, source_target_pairs={{16,32},{32,16},{48,64},{64,48},{80,96},{96,80},{17,33},{33,17},{4... | collective-permute-start | bytes 276488 | tf_op jit(solution)/shard_map/ppermute | solution.py:781
  24.4 29.7 %copy-start.1 = (bf16[2,192,576]{2,1,0:T(8,128)(2,1)S(1)}, bf16[2,192,576]{2,1,0:T(8,128)(2,1)}, u32[]{:S(2)}) copy-start(bf16[2,192,576]{2,1,0:T(8,128)(2,1)} %qkv_ref.3) | copy-start | bytes 1327108
  24.4 29.6 %copy-start.3 = (f32[2,6,225]{2,0,1:T(2,128)S(1)}, f32[2,6,225]{2,0,1:T(2,128)}, u32[]{:S(2)}) copy-start(f32[2,6,225]{2,0,1:T(2,128)} %param.12) | copy-start | bytes 32404

commit v7 on v6

--- a/solution.py
+++ b/solution.py
@@ -333,7 +333,7 @@
             window_s[1, place, :] = upper
         return carry
 
-    lax.fori_loop(0, WS, gather, 0, unroll=2)
+    lax.fori_loop(0, WS, gather, 0, unroll=4)
     masks = attention_masks()
 
     def windows(c, carry):
@@ -401,7 +401,7 @@
         return carry
 
     piece_s[...] = jnp.zeros_like(piece_s)
-    lax.fori_loop(0, WS, scatter, 0, unroll=2)
+    lax.fori_loop(0, WS, scatter, 0, unroll=4)
 
 
 def shuffled_attention(got, gains, qkv_weight, proj_weight, table):

time: 98.1 us -> 97.8 us (level)
  no operation moved by 1% of the time
where the time goes in v7:
time: 97.8 us; the launch traced here: 97.6 us
  blocking collectives  56 us (57%)
  Pallas kernels  32.7 us (33%)
  starting transfers between devices  8.67 us (9%)
    all_to_all x1, blocking collectives, on_device(): got = lax.all_to_all(outgoing, members, 0, 0, tiled=True)  29.6 us
    all_to_all x1, blocking collectives, on_device(): back = lax.all_to_all(branch, members, 0, 0, tiled=True)  26.4 us
    pallas_call x1, Pallas kernels, second_finish(): pl.pallas_call(second_kernel, grid=(height // (2 * WS),), in_specs=[RESID...  11 us
    pallas_call x1, Pallas kernels, shuffled_attention(): pl.pallas_call(shuffled_kernel, in_specs=[RESIDENT] * 5, out_specs=RESIDE...  6.09 us
    pallas_call x1, Pallas kernels, outer_finish(): pl.pallas_call(outer_kernel, grid=(WS // rows,), in_specs=[RESIDENT] * 11...  4.58 us
    ppermute x2, starting transfers between devices, swap(): lax.ppermute(facing, axes, pairs(0))  4.45 us
    pallas_call x1, Pallas kernels, middle_finish(): pl.pallas_call(middle_kernel, grid=(inner // (2 * WS),), in_specs=[RESIDE...  4.36 us
    ppermute x2, starting transfers between devices, swap(): lax.ppermute(behind, axes, pairs(1))  4.22 us
  transfers between devices with their start and end apart: 4, of which 0 were waited for; matrix products, arithmetic and copies ran while one was open for 0% of the time, Pallas kernels for 8%

profile of v7, /device:TPU:1, one launch (start us, length us, event | category | flops | bytes accessed | tf_op | source)
XLA Modules:
  0.0 97.6 jit_solution(2385600553746808300)
XLA Ops:
  0.0 0.0 copy-start
  0.0 0.0 copy-start.2
  0.0 3.0 %edge_attention.1 = (f32[32,8,192]{2,1,0:T(8,128)S(1)}, f32[32,8,192]{2,1,0:T(8,128)S(1)}, bf16[32,8,192]{2,1,0:T(8,128)(2,1)S(1)}, bf16[32,8,192]{2,1,0:T(8,128...) custom-call(bf16[32,64,192]{2,1,0:T(8,128)(2,1)} %x_ref.1, ...), custom_call_target="tpu_custom_call" | custom-call | flops 500000000 | bytes 1048576 | tf_op jit(solution)/shard_map/edge_attention/pallas_call | solution.py:259
  3.1 1.5 %collective-permute-start = (bf16[32,8,192]{2,1,0:T(8,128)(2,1)S(1)}, bf16[32,8,192]{2,1,0:T(8,128)(2,1)S(1)}, u32[]{:S(2)}, u32[]{:S(2)}) collective-permute-start(bf16[32,8,192]{2,1,0:T(8,128)(2,1)S(1)} %get-tuple-element.27), channel_id=1, source_target_pairs={{0,1},{1,0},{2,3},{3,2},{4,5},{5,4},{6,7},{7,6},{8,9},{9,8},{10,11... | collective-permute-start | bytes 294920 | tf_op jit(solution)/shard_map/ppermute | solution.py:781
  4.5 3.6 %collective-permute-start.1 = (bf16[32,8,192]{2,1,0:T(8,128)(2,1)S(1)}, bf16[32,8,192]{2,1,0:T(8,128)(2,1)S(1)}, u32[]{:S(2)}, u32[]{:S(2)}) collective-permute-start(bf16[32,8,192]{2,1,0:T(8,128)(2,1)S(1)} %get-tuple-element.28), channel_id=1, source_target_pairs={{1,2},{2,1},{3,4},{4,3},{5,6},{6,5},{7,8},{8,7},{9,10},{10,9},{11,... | collective-permute-start | bytes 294920 | tf_op jit(solution)/shard_map/ppermute | solution.py:781
  8.1 0.0 copy-done
  8.1 0.0 copy-done.2
  8.1 0.0 copy-done.4
  8.1 3.4 %inner_attention.1 = (f32[32,64,192]{2,1,0:T(8,128)S(1)}, bf16[32,64,192]{2,1,0:T(8,128)(2,1)S(1)}) custom-call(bf16[32,64,192]{2,1,0:T(8,128)(2,1)S(1)} %copy-done, f32[3,2,192]{2,1,0:T(2,128)S(1)} %bitcast.7, bf16[192,768]{1,0:T(8,128)(2,1)S(1)} %get-tuple-element.19.pad_ref, bf16[2,192,192]{2,1,0:T(8,128)(2,1)S(1)} %copy-done.2, ...), custom_call_target="tpu_custom_call" | custom-call | flops 8000000000 | bytes 1048576 | tf_op jit(solution)/shard_map/inner_attention/pallas_call | solution.py:294
  11.6 0.0 copy-start.5
  11.6 0.0 copy-start.6
  11.6 0.0 copy-start.7
  11.6 0.0 collective-permute-done.partner_ref
  11.6 0.0 collective-permute-done.1.other_ref
  11.6 0.1 turn.1
  11.8 3.0 %collective-permute-start.2 = (bf16[3,80,192]{2,1,0:T(8,128)(2,1)S(1)}, bf16[3,80,192]{2,1,0:T(8,128)(2,1)S(1)}, u32[]{:S(2)}, u32[]{:S(2)}) collective-permute-start(bf16[3,80,192]{2,1,0:T(8,128)(2,1)S(1)} %get-tuple-element.31), channel_id=1, source_target_pairs={{0,16},{16,0},{32,48},{48,32},{64,80},{80,64},{96,112},{112,96},{1... | collective-permute-start | bytes 276488 | tf_op jit(solution)/shard_map/ppermute | solution.py:781
  14.8 0.7 collective-permute-start.3
  15.4 0.0 copy-done.5
  15.4 0.0 copy-done.6
  15.4 0.0 copy-done.7
  15.5 4.4 %middle_finish.1.middle_ref = bf16[16,64,192]{2,1,0:T(8,128)(2,1)S(1)} custom-call(f32[32,64,192]{2,1,0:T(8,128)S(1)} %get-tuple-element.25.sum_ref, bf16[32,64,192]{2,1,0:T(8,128)(2,1)S(1)} %get-tuple-element.26.normed_ref, bf16[32,8,192]{2,1,0:T(8,128)(2,1)S(1)} %get-tuple-element.29.left_ref, bf16[32,8,192]{2,1,0:T(8,128)(2,1)S(1)} %get-tuple-element.30.right_ref, ...), custom_call_target="tpu_custom_call" | custom-call | flops 8000000000 | bytes 1048576 | tf_op jit(solution)/shard_map/middle_finish/pallas_call | solution.py:515
  19.8 0.0 collective-permute-done.2.partner_ref
  19.8 0.0 collective-permute-done.3.other_ref
  19.8 4.6 %outer_finish.1 = bf16[128,24,128]{2,1,0:T(8,128)(2,1)S(1)} custom-call(f32[32,64,192]{2,1,0:T(8,128)S(1)} %get-tuple-element.25.sum_ref, bf16[16,64,192]{2,1,0:T(8,128)(2,1)S(1)} %middle_finish.1.middle_ref, bf16[32,64,192]{2,1,0:T(8,128)(2,1)S(1)} %get-tuple-element.26.normed_ref, bf16[3,80,192]{2,1,0:T(8,128)(2,1)S(1)} %collective-permute-done.2.partner_ref, ...), custom_call_target="tpu_custom_call" | custom-call | flops 8000000000 | bytes 1048576 | tf_op jit(solution)/shard_map/outer_finish/pallas_call | solution.py:646
  24.4 0.0 copy-start.1
  24.4 0.0 copy-start.3
  24.4 29.6 %all_to_all.10.got_ref = bf16[128,24,128]{2,1,0:T(8,128)(2,1)S(1)} all-to-all(bf16[128,24,128]{2,1,0:T(8,128)(2,1)S(1)} %outer_finish.1), channel_id=1, replica_groups=mesh['row'=8,'block'=8,'core'=2] {'row','block','core'}, dimensions={0} | all-to-all | bytes 1572864 | tf_op jit(solution)/shard_map/all_to_all | solution.py:813
  54.1 0.0 copy-done.1
  54.1 0.0 copy-done.3
  54.1 6.1 %shuffled_attention.1 = bf16[128,40,128]{2,1,0:T(8,128)(2,1)S(1)} custom-call(bf16[128,24,128]{2,1,0:T(8,128)(2,1)S(1)} %all_to_all.10.got_ref, f32[3,2,192]{2,1,0:T(2,128)S(1)} %bitcast.10, bf16[2,192,576]{2,1,0:T(8,128)(2,1)S(1)} %copy-done.1, bf16[2,192,192]{2,1,0:T(8,128)(2,1)S(1)} %copy-done.2, f32[6,2,225]{2,1,0:T(2,128)S(1)} %bitcast.5), custom_call_target="tpu_custom_call" | custom-call | flops 10000000000 | bytes 1048576 | tf_op jit(solution)/shard_map/shuffled_attention/pallas_call | solution.py:409
  60.2 26.4 %all_to_all.11.back_ref = bf16[128,40,128]{2,1,0:T(8,128)(2,1)S(1)} all-to-all(bf16[128,40,128]{2,1,0:T(8,128)(2,1)S(1)} %shuffled_attention.1), channel_id=1, replica_groups=mesh['row'=8,'block'=8,'core'=2] {'row','block','core'}, dimensions={0} | all-to-all | bytes 2621440 | tf_op jit(solution)/shard_map/all_to_all | solution.py:815
  86.6 11.0 %second_finish.1 = bf16[32,64,192]{2,1,0:T(8,128)(2,1)} custom-call(bf16[128,40,128]{2,1,0:T(8,128)(2,1)S(1)} %all_to_all.11.back_ref, f32[3,2,192]{2,1,0:T(2,128)S(1)} %bitcast.11, f32[49,2,192]{2,1,0:T(2,128)S(1)} %bitcast.17, bf16[2,192,768]{2,1,0:T(8,128)(2,1)S(1)} %copy-done.5, bf16[2,192,768]{2,1,0:T(8,128)(2,1)S(1)} %bitcast.14), custom_call_target="tpu_custom_call" | custom-call | flops 10000000000 | bytes 1048576 | tf_op jit(solution)/shard_map/second_finish/pallas_call | solution.py:754
  (1 shorter events, 0.0 us)
Async XLA Ops:
  0.0 8.1 %copy-start = (bf16[32,64,192]{2,1,0:T(8,128)(2,1)S(1)}, bf16[32,64,192]{2,1,0:T(8,128)(2,1)}, u32[]{:S(2)}) copy-start(bf16[32,64,192]{2,1,0:T(8,128)(2,1)} %x_ref.1) | copy-start | bytes 2359300
  0.0 8.1 %copy-start.2 = (bf16[2,192,192]{2,1,0:T(8,128)(2,1)S(1)}, bf16[2,192,192]{2,1,0:T(8,128)(2,1)}, u32[]{:S(2)}) copy-start(bf16[2,192,192]{2,1,0:T(8,128)(2,1)} %proj_ref.5) | copy-start | bytes 442372
  0.0 8.1 %copy-start.4 = (f32[2,3,192]{2,0,1:T(2,128)S(1)}, f32[2,3,192]{2,0,1:T(2,128)}, u32[]{:S(2)}) copy-start(f32[2,3,192]{2,0,1:T(2,128)} %param.9) | copy-start | bytes 13828
  3.1 8.5 %collective-permute-start = (bf16[32,8,192]{2,1,0:T(8,128)(2,1)S(1)}, bf16[32,8,192]{2,1,0:T(8,128)(2,1)S(1)}, u32[]{:S(2)}, u32[]{:S(2)}) collective-permute-start(bf16[32,8,192]{2,1,0:T(8,128)(2,1)S(1)} %get-tuple-element.27), channel_id=1, source_target_pairs={{0,1},{1,0},{2,3},{3,2},{4,5},{5,4},{6,7},{7,6},{8,9},{9,8},{10,11... | collective-permute-start | bytes 294920 | tf_op jit(solution)/shard_map/ppermute | solution.py:781
  4.5 7.1 %collective-permute-start.1 = (bf16[32,8,192]{2,1,0:T(8,128)(2,1)S(1)}, bf16[32,8,192]{2,1,0:T(8,128)(2,1)S(1)}, u32[]{:S(2)}, u32[]{:S(2)}) collective-permute-start(bf16[32,8,192]{2,1,0:T(8,128)(2,1)S(1)} %get-tuple-element.28), channel_id=1, source_target_pairs={{1,2},{2,1},{3,4},{4,3},{5,6},{6,5},{7,8},{8,7},{9,10},{10,9},{11,... | collective-permute-start | bytes 294920 | tf_op jit(solution)/shard_map/ppermute | solution.py:781
  11.6 3.9 %copy-start.5 = (bf16[2,192,768]{2,1,0:T(8,128)(2,1)S(1)}, bf16[2,192,768]{2,1,0:T(8,128)(2,1)}, u32[]{:S(2)}) copy-start(bf16[2,192,768]{2,1,0:T(8,128)(2,1)} %up_ref.5) | copy-start | bytes 1769476
  11.6 3.9 %copy-start.6 = (bf16[2,768,192]{1,2,0:T(8,128)(2,1)S(1)}, bf16[2,768,192]{1,2,0:T(8,128)(2,1)}, u32[]{:S(2)}) copy-start(bf16[2,768,192]{1,2,0:T(8,128)(2,1)} %param.15) | copy-start | bytes 1769476
  11.6 3.9 %copy-start.7 = (f32[2,49,192]{2,0,1:T(2,128)S(1)}, f32[2,49,192]{2,0,1:T(2,128)}, u32[]{:S(2)}) copy-start(f32[2,49,192]{2,0,1:T(2,128)} %param.13) | copy-start | bytes 225796
  11.8 8.1 %collective-permute-start.2 = (bf16[3,80,192]{2,1,0:T(8,128)(2,1)S(1)}, bf16[3,80,192]{2,1,0:T(8,128)(2,1)S(1)}, u32[]{:S(2)}, u32[]{:S(2)}) collective-permute-start(bf16[3,80,192]{2,1,0:T(8,128)(2,1)S(1)} %get-tuple-element.31), channel_id=1, source_target_pairs={{0,16},{16,0},{32,48},{48,32},{64,80},{80,64},{96,112},{112,96},{1... | collective-permute-start | bytes 276488 | tf_op jit(solution)/shard_map/ppermute | solution.py:781
  14.8 5.1 %collective-permute-start.3 = (bf16[3,80,192]{2,1,0:T(8,128)(2,1)S(1)}, bf16[3,80,192]{2,1,0:T(8,128)(2,1)S(1)}, u32[]{:S(2)}, u32[]{:S(2)}) collective-permute-start(bf16[3,80,192]{2,1,0:T(8,128)(2,1)S(1)} %get-tuple-element.32), channel_id=1, source_target_pairs={{16,32},{32,16},{48,64},{64,48},{80,96},{96,80},{17,33},{33,17},{4... | collective-permute-start | bytes 276488 | tf_op jit(solution)/shard_map/ppermute | solution.py:781
  24.4 29.7 %copy-start.1 = (bf16[2,192,576]{2,1,0:T(8,128)(2,1)S(1)}, bf16[2,192,576]{2,1,0:T(8,128)(2,1)}, u32[]{:S(2)}) copy-start(bf16[2,192,576]{2,1,0:T(8,128)(2,1)} %qkv_ref.3) | copy-start | bytes 1327108
  24.4 29.6 %copy-start.3 = (f32[2,6,225]{2,0,1:T(2,128)S(1)}, f32[2,6,225]{2,0,1:T(2,128)}, u32[]{:S(2)}) copy-start(f32[2,6,225]{2,0,1:T(2,128)} %param.12) | copy-start | bytes 32404
